TPU v7x, 8 devices: a whole 2x2x1 slice. The times are simulated.
8 devices in a mesh: ep: 2 (over z, y), dp: 4 (over x, core).
Axes of the slice: x: 2, y: 2, z: 1, core: 2. Of those that a mesh axis runs over, the one named last changes fastest.
Arguments:
- tokens: bfloat16 [8192, 1536], P(('dp', 'ep'))
- d_out: bfloat16 [8192, 1536], P(('dp', 'ep'))
- expert_ids: int32 [8192, 8], P(('dp', 'ep'))
- norm_gain: bfloat16 [1536], replicated
- router: bfloat16 [1536, 40], replicated
- w_gate: bfloat16 [40, 1536, 512], P('ep')
- w_up: bfloat16 [40, 1536, 512], P('ep')
- w_down: bfloat16 [40, 512, 1536], P('ep')
Outputs:
- output 1: bfloat16 [8192, 1536], P(('dp', 'ep'))
- output 2: float32 [1], replicated
- output 3: bfloat16 [8192, 1536], P(('dp', 'ep'))
- output 4: float32 [1536, 40], replicated
- output 5: bfloat16 [40, 1536, 512], P('ep')
- output 6: bfloat16 [40, 1536, 512], P('ep')
- output 7: bfloat16 [40, 512, 1536], P('ep')
All inputs are finite; a program needn't handle non-finite values.
Results may differ from a plain program's by a relative error of at most 0.0142087.
Values are sent between devices in bfloat16 or wider.
A program may use at most 1 GiB of HBM per device.

v0:
```python
import jax
import jax.numpy as jnp
from jax import lax
from jax.sharding import PartitionSpec as P

AUX_COEF = 0.001
NORM_EPS = 1e-6


def route_rows(expert_ids, expert_hits, capacity, group_size):
    tok_rows, top_k, experts = expert_hits.shape
    flat_ids = expert_ids.reshape(-1)
    flat_hits = expert_hits.reshape(tok_rows * top_k, experts)
    slot_rank = jnp.sum((jnp.cumsum(flat_hits, axis=0) - 1) * flat_hits, axis=1)
    local_experts = experts // group_size
    dest_row = ((flat_ids % local_experts) * group_size + flat_ids // local_experts) * capacity + slot_rank
    filler = jnp.full((experts * capacity,), tok_rows * top_k, jnp.int32).at[dest_row].set(jnp.arange(tok_rows * top_k, dtype=jnp.int32))
    return dest_row, filler


def norm_forward(tokens32, gain32):
    inv_rms = lax.rsqrt(jnp.mean(tokens32 * tokens32, axis=1, keepdims=True) + NORM_EPS)
    return inv_rms, (tokens32 * inv_rms * gain32).astype(jnp.bfloat16)


def norm_backward(tokens32, inv_rms, gain32, d_normed):
    d_scaled = d_normed * gain32
    return inv_rms * (d_scaled - tokens32 * (inv_rms * inv_rms) * jnp.mean(d_scaled * tokens32, axis=1, keepdims=True))


def solution(mesh):
    ep_size = mesh.shape["ep"]
    dp_size = mesh.shape["dp"]
    tok_spec = P(("dp", "ep"), None)
    exp_spec = P("ep", None, None)

    def device_step(tokens, d_out, expert_ids, norm_gain, router, w_gate, w_up, w_down):
        tok_rows, model_width = tokens.shape
        top_k = expert_ids.shape[1]
        local_experts = w_gate.shape[0]
        experts = local_experts * ep_size
        total_tok = tok_rows * ep_size * dp_size
        capacity = ((2 * tok_rows * top_k + 8 * experts - 1) // (8 * experts)) * 8
        group_rows = ep_size * capacity
        buffer_shape = (local_experts, ep_size, capacity, model_width)

        tokens32 = tokens.astype(jnp.float32)
        gain32 = norm_gain.astype(jnp.float32)
        inv_rms, normed = norm_forward(tokens32, gain32)
        logits = jnp.dot(normed, router, preferred_element_type=jnp.float32)
        router_probs = jax.nn.softmax(logits, axis=1)
        gate_vals = jnp.take_along_axis(router_probs, expert_ids, axis=1)
        expert_hits = (expert_ids[:, :, None] == jnp.arange(experts)[None, None, :]).astype(jnp.int32)
        local_stats = jnp.stack([jnp.sum(expert_hits, axis=(0, 1)).astype(jnp.float32), jnp.sum(router_probs, axis=0)])
        global_stats = lax.psum(local_stats, ("ep", "dp"))
        expert_frac = global_stats[0] / (total_tok * top_k)
        aux_loss = AUX_COEF * experts * jnp.sum(expert_frac * global_stats[1]) / total_tok

        dest_row, filler = route_rows(expert_ids, expert_hits, capacity, ep_size)
        token_of_row = filler // top_k
        packed = jnp.take(normed, token_of_row, axis=0, mode="fill", fill_value=0).reshape(buffer_shape)
        expert_rows = lax.all_to_all(packed, "ep", 1, 1, tiled=True).reshape(local_experts, group_rows, model_width)
        act_gate = jnp.einsum("erd,edf->erf", expert_rows, w_gate, preferred_element_type=jnp.float32)
        act_up = jnp.einsum("erd,edf->erf", expert_rows, w_up, preferred_element_type=jnp.float32)
        gate_sig = jax.nn.sigmoid(act_gate)
        gate_silu = act_gate * gate_sig
        hidden = (gate_silu * act_up).astype(jnp.bfloat16)
        result = jnp.einsum("erf,efd->erd", hidden, w_down, preferred_element_type=jnp.float32).astype(jnp.bfloat16)
        returned = lax.all_to_all(result.reshape(buffer_shape), "ep", 1, 1, tiled=True).reshape(experts * capacity, model_width)
        picked = jnp.take(returned, dest_row, axis=0).reshape(tok_rows, top_k, model_width)
        layer_out = (tokens32 + jnp.sum(gate_vals[:, :, None] * picked.astype(jnp.float32), axis=1)).astype(jnp.bfloat16)

        d_gates = jnp.einsum("td,tkd->tk", d_out, picked, preferred_element_type=jnp.float32)
        gate_of_row = jnp.take(gate_vals.reshape(-1), filler, axis=0, mode="fill", fill_value=0)
        d_rows = (jnp.take(d_out, token_of_row, axis=0, mode="fill", fill_value=0).astype(jnp.float32) * gate_of_row[:, None]).astype(jnp.bfloat16)
        d_expert_rows = lax.all_to_all(d_rows.reshape(buffer_shape), "ep", 1, 1, tiled=True).reshape(local_experts, group_rows, model_width)
        d_hidden = jnp.einsum("erd,efd->erf", d_expert_rows, w_down, preferred_element_type=jnp.float32)
        grad_down = jnp.einsum("erf,erd->efd", hidden, d_expert_rows, preferred_element_type=jnp.float32)
        d_act_gate = (d_hidden * act_up * gate_sig * (1.0 + act_gate * (1.0 - gate_sig))).astype(jnp.bfloat16)
        d_act_up = (d_hidden * gate_silu).astype(jnp.bfloat16)
        d_expert_in = (jnp.einsum("erf,edf->erd", d_act_gate, w_gate, preferred_element_type=jnp.float32) + jnp.einsum("erf,edf->erd", d_act_up, w_up, preferred_element_type=jnp.float32)).astype(jnp.bfloat16)
        grad_gate = jnp.einsum("erd,erf->edf", expert_rows, d_act_gate, preferred_element_type=jnp.float32)
        grad_up = jnp.einsum("erd,erf->edf", expert_rows, d_act_up, preferred_element_type=jnp.float32)
        d_returned = lax.all_to_all(d_expert_in.reshape(buffer_shape), "ep", 1, 1, tiled=True).reshape(experts * capacity, model_width)
        d_normed = jnp.sum(jnp.take(d_returned, dest_row, axis=0).reshape(tok_rows, top_k, model_width).astype(jnp.float32), axis=1)

        d_probs = jnp.einsum("tk,tke->te", d_gates, expert_hits.astype(jnp.float32)) + (AUX_COEF * experts / total_tok) * expert_frac[None, :]
        d_logits = (router_probs * (d_probs - jnp.sum(router_probs * d_probs, axis=1, keepdims=True))).astype(jnp.bfloat16)
        grad_router = lax.psum(lax.dot_general(normed, d_logits, (((0,), (0,)), ((), ())), preferred_element_type=jnp.float32), ("ep", "dp"))
        d_normed = d_normed + lax.dot_general(d_logits, router, (((1,), (1,)), ((), ())), preferred_element_type=jnp.float32)
        d_tokens = (d_out.astype(jnp.float32) + norm_backward(tokens32, inv_rms, gain32, d_normed)).astype(jnp.bfloat16)
        grad_gate = lax.psum(grad_gate, "dp").astype(jnp.bfloat16)
        grad_up = lax.psum(grad_up, "dp").astype(jnp.bfloat16)
        grad_down = lax.psum(grad_down, "dp").astype(jnp.bfloat16)
        return layer_out, aux_loss.reshape(1), d_tokens, grad_router, grad_gate, grad_up, grad_down

    return jax.shard_map(device_step, mesh=mesh, in_specs=(tok_spec, tok_spec, tok_spec, P(None), P(None, None), exp_spec, exp_spec, exp_spec), out_specs=(tok_spec, P(None), tok_spec, P(None, None), exp_spec, exp_spec, exp_spec), check_vma=False)
```

profile of v0, /device:TPU:0, one launch (start us, length us, event | category | flops | bytes accessed | tf_op | source)
XLA Modules:
  0.0 6203.3 jit_solution(9429177752259482010)
XLA Ops:
  31.3 30.5 scatter_custom_fusion
  65.1 54.7 gather_fusion.2
  119.8 34.3 broadcast_select_fusion
  154.1 33.7 copy.73
  207.2 101.0 %gather_fusion.4 = bf16[16640,1536]{1,0:T(8,128)(2,1)} fusion(bf16[1024,1536]{1,0:T(8,128)(2,1)} %param.13, s32[17408]{0:T(1024)S(1)} %pad_clamp_fusion.1), kind=kCustom, calls=%fused_computation.2.clone | custom fusion | bytes 102302720 | tf_op jit(solution)/shard_map/jit(_take)/gather | solution.py:75
  312.3 65.5 %gather_fusion.1 = f32[8192]{0:T(1024)S(1)} fusion(f32[1024,40]{0,1:T(8,128)S(1)} %get-tuple-element.15, s32[8192]{0:T(1024)S(1)} %reshape.274), kind=kCustom, calls=%fused_computation.5 | custom fusion | bytes 131072 | tf_op jit(solution)/shard_map/jit(take_along_axis)/gather | solution.py:52
  378.8 85.6 %gather_fusion = f32[16640]{0:T(1024)S(1)} fusion(f32[8192]{0:T(1024)S(1)} %select_n.90, s32[17408]{0:T(1024)S(1)} %pad_clamp_fusion), kind=kCustom, calls=%fused_computation.4 | custom fusion | bytes 199680 | tf_op jit(solution)/shard_map/jit(_take)/gather | solution.py:74
  464.4 34.0 multiply_convert_fusion
  498.4 34.7 copy.78
  533.1 225.8 %all-to-all-done = bf16[20,2,416,1536]{3,2,0,1:T(8,128)(2,1)} async-done(((bf16[20,2,416,1536]{3,2,0,1:T(8,128)(2,1)}), bf16[20,2,416,1536]{3,2,0,1:T(8,128)(2,1)}, u32[]{:S(2)}, u32[]{:S(2)}) %all-to-all-start) | async-done | bytes 51118112 | tf_op jit(solution)/shard_map/all_to_all | solution.py:62
  777.9 34.3 copy.74
  812.3 46.0 fusion.37
  858.3 469.3 %all-to-all-done.2 = bf16[20,2,416,1536]{3,2,0,1:T(8,128)(2,1)} async-done(((bf16[20,2,416,1536]{3,2,0,1:T(8,128)(2,1)}), bf16[20,2,416,1536]{3,2,0,1:T(8,128)(2,1)}, u32[]{:S(2)}, u32[]{:S(2)}) %all-to-all-start.2) | async-done | bytes 51118112 | tf_op jit(solution)/shard_map/all_to_all | solution.py:76
  1327.6 33.6 copy.79
  1361.2 46.1 fusion.38
  1407.3 75.6 %multiply_convert_fusion.3 = (bf16[20,832,512]{2,1,0:T(8,128)(2,1)}, bf16[20,832,512]{2,1,0:T(8,128)(2,1)}, bf16[20,832,512]{2,1,0:T(8,128)(2,1)}) fusion(f32[20,832,512]{2,1,0:T(8,128)} %fusion.37, f32[20,832,512]{2,1,0:T(8,128)} %fusion.38, bf16[20,832,1536]{2,1,0:T(8,128)(2,1)} %bitcast.75, bf16[20,1536,512]{2,1,0:T(8,128)(2,1)} %param.18), kind=kOutput, calls=%fused_computation.15 | convolution fusion | flops 26300252160 | bytes 201850880 | tf_op jit(solution)/shard_map/erd,edf->erf/dot_general | solution.py:64
  1482.9 58.7 fusion.39
  1541.6 65.1 %add_convert_fusion = bf16[20,832,1536]{2,1,0:T(8,128)(2,1)} fusion(f32[20,832,1536]{2,1,0:T(8,128)} %fusion.39, bf16[20,832,512]{2,1,0:T(8,128)(2,1)} %get-tuple-element.22, bf16[20,1536,512]{2,1,0:T(8,128)(2,1)} %param.18), kind=kOutput, calls=%fused_computation.7 | convolution fusion | flops 26223575040 | bytes 201850880 | tf_op jit(solution)/shard_map/erf,edf->erd/dot_general | solution.py:81
  1606.7 34.6 copy.80
  1660.5 566.3 %psum.35 = f32[2,40]{1,0:T(2,128)S(1)} all-reduce(f32[2,40]{1,0:T(2,128)S(1)} %pad_maximum_fusion), channel_id=1, replica_groups=mesh['ep'=2,'dp'=4] {'ep','dp'}, use_global_device_ids=true, to_apply=%region_10.13 | all-reduce | flops 80 | bytes 640 | tf_op jit(solution)/shard_map/psum | solution.py:55
  2229.8 44.1 convolution_convert_fusion
  2273.9 33.7 copy.75
  2307.7 54.0 fusion.41
  2361.7 54.6 fusion.42
  2416.3 57.2 fusion.43
  2492.3 3157.1 %all-reduce.5 = (bf16[20,1536,512]{2,1,0:T(8,128)(2,1)}, bf16[20,1536,512]{2,1,0:T(8,128)(2,1)}, bf16[20,512,1536]{2,1,0:T(8,128)(2,1)}) all-reduce(f32[20,1536,512]{2,1,0:T(8,128)} %fusion.41, f32[20,1536,512]{2,1,0:T(8,128)} %fusion.42, f32[20,512,1536]{2,1,0:T(8,128)} %fusion.43), channel_id=1, replica_groups=mesh['ep'=2,'dp'=4] {'dp'}, use_global_device_ids=true, to_apply=%region_16.19 | all-reduce | flops 47185920 | bytes 283115520 | tf_op jit(solution)/shard_map/psum | solution.py:92
  5649.4 34.3 copy.81
  5683.7 175.0 %gather_fusion.5 = bf16[8192,1536]{1,0:T(8,128)(2,1)} fusion(bf16[16640,1536]{1,0:T(8,128)(2,1)} %bitcast.70, s32[8192]{0:T(1024)S(1)} %copy-done.19), kind=kCustom, calls=%fused_computation.3.clone | custom fusion | bytes 50364416 | tf_op jit(solution)/shard_map/jit(_take)/gather | solution.py:85
  5858.7 34.3 copy.76
  5893.1 175.0 %gather_fusion.3 = bf16[8192,1536]{1,0:T(8,128)(2,1)} fusion(bf16[16640,1536]{1,0:T(8,128)(2,1)} %bitcast.69, s32[8192]{0:T(1024)S(1)} %copy-done.19), kind=kCustom, calls=%fused_computation.1.clone | custom fusion | bytes 50364416 | tf_op jit(solution)/shard_map/jit(_take)/gather | solution.py:70
  6068.1 49.9 convert_reduce_fusion
  6159.1 34.3 all-reduce.4.cloned.1.call-done
  (123 shorter events, 153.5 us)
Async XLA Ops:
  7.2 303.3 %copy-start = (bf16[1536,40]{0,1:T(8,128)(2,1)S(1)}, bf16[1536,40]{0,1:T(8,128)(2,1)}, u32[]{:S(2)}) copy-start(bf16[1536,40]{0,1:T(8,128)(2,1)} %param.16) | copy-start | bytes 368644
  8.7 53.2 copy-start.15
  10.9 108.9 %copy-start.22 = (f32[1536]{0:T(1024)}, f32[1536]{0:T(1024)S(1)}, u32[]{:S(2)}) copy-start(f32[1536]{0:T(1024)S(1)} %convert_element_type.85) | copy-start | bytes 18436
  14.1 105.7 %copy-start.24 = (f32[1024]{0:T(1024)}, f32[1024]{0:T(1024)S(1)}, u32[]{:S(2)}) copy-start(f32[1024]{0:T(1024)S(1)} %get-tuple-element.28) | copy-start | bytes 12292
  61.8 58.0 copy-start.20
  65.1 54.8 copy-start.3
  187.9 571.0 %all-to-all-start = ((bf16[20,2,416,1536]{3,2,0,1:T(8,128)(2,1)}), bf16[20,2,416,1536]{3,2,0,1:T(8,128)(2,1)}, u32[]{:S(2)}, u32[]{:S(2)}) async-start(bf16[20,2,416,1536]{3,2,0,1:T(8,128)(2,1)} %copy.73), calls=%async_computation | async-start | bytes 102236160 | tf_op jit(solution)/shard_map/all_to_all | solution.py:62
  207.1 101.1 %copy-start.9 = (s32[1024,8]{0,1:T(8,128)S(1)}, s32[1024,8]{0,1:T(8,128)}, u32[]{:S(2)}) copy-start(s32[1024,8]{0,1:T(8,128)} %param.14) | copy-start | bytes 98308
  207.2 103.3 %copy-start.4 = (bf16[1024,1536]{1,0:T(8,128)(2,1)S(1)}, bf16[1024,1536]{1,0:T(8,128)(2,1)}, u32[]{:S(2)}) copy-start(bf16[1024,1536]{1,0:T(8,128)(2,1)} %copy-done.3) | copy-start | bytes 9437188
  312.3 65.6 %copy-start.1 = (f32[1024,40]{0,1:T(8,128)}, f32[1024,40]{0,1:T(8,128)S(1)}, u32[]{:S(2)}) copy-start(f32[1024,40]{0,1:T(8,128)S(1)} %get-tuple-element.15) | copy-start | bytes 491524
  312.3 66.0 %copy-start.10 = (s32[1024,8]{0,1:T(8,128)S(1)}, s32[1024,8]{0,1:T(8,128)}, u32[]{:S(2)}) copy-start(s32[1024,8]{0,1:T(8,128)} %param.14) | copy-start | bytes 98308
  312.3 66.5 %copy-start.14 = (s32[16640]{0:T(1024)S(1)}, s32[16640]{0:T(1024)}, u32[]{:S(2)}) copy-start(s32[16640]{0:T(1024)} %copy-done.13) | copy-start | bytes 199684
  378.5 85.9 %copy-start.7 = (f32[1024,8]{1,0:T(8,128)}, f32[1024,8]{1,0:T(8,128)S(1)}, u32[]{:S(2)}) copy-start(f32[1024,8]{1,0:T(8,128)S(1)} %copy.67) | copy-start | bytes 98308
  378.8 85.6 %copy-start.21 = (pred[16640]{0:T(1024)(128)(4,1)S(1)}, pred[16640]{0:T(1024)(128)(4,1)}, u32[]{:S(2)}) copy-start(pred[16640]{0:T(1024)(128)(4,1)} %copy-done.20) | copy-start | bytes 49924
  758.9 568.7 %all-to-all-start.2 = ((bf16[20,2,416,1536]{3,2,0,1:T(8,128)(2,1)}), bf16[20,2,416,1536]{3,2,0,1:T(8,128)(2,1)}, u32[]{:S(2)}, u32[]{:S(2)}) async-start(bf16[20,2,416,1536]{3,2,0,1:T(8,128)(2,1)} %copy.78), calls=%async_computation.2 | async-start | bytes 102236160 | tf_op jit(solution)/shard_map/all_to_all | solution.py:76
  1641.3 19.2 copy-start.29
  1641.3 587.2 %copy-start.16 = (s32[8192]{0:T(1024)S(1)}, s32[8192]{0:T(1024)}, u32[]{:S(2)}) copy-start(s32[8192]{0:T(1024)} %copy-done.15) | copy-start | bytes 98308
  1641.3 587.2 %copy-start.18 = (s32[8192]{0:T(1024)S(1)}, s32[8192]{0:T(1024)}, u32[]{:S(2)}) copy-start(s32[8192]{0:T(1024)} %copy-done.17) | copy-start | bytes 98308
  1641.3 832.2 %all-to-all-start.3 = ((bf16[20,2,416,1536]{3,2,0,1:T(8,128)(2,1)}), bf16[20,2,416,1536]{3,2,0,1:T(8,128)(2,1)}, u32[]{:S(2)}, u32[]{:S(2)}) async-start(bf16[20,2,416,1536]{3,2,0,1:T(8,128)(2,1)} %copy.80), calls=%async_computation.3 | async-start | bytes 102236160 | tf_op jit(solution)/shard_map/all_to_all | solution.py:84
  2473.5 3385.2 %all-to-all-start.1 = ((bf16[20,2,416,1536]{3,2,0,1:T(8,128)(2,1)}), bf16[20,2,416,1536]{3,2,0,1:T(8,128)(2,1)}, u32[]{:S(2)}, u32[]{:S(2)}) async-start(bf16[20,2,416,1536]{3,2,0,1:T(8,128)(2,1)} %copy.75), calls=%async_computation.1 | async-start | bytes 102236160 | tf_op jit(solution)/shard_map/all_to_all | solution.py:69
  2492.3 3701.1 %all-reduce.4.cloned.1.call-start = ((), (), s32[]{:S(2)}) async-start(), calls=%async_computation.4 | async-start | bytes 491520 | tf_op jit(solution)/shard_map/psum | solution.py:89
  5649.4 34.3 copy-start.19
  5893.1 175.0 %copy-start.8 = (f32[1024,8]{1,0:T(8,128)S(1)}, f32[1024,8]{1,0:T(8,128)}, u32[]{:S(2)}) copy-start(f32[1024,8]{1,0:T(8,128)} %copy-done.7) | copy-start | bytes 98308
  5893.1 175.0 %copy-start.26 = (pred[8192]{0:T(1024)(128)(4,1)S(1)}, pred[8192]{0:T(1024)(128)(4,1)}, u32[]{:S(2)}) copy-start(pred[8192]{0:T(1024)(128)(4,1)} %get-tuple-element.16) | copy-start | bytes 24580
  6068.1 49.9 copy-start.6
  6118.0 21.3 copy-start.12
  6118.0 21.5 copy-start.2
  6118.0 21.5 copy-start.28
  6118.0 21.7 copy-start.5
  6118.0 23.0 copy-start.23
  6118.1 30.7 copy-start.25
  6118.1 30.7 copy-start.27
  (3 other events, 20.2 us)
Sparse Core Ops, SparseCore 0:
  6148.9 44.4 all-reduce.3
where the time goes:
time: 6220 us; the launch traced here: 6200 us
  blocking collectives  3720 us (60%)
  local copies, waits for them, and re-layouts  972 us (16%)
  waiting for transfers between devices  729 us (12%)
  matrix products  532 us (9%)
  other arithmetic  154 us (2%)
  starting transfers between devices  76 us (1%)
    psum x1, blocking collectives, device_step(): grad_gate = lax.psum(grad_gate, 'dp').astype(jnp.bfloat16)  3160 us
    psum x1, blocking collectives, device_step(): global_stats = lax.psum(local_stats, ('ep', 'dp'))  566 us
    all_to_all x1, waiting for transfers between devices, device_step(): lax.all_to_all(d_rows.reshape(buffer_shape), 'ep', 1, 1, tiled=True)  469 us
    all_to_all x1, waiting for transfers between devices, device_step(): lax.all_to_all(packed, 'ep', 1, 1, tiled=True)  226 us
    gather x1, local copies, waits for them, and re-layouts, device_step(): jnp.take(returned, dest_row, axis=0).reshape(tok_rows, top_k, model_width)  175 us
    gather x1, local copies, waits for them, and re-layouts, device_step(): jnp.take(d_returned, dest_row, axis=0).reshape(tok_rows, top_k, model_width)  175 us
  transfers between devices with their start and end apart: 5, of which 3 were waited for; matrix products, arithmetic and copies ran while one was open for 14% of the time, Pallas kernels for 0%

commit v1 on v0

v1 whole, which is shorter than its diff:
```python
import functools

import jax
import jax.numpy as jnp
from jax import lax
from jax.experimental import pallas as pl
from jax.experimental.pallas import tpu as pltpu
from jax.sharding import PartitionSpec as P

AUX_COEF = 0.001
NORM_EPS = 1e-6
MAX_HITS = 416
BLOCK = 256
GROUP = 16
TILE = 256
CHUNK = 128
MIX = 256
NT_DIMS = (((1,), (1,)), ((), ()))
TN_DIMS = (((0,), (0,)), ((), ()))
VMEM_LIMIT = 60 * 1024 * 1024


def norm_forward(tokens32, gain32):
    inv_rms = lax.rsqrt(jnp.mean(tokens32 * tokens32, axis=1, keepdims=True) + NORM_EPS)
    return inv_rms, (tokens32 * inv_rms * gain32).astype(jnp.bfloat16)


def norm_backward(tokens32, inv_rms, gain32, d_normed):
    d_scaled = d_normed * gain32
    return inv_rms * (d_scaled - tokens32 * (inv_rms * inv_rms) * jnp.mean(d_scaled * tokens32, axis=1, keepdims=True))


def dot32(left, right, dims=(((1,), (0,)), ((), ()))):
    return lax.dot_general(left, right, dims, preferred_element_type=jnp.float32)


def dispatch_kernel(scaled, n_exp, order, n_chunk, seg_len, seg_src, seg_dst, tail_at, tail_len, src, pos, gates, out, stack, blank, sems, tail_sem):
    step = pl.program_id(0)
    last = pl.num_programs(0) - 1
    slot = lax.rem(step, 2)

    def segment_copy(blk, buf, exp, grp):
        at = blk * n_exp + exp
        from_row = pl.multiple_of((seg_src[at] + grp) * GROUP, GROUP)
        to_row = pl.multiple_of((seg_dst[at] + grp) * GROUP, GROUP)
        return pltpu.make_async_copy(stack.at[buf, pl.ds(from_row, GROUP), :], out.at[pl.ds(to_row, GROUP), :], sems.at[buf])

    def each_segment(blk, buf, act):
        for exp in range(n_exp):
            @pl.loop(0, seg_len[blk * n_exp + exp])
            def _(grp):
                act(segment_copy(blk, buf, exp, grp))

    def each_tail(act):
        for exp in range(n_exp):
            @pl.loop(0, tail_len[exp])
            def _(grp):
                to_row = pl.multiple_of((tail_at[exp] + grp) * GROUP, GROUP)
                act(pltpu.make_async_copy(blank, out.at[pl.ds(to_row, GROUP), :], tail_sem))

    @pl.when(step == 0)
    def _():
        blank[...] = jnp.zeros_like(blank)
        each_tail(lambda copy: copy.start())

    @pl.when(step >= 2)
    def _():
        each_segment(step - 2, slot, lambda copy: copy.wait())

    @pl.loop(0, n_chunk[step])
    def _(chunk):
        row = lax.broadcasted_iota(jnp.int32, (CHUNK, BLOCK), 0) + chunk * CHUNK
        hit = pos[0, 0:1, :] == row
        if scaled:
            weight = jnp.where(hit, gates[0, 0:1, :], 0.0)
        for k in range(1, pos.shape[1]):
            here = pos[0, k:k + 1, :] == row
            hit = jnp.logical_or(hit, here)
            if scaled:
                weight = jnp.where(here, gates[0, k:k + 1, :], weight)
        picked = dot32(jnp.where(hit, 1.0, 0.0).astype(jnp.bfloat16), src[...])
        if scaled:
            picked = picked * jnp.sum(weight, axis=1, keepdims=True)
        stack[slot, pl.ds(pl.multiple_of(chunk * CHUNK, CHUNK), CHUNK), :] = picked.astype(jnp.bfloat16)

    each_segment(step, slot, lambda copy: copy.start())

    @pl.when(step == last)
    def _():
        each_segment(step - 1, 1 - slot, lambda copy: copy.wait())
        each_segment(step, slot, lambda copy: copy.wait())
        each_tail(lambda copy: copy.wait())


def dispatch(src, pos, gates, plan, rows, scaled):
    blocks, top_k, _ = pos.shape
    width = src.shape[1]
    n_exp = plan["tail_at"].shape[0]
    stack_rows = -(-(BLOCK * top_k + n_exp * (GROUP - 1)) // CHUNK) * CHUNK
    return pl.pallas_call(
        functools.partial(dispatch_kernel, scaled, n_exp),
        out_shape=jax.ShapeDtypeStruct((rows, width), jnp.bfloat16),
        grid_spec=pltpu.PrefetchScalarGridSpec(
            num_scalar_prefetch=7,
            grid=(blocks,),
            in_specs=[
                pl.BlockSpec((BLOCK, width), lambda i, order, *_: (order[i], 0)),
                pl.BlockSpec((1, top_k, BLOCK), lambda i, *_: (i, 0, 0)),
                pl.BlockSpec((1, top_k, BLOCK), lambda i, *_: (i, 0, 0)),
            ],
            out_specs=pl.BlockSpec(memory_space=pl.ANY),
            scratch_shapes=[
                pltpu.VMEM((2, stack_rows, width), jnp.bfloat16),
                pltpu.VMEM((GROUP, width), jnp.bfloat16),
                pltpu.SemaphoreType.DMA((2,)),
                pltpu.SemaphoreType.DMA,
            ],
        ),
        compiler_params=pltpu.CompilerParams(dimension_semantics=("arbitrary",), vmem_limit_bytes=VMEM_LIMIT),
        cost_estimate=pl.CostEstimate(flops=20_000_000_000, bytes_accessed=80_000_000, transcendentals=0),
        name="dispatch_scaled" if scaled else "dispatch",
    )(plan["order"], plan["n_chunk"], plan["seg_len"], plan["seg_src"], plan["seg_dst"], plan["tail_at"], plan["tail_len"], src, pos, gates)


def combine_kernel(weighted, n_exp, order, n_mix, seg_len, seg_src, seg_dst, rows, pos, gates, d_out, *rest):
    if weighted:
        out, d_gates, stack, sems = rest
    else:
        out, stack, sems = rest
    step = pl.program_id(0)
    last = pl.num_programs(0) - 1
    slot = lax.rem(step, 2)

    def each_segment(blk, buf, act):
        for exp in range(n_exp):
            @pl.loop(0, seg_len[blk * n_exp + exp])
            def _(grp):
                at = blk * n_exp + exp
                to_row = pl.multiple_of((seg_src[at] + grp) * GROUP, GROUP)
                from_row = pl.multiple_of((seg_dst[at] + grp) * GROUP, GROUP)
                act(pltpu.make_async_copy(rows.at[pl.ds(from_row, GROUP), :], stack.at[buf, pl.ds(to_row, GROUP), :], sems.at[buf]))

    @pl.when(step == 0)
    def _():
        @pl.loop(0, stack.shape[1] // MIX)
        def _(part):
            stack[:, pl.ds(pl.multiple_of(part * MIX, MIX), MIX), :] = jnp.zeros((2, MIX, stack.shape[2]), stack.dtype)
        each_segment(0, 0, lambda copy: copy.start())

    @pl.when(step < last)
    def _():
        each_segment(step + 1, 1 - slot, lambda copy: copy.start())

    each_segment(step, slot, lambda copy: copy.wait())
    out[...] = jnp.zeros_like(out)
    if weighted:
        d_gates[...] = jnp.zeros_like(d_gates)

    @pl.loop(0, n_mix[step])
    def _(part):
        col = lax.broadcasted_iota(jnp.int32, (BLOCK, MIX), 1) + part * MIX
        part_rows = stack[slot, pl.ds(pl.multiple_of(part * MIX, MIX), MIX), :]
        top_k = pos.shape[2]
        if weighted:
            cross = dot32(d_out[...], part_rows, NT_DIMS)
            weight = jnp.zeros((BLOCK, MIX), jnp.float32)
            d_cols = []
            for k in range(top_k):
                here = pos[0, :, k:k + 1] == col
                weight = jnp.where(here, gates[0, :, k:k + 1], weight)
                d_cols.append(jnp.sum(jnp.where(here, cross, 0.0), axis=1, keepdims=True))
            d_gates[0] += jnp.concatenate(d_cols, axis=1)
            high = weight.astype(jnp.bfloat16)
            left = weight - high.astype(jnp.float32)
            mid = left.astype(jnp.bfloat16)
            low = (left - mid.astype(jnp.float32)).astype(jnp.bfloat16)
            out[...] += dot32(high, part_rows) + dot32(mid, part_rows) + dot32(low, part_rows)
        else:
            hit = pos[0, :, 0:1] == col
            for k in range(1, top_k):
                hit = jnp.logical_or(hit, pos[0, :, k:k + 1] == col)
            out[...] += dot32(jnp.where(hit, 1.0, 0.0).astype(jnp.bfloat16), part_rows)


def combine(rows, pos_t, gates_t, d_out, plan, weighted):
    blocks, _, top_k = pos_t.shape
    width = rows.shape[1]
    n_exp = plan["tail_at"].shape[0]
    stack_rows = -(-(BLOCK * top_k + n_exp * (GROUP - 1)) // MIX) * MIX
    out_shape = [jax.ShapeDtypeStruct((blocks * BLOCK, width), jnp.float32)]
    out_specs = [pl.BlockSpec((BLOCK, width), lambda i, *_: (i, 0))]
    if weighted:
        out_shape.append(jax.ShapeDtypeStruct((blocks, BLOCK, top_k), jnp.float32))
        out_specs.append(pl.BlockSpec((1, BLOCK, top_k), lambda i, *_: (i, 0, 0)))
    d_spec = pl.BlockSpec((BLOCK, width), lambda i, order, *_: (order[i], 0)) if weighted else pl.BlockSpec((GROUP, width), lambda i, *_: (0, 0))
    return pl.pallas_call(
        functools.partial(combine_kernel, weighted, n_exp),
        out_shape=out_shape,
        grid_spec=pltpu.PrefetchScalarGridSpec(
            num_scalar_prefetch=5,
            grid=(blocks,),
            in_specs=[
                pl.BlockSpec(memory_space=pl.ANY),
                pl.BlockSpec((1, BLOCK, top_k), lambda i, *_: (i, 0, 0)),
                pl.BlockSpec((1, BLOCK, top_k), lambda i, *_: (i, 0, 0)),
                d_spec,
            ],
            out_specs=out_specs,
            scratch_shapes=[
                pltpu.VMEM((2, stack_rows, width), jnp.bfloat16),
                pltpu.SemaphoreType.DMA((2,)),
            ],
        ),
        compiler_params=pltpu.CompilerParams(dimension_semantics=("arbitrary",), vmem_limit_bytes=VMEM_LIMIT),
        cost_estimate=pl.CostEstimate(flops=30_000_000_000 if weighted else 10_000_000_000, bytes_accessed=60_000_000, transcendentals=0),
        name="combine_weighted" if weighted else "combine",
    )(plan["order"], plan["n_mix"], plan["seg_len"], plan["seg_src"], plan["seg_dst"], rows, pos_t, gates_t, d_out)


def forward_kernel(tile_exp, tile_at, own_at, tile_kind, x, w_gate, w_up, w_down, act_gate, act_up, hidden, result):
    kind = tile_kind[pl.program_id(0)]

    @pl.when(kind > 0)
    def _():
        a = dot32(x[...], w_gate[0])
        b = dot32(x[...], w_up[0])
        u = (a * jax.nn.sigmoid(a) * b).astype(jnp.bfloat16)
        act_gate[...] = a
        act_up[...] = b
        hidden[...] = u

    @pl.when(kind > 1)
    def _():
        result[...] = dot32(hidden[...], w_down[0]).astype(jnp.bfloat16)


def inward_kernel(tile_exp, tile_at, own_at, tile_kind, d_rows, act_gate, act_up, w_gate, w_up, w_down, d_gate, d_up, d_in):
    kind = tile_kind[pl.program_id(0)]

    @pl.when(kind > 0)
    def _():
        d_hidden = dot32(d_rows[...], w_down[0], NT_DIMS)
        a = act_gate[...]
        sig = jax.nn.sigmoid(a)
        d_gate[...] = (d_hidden * act_up[...] * sig * (1.0 + a * (1.0 - sig))).astype(jnp.bfloat16)
        d_up[...] = (d_hidden * (a * sig)).astype(jnp.bfloat16)

    @pl.when(kind > 1)
    def _():
        d_in[...] = (dot32(d_gate[...], w_gate[0], NT_DIMS) + dot32(d_up[...], w_up[0], NT_DIMS)).astype(jnp.bfloat16)


def grads_kernel(pair_tile, pair_next, pair_exp, pair_kind, pair_first, pair_last, x0, x1, a0, a1, b0, b1, u0, u1, d0, d1, g_gate, g_up, g_down, s_gate, s_up, s_down):
    step = pl.program_id(0)

    @pl.when(pair_first[step] > 0)
    def _():
        s_gate[...] = jnp.zeros_like(s_gate)
        s_up[...] = jnp.zeros_like(s_up)
        s_down[...] = jnp.zeros_like(s_down)

    def add(total, left, right):
        total[...] += dot32(left, right, TN_DIMS)

    @pl.when(pair_kind[step] > 1)
    def _():
        x = jnp.concatenate([x0[...], x1[...]], axis=0)
        d = jnp.concatenate([d0[...], d1[...]], axis=0)
        add(s_gate, x, jnp.concatenate([a0[...], a1[...]], axis=0))
        add(s_up, x, jnp.concatenate([b0[...], b1[...]], axis=0))
        add(s_down, jnp.concatenate([u0[...], u1[...]], axis=0), d)

    @pl.when(pair_kind[step] == 1)
    def _():
        add(s_gate, x0[...], a0[...])
        add(s_up, x0[...], b0[...])
        add(s_down, u0[...], d0[...])

    @pl.when(pair_last[step] > 0)
    def _():
        g_gate[0] = s_gate[...].astype(jnp.bfloat16)
        g_up[0] = s_up[...].astype(jnp.bfloat16)
        g_down[0] = s_down[...].astype(jnp.bfloat16)


def tile_specs(width, mid):
    wide = pl.BlockSpec((TILE, width), lambda t, exp, at, own, kind: (at[t], 0))
    thin = pl.BlockSpec((TILE, mid), lambda t, exp, at, own, kind: (at[t], 0))
    owned = pl.BlockSpec((TILE, width), lambda t, exp, at, own, kind: (own[t], 0))
    w_in = pl.BlockSpec((1, width, mid), lambda t, exp, at, own, kind: (exp[t], 0, 0))
    w_out = pl.BlockSpec((1, mid, width), lambda t, exp, at, own, kind: (exp[t], 0, 0))
    return wide, thin, owned, w_in, w_out


def forward_tiles(x, w_gate, w_up, w_down, plan):
    rows, width = x.shape
    mid = w_gate.shape[2]
    max_tiles = rows // TILE
    wide, thin, owned, w_in, w_out = tile_specs(width, mid)
    return pl.pallas_call(
        forward_kernel,
        out_shape=[
            jax.ShapeDtypeStruct((rows, mid), jnp.float32),
            jax.ShapeDtypeStruct((rows, mid), jnp.float32),
            jax.ShapeDtypeStruct((rows, mid), jnp.bfloat16),
            jax.ShapeDtypeStruct((rows, width), jnp.bfloat16),
        ],
        grid_spec=pltpu.PrefetchScalarGridSpec(
            num_scalar_prefetch=4,
            grid=(max_tiles,),
            in_specs=[wide, w_in, w_in, w_out],
            out_specs=[thin, thin, thin, owned],
        ),
        compiler_params=pltpu.CompilerParams(dimension_semantics=("arbitrary",), vmem_limit_bytes=VMEM_LIMIT),
        cost_estimate=pl.CostEstimate(flops=70_000_000_000, bytes_accessed=250_000_000, transcendentals=0),
        name="forward_tiles",
    )(plan["tile_exp"], plan["tile_at"], plan["own_at"], plan["tile_kind"], x, w_gate, w_up, w_down)


def inward_tiles(d_rows, act_gate, act_up, w_gate, w_up, w_down, plan):
    rows, width = d_rows.shape
    mid = w_gate.shape[2]
    max_tiles = rows // TILE
    wide, thin, owned, w_in, w_out = tile_specs(width, mid)
    return pl.pallas_call(
        inward_kernel,
        out_shape=[
            jax.ShapeDtypeStruct((rows, mid), jnp.bfloat16),
            jax.ShapeDtypeStruct((rows, mid), jnp.bfloat16),
            jax.ShapeDtypeStruct((rows, width), jnp.bfloat16),
        ],
        grid_spec=pltpu.PrefetchScalarGridSpec(
            num_scalar_prefetch=4,
            grid=(max_tiles,),
            in_specs=[wide, thin, thin, w_in, w_in, w_out],
            out_specs=[thin, thin, owned],
        ),
        compiler_params=pltpu.CompilerParams(dimension_semantics=("arbitrary",), vmem_limit_bytes=VMEM_LIMIT),
        cost_estimate=pl.CostEstimate(flops=60_000_000_000, bytes_accessed=250_000_000, transcendentals=0),
        name="inward_tiles",
    )(plan["tile_exp"], plan["tile_at"], plan["own_at"], plan["tile_kind"], d_rows, act_gate, act_up, w_gate, w_up, w_down)


def grad_tiles(x, d_gate, d_up, hidden, d_rows, plan):
    rows, width = x.shape
    mid = d_gate.shape[1]
    n_exp = plan["tail_at"].shape[0]
    wide0 = pl.BlockSpec((TILE, width), lambda s, tile, *_: (tile[s], 0))
    thin0 = pl.BlockSpec((TILE, mid), lambda s, tile, *_: (tile[s], 0))
    wide1 = pl.BlockSpec((TILE, width), lambda s, tile, after, *_: (after[s], 0))
    thin1 = pl.BlockSpec((TILE, mid), lambda s, tile, after, *_: (after[s], 0))
    g_in = pl.BlockSpec((1, width, mid), lambda s, tile, after, exp, *_: (exp[s], 0, 0))
    g_out = pl.BlockSpec((1, mid, width), lambda s, tile, after, exp, *_: (exp[s], 0, 0))
    return pl.pallas_call(
        grads_kernel,
        out_shape=[
            jax.ShapeDtypeStruct((n_exp, width, mid), jnp.bfloat16),
            jax.ShapeDtypeStruct((n_exp, width, mid), jnp.bfloat16),
            jax.ShapeDtypeStruct((n_exp, mid, width), jnp.bfloat16),
        ],
        grid_spec=pltpu.PrefetchScalarGridSpec(
            num_scalar_prefetch=6,
            grid=(plan["pair_tile"].shape[0],),
            in_specs=[wide0, wide1, thin0, thin1, thin0, thin1, thin0, thin1, wide0, wide1],
            out_specs=[g_in, g_in, g_out],
            scratch_shapes=[
                pltpu.VMEM((width, mid), jnp.float32),
                pltpu.VMEM((width, mid), jnp.float32),
                pltpu.VMEM((mid, width), jnp.float32),
            ],
        ),
        compiler_params=pltpu.CompilerParams(dimension_semantics=("arbitrary",), vmem_limit_bytes=VMEM_LIMIT),
        cost_estimate=pl.CostEstimate(flops=85_000_000_000, bytes_accessed=250_000_000, transcendentals=0),
        name="grad_tiles",
    )(plan["pair_tile"], plan["pair_next"], plan["pair_exp"], plan["pair_kind"], plan["pair_first"], plan["pair_last"], x, x, d_gate, d_gate, d_up, d_up, hidden, hidden, d_rows, d_rows)


def exclusive(values, axis=0):
    return jnp.cumsum(values, axis=axis) - values


def make_plan(local_ids, order, own_blocks, n_exp, max_tiles):
    blocks = local_ids.shape[0]
    onehot = (local_ids[:, :, None, :] == jnp.arange(n_exp)[None, None, :, None]).astype(jnp.float32)
    hits = jnp.sum(onehot, axis=1)
    before = jnp.triu(jnp.ones((BLOCK, BLOCK), jnp.bfloat16), 1)
    rank = jnp.einsum("oet,ts->oes", hits.astype(jnp.bfloat16), before, preferred_element_type=jnp.float32)
    seg_len = (jnp.sum(hits, axis=2).astype(jnp.int32) + GROUP - 1) // GROUP
    seg_src = exclusive(seg_len, 1)
    per_tile = TILE // GROUP
    groups = jnp.sum(seg_len, axis=0)
    tiles = (groups + per_tile - 1) // per_tile
    tile_base = exclusive(tiles)
    seg_dst = tile_base[None, :] * per_tile + exclusive(seg_len, 0)
    place = rank + (seg_src * GROUP).astype(jnp.float32)[:, :, None]
    pos = jnp.sum(onehot * (place[:, None] + 1.0), axis=2).astype(jnp.int32) - 1
    own_tiles = (jnp.sum(seg_len[:own_blocks], axis=0) + per_tile - 1) // per_tile
    tile_ids = jnp.arange(max_tiles)
    tile_at = jnp.minimum(tile_ids, jnp.sum(tiles) - 1)
    tile_exp = jnp.sum((tile_at[:, None] >= (tile_base + tiles)[None, :]).astype(jnp.int32), axis=1)
    own_at = jnp.minimum(tile_at, (tile_base + own_tiles)[tile_exp] - 1)
    is_own = own_at == tile_at
    pairs = (tiles + 1) // 2
    pair_base = exclusive(pairs)
    pair_ids = jnp.arange(n_exp * ((max_tiles // n_exp + 1) // 2))
    pair_at = jnp.minimum(pair_ids, jnp.sum(pairs) - 1)
    pair_live = pair_ids == pair_at
    pair_exp = jnp.sum((pair_at[:, None] >= (pair_base + pairs)[None, :]).astype(jnp.int32), axis=1)
    nth = pair_at - pair_base[pair_exp]
    pair_tile = tile_base[pair_exp] + 2 * nth
    is_pair = 2 * nth + 1 < tiles[pair_exp]
    stack_rows = jnp.sum(seg_len, axis=1) * GROUP
    plan = {
        "order": order,
        "n_chunk": (stack_rows + CHUNK - 1) // CHUNK,
        "n_mix": (stack_rows + MIX - 1) // MIX,
        "seg_len": seg_len.reshape(-1),
        "seg_src": seg_src.reshape(-1),
        "seg_dst": seg_dst.reshape(-1),
        "tail_at": tile_base * per_tile + groups,
        "tail_len": tiles * per_tile - groups,
        "tile_exp": tile_exp,
        "tile_at": tile_at,
        "own_at": own_at,
        "tile_kind": jnp.where(tile_ids == tile_at, jnp.where(is_own, 2, 1), 0),
        "pair_tile": pair_tile,
        "pair_next": pair_tile + is_pair,
        "pair_exp": pair_exp,
        "pair_kind": jnp.where(pair_live, jnp.where(is_pair, 2, 1), 0),
        "pair_first": pair_live & (nth == 0),
        "pair_last": pair_live & (nth == pairs[pair_exp] - 1),
    }
    return jax.tree.map(lambda value: value.astype(jnp.int32), plan), pos


def solution(mesh):
    ep_size = mesh.shape["ep"]
    dp_size = mesh.shape["dp"]
    devices = ep_size * dp_size
    cores = 2
    tok_spec = P(("dp", "ep"), None)
    exp_spec = P("ep", None, None)
    core_perm = [(i, i ^ 1) for i in range(dp_size)]
    ep_perm = [(i, i ^ 1) for i in range(ep_size)]
    core_groups = [[i, i + 1] for i in range(0, dp_size, cores)]

    def to_owner(parts):
        half = parts.shape[0] // 2
        mine = parts[half:] + lax.ppermute(parts[:half], "dp", core_perm)
        quarter = half // 2
        return mine[quarter:] + lax.ppermute(mine[:quarter], "ep", ep_perm)

    def device_step(tokens, d_out, expert_ids, norm_gain, router, w_gate, w_up, w_down):
        tok_rows, model_width = tokens.shape
        top_k = expert_ids.shape[1]
        local_experts = w_gate.shape[0]
        experts = local_experts * ep_size
        total_tok = tok_rows * devices
        n_exp = local_experts // cores
        dev_blocks = tok_rows // BLOCK
        own_devs = devices // 2
        own_blocks = own_devs * dev_blocks
        seg_pad = devices * dev_blocks * (GROUP - 1)
        max_tiles = n_exp * -(-(devices * MAX_HITS + seg_pad) // TILE)

        ep_at = lax.axis_index("ep")
        dp_at = lax.axis_index("dp")
        core_at = lax.rem(dp_at, cores)
        x_at = lax.div(dp_at, cores)

        def dev_of(x, core, ep):
            return (x * cores + core) * ep_size + ep

        dev_order = jnp.stack(
            [dev_of(x_at, 1 - core_at, 1 - ep_at), dev_of(x_at, 1 - core_at, ep_at), dev_of(x_at, core_at, 1 - ep_at), dev_of(x_at, core_at, ep_at)]
            + [dev_of(1 - x_at, core, ep) for core in range(cores) for ep in range(ep_size)]
        )
        order = (dev_order[:, None] * dev_blocks + jnp.arange(dev_blocks)[None, :]).reshape(-1).astype(jnp.int32)

        tokens32 = tokens.astype(jnp.float32)
        gain32 = norm_gain.astype(jnp.float32)
        inv_rms, normed = norm_forward(tokens32, gain32)
        logits = jnp.dot(normed, router, preferred_element_type=jnp.float32)
        router_probs = jax.nn.softmax(logits, axis=1)
        expert_hits = expert_ids[:, :, None] == jnp.arange(experts)[None, None, :]
        gate_vals = jnp.sum(jnp.where(expert_hits, router_probs[:, None, :], 0.0), axis=2)

        prob_sums = jnp.pad(jnp.sum(router_probs, axis=0), (0, tok_rows - experts))
        packet = jnp.concatenate([expert_ids.astype(jnp.float32).T, gate_vals.T, prob_sums[None]], axis=0)
        packets = lax.all_gather(packet, ("dp", "ep"))
        all_normed = lax.all_gather(normed, ("dp", "ep"), tiled=True)
        d_out_late, _ = lax.optimization_barrier((d_out, all_normed[:8]))
        all_d_out = lax.all_gather(d_out_late, ("dp", "ep"), tiled=True)

        all_ids = packets[:, :top_k].astype(jnp.int32)
        counts = jnp.sum((all_ids[..., None] == jnp.arange(experts)).astype(jnp.float32), axis=(0, 1, 2))
        expert_frac = counts / (total_tok * top_k)
        aux_loss = AUX_COEF * experts * jnp.sum(expert_frac * jnp.sum(packets[:, 2 * top_k, :experts], axis=0)) / total_tok

        turned = jnp.take(packets, dev_order, axis=0)

        def by_block(rows):
            return rows.reshape(devices, top_k, dev_blocks, BLOCK).transpose(0, 2, 1, 3).reshape(devices * dev_blocks, top_k, BLOCK)

        first_expert = ep_at * local_experts + core_at * n_exp
        block_ids = by_block(turned[:, :top_k]).astype(jnp.int32) - first_expert
        block_ids = jnp.where((block_ids >= 0) & (block_ids < n_exp), block_ids, n_exp)
        block_gates = by_block(turned[:, top_k:2 * top_k])
        plan, pos = make_plan(block_ids, order, own_blocks, n_exp, max_tiles)
        plan["tile_exp"] = plan["tile_exp"] + core_at * n_exp
        pos_t = pos[:own_blocks].transpose(0, 2, 1)
        gates_t = block_gates[:own_blocks].transpose(0, 2, 1)

        rows = max_tiles * TILE
        x = dispatch(all_normed, pos, block_gates, plan, rows, False)
        act_gate, act_up, hidden, result = forward_tiles(x, w_gate, w_up, w_down, plan)
        d_rows = dispatch(all_d_out, pos, block_gates, plan, rows, True)
        mixed_parts, d_gate_parts = combine(result, pos_t, gates_t, all_d_out, plan, True)
        d_act_gate, d_act_up, d_expert_in = inward_tiles(d_rows, act_gate, act_up, w_gate, w_up, w_down, plan)
        (d_normed_parts,) = combine(d_expert_in, pos_t, gates_t, all_d_out, plan, False)
        grad_gate, grad_up, grad_down = grad_tiles(x, d_act_gate, d_act_up, hidden, d_rows, plan)

        def both_cores(grad):
            return lax.all_gather(grad, "dp", axis_index_groups=core_groups, tiled=True)

        layer_out = (tokens32 + to_owner(mixed_parts)).astype(jnp.bfloat16)
        d_gates = to_owner(d_gate_parts).reshape(tok_rows, top_k)
        d_probs = jnp.sum(jnp.where(expert_hits, d_gates[:, :, None], 0.0), axis=1) + (AUX_COEF * experts / total_tok) * expert_frac[None, :]
        d_logits = (router_probs * (d_probs - jnp.sum(router_probs * d_probs, axis=1, keepdims=True))).astype(jnp.bfloat16)
        grad_router = lax.psum(lax.dot_general(normed, d_logits, TN_DIMS, preferred_element_type=jnp.float32), ("ep", "dp"))
        d_normed = to_owner(d_normed_parts) + lax.dot_general(d_logits, router, NT_DIMS, preferred_element_type=jnp.float32)
        d_tokens = (d_out.astype(jnp.float32) + norm_backward(tokens32, inv_rms, gain32, d_normed)).astype(jnp.bfloat16)
        return layer_out, aux_loss.reshape(1), d_tokens, grad_router, both_cores(grad_gate), both_cores(grad_up), both_cores(grad_down)

    return jax.shard_map(device_step, mesh=mesh, in_specs=(tok_spec, tok_spec, tok_spec, P(None), P(None, None), exp_spec, exp_spec, exp_spec), out_specs=(tok_spec, P(None), tok_spec, P(None, None), exp_spec, exp_spec, exp_spec), check_vma=False)
```

time: 6220 us -> 1440 us (0.23)
  blocking collectives: 3720 us -> 21.1 us
  local copies, waits for them, and re-layouts: 972 us -> 131 us
  Pallas kernels: 0 us -> 779 us
  matrix products: 532 us -> 3.56 us
  waiting for transfers between devices: 729 us -> 331 us
    psum x2 -> x0, blocking collectives: 3720 us -> none  [the longest x1 3160 us: device_step(): grad_gate = lax.psum(grad_gate, 'dp').astype(jnp.bfloat16)]
    pallas_call x0 -> x7, Pallas kernels: none -> 779 us  [the longest x2 172 us: dispatch(): pl.pallas_call(functools.partial(dispatch_kernel, scaled, n_exp), out_sha...]
    all_to_all x4 -> x0, waiting for transfers between devices: 695 us -> none  [the longest x1 469 us: device_step(): lax.all_to_all(d_rows.reshape(buffer_shape), 'ep', 1, 1, tiled=True)]
    gather x10 -> x6, local copies, waits for them, and re-layouts: 660 us -> 4.04 us  [the longest x1 0.7 us: make_plan(): pair_tile = tile_base[pair_exp] + 2 * nth]
    dot_general x12 -> x3, matrix products: 530 us -> 2.53 us  [the longest x1 1.32 us: device_step(): lax.dot_general(normed, d_logits, TN_DIMS, preferred_element_type=jnp.flo...]
    ppermute x0 -> x6, waiting for transfers between devices: none -> 253 us  [the longest x3 253 us: to_owner(): return mine[quarter:] + lax.ppermute(mine[:quarter], 'ep', ep_perm)]
    reshape x4 -> x0, local copies, waits for them, and re-layouts: 137 us -> none  [the longest x1 34.7 us: device_step(): d_rows.reshape(buffer_shape)]
    all_to_all x4 -> x0, local copies, waits for them, and re-layouts: 137 us -> none  [the longest x1 34.3 us: device_step(): lax.all_to_all(packed, 'ep', 1, 1, tiled=True)]
  transfers between devices with their start and end apart: 5 -> 12, of which waited for: 3 -> 4; matrix products, arithmetic and copies ran while one was open for 14% -> 10% of each run, Pallas kernels for 0% -> 27%
where the time goes in v1:
time: 1440 us; the launch traced here: 1430 us
  Pallas kernels  779 us (54%)
  waiting for transfers between devices  331 us (23%)
  local copies, waits for them, and re-layouts  131 us (9%)
  other arithmetic  94 us (7%)
  starting transfers between devices  55.3 us (4%)
  blocking collectives  21.1 us (1%)
  between operations  17.7 us (1%)
    ppermute x3, waiting for transfers between devices, to_owner(): return mine[quarter:] + lax.ppermute(mine[:quarter], 'ep', ep_perm)  253 us
    pallas_call x2, Pallas kernels, dispatch(): pl.pallas_call(functools.partial(dispatch_kernel, scaled, n_exp), out_sha...  172 us
    pallas_call x2, Pallas kernels, combine(): pl.pallas_call(functools.partial(combine_kernel, weighted, n_exp), out_sh...  156 us
    pallas_call x1, Pallas kernels, inward_tiles(): pl.pallas_call(inward_kernel, out_shape=[jax.ShapeDtypeStruct((rows, mid)...  155 us
    pallas_call x1, Pallas kernels, forward_tiles(): pl.pallas_call(forward_kernel, out_shape=[jax.ShapeDtypeStruct((rows, mid...  153 us
    pallas_call x1, Pallas kernels, grad_tiles(): pl.pallas_call(grads_kernel, out_shape=[jax.ShapeDtypeStruct((n_exp, widt...  143 us
    unnamed x56, local copies, waits for them, and re-layouts  79.9 us
    ppermute x3, starting transfers between devices, to_owner(): return mine[quarter:] + lax.ppermute(mine[:quarter], 'ep', ep_perm)  52 us
  transfers between devices with their start and end apart: 12, of which 4 were waited for; matrix products, arithmetic and copies ran while one was open for 10% of the time, Pallas kernels for 27%

profile of v1, /device:TPU:0, one launch (start us, length us, event | category | flops | bytes accessed | tf_op | source)
XLA Modules:
  0.0 1433.3 jit_solution(339174213948593174)
XLA Ops:
  11.7 4.3 fusion.2
  19.9 21.1 %all-gather.1 = f32[8,17,1024]{2,1,0:T(8,128)S(1)} all-gather(f32[1,17,1024]{2,1,0:T(8,128)S(1)} %maximum_bitcast_fusion), channel_id=2, replica_groups=mesh['ep'=2,'dp'=4] {'dp','ep'}, dimensions={0}, use_global_device_ids=true | all-gather | bytes 626688 | tf_op jit(solution)/shard_map/all_gather | solution.py:490
  52.3 4.7 broadcast_add_fusion
  57.0 3.5 copy.52.pos
  62.3 4.5 compare_select_fusion.1
  70.4 13.0 and_convert_fusion
  84.6 7.0 select_select_fusion
  91.6 6.8 convert_add_fusion.2
  100.9 41.4 %all-gather.8.cloned.1.call-done.src = bf16[8192,1536]{1,0:T(8,128)(2,1)} async-done(((bf16[1024,1536]{1,0:T(8,128)(2,1)}), bf16[8192,1536]{1,0:T(8,128)(2,1)}) %all-gather.8.cloned.1.call-update) | async-done | bytes 25165840 | tf_op jit(solution)/shard_map/all_gather | solution.py:491
  142.2 83.1 %dispatch.1.x.x0.x1 = bf16[38400,1536]{1,0:T(8,128)(2,1)} custom-call(s32[32]{0:T(128)} %add.318.order, s32[32]{0:T(128)} %get-tuple-element.118.n_chunk, s32[320]{0:T(512)} %copy-done.17, s32[320]{0:T(512)} %sub.176.seg_src, s32[320]{0:T(512)} %get-tuple-element.55.seg_dst, s32[10]{0:T(128)} %get-tuple-element.49.tail_at, s32[10]{0:T(128)} %get-tuple-element.73.tail_len, ...), custom_call_target="tpu_custom_call" | custom-call | flops 20000000000 | bytes 80000000 | tf_op jit(solution)/shard_map/dispatch/pallas_call | solution.py:100
  225.4 153.2 %forward_tiles.1 = (f32[38400,512]{1,0:T(8,128)}, f32[38400,512]{1,0:T(8,128)}, bf16[38400,512]{1,0:T(8,128)(2,1)}, bf16[38400,1536]{1,0:T(8,128)(2,1)}) custom-call(s32[150]{0:T(256)} %get-tuple-element.135.tile_exp, s32[150]{0:T(256)} %copy-done.22, s32[150]{0:T(256)} %get-tuple-element.52.own_at, s32[150]{0:T(256)} %get-tuple-element.51.tile_kind, ...), custom_call_target="tpu_custom_call" | custom-call | flops 70000001024 | bytes 250000000 | tf_op jit(solution)/shard_map/forward_tiles/pallas_call | solution.py:300
  378.6 88.8 %dispatch_scaled.1.d_rows.d0.d1 = bf16[38400,1536]{1,0:T(8,128)(2,1)} custom-call(s32[32]{0:T(128)} %add.318.order, s32[32]{0:T(128)} %get-tuple-element.118.n_chunk, s32[320]{0:T(512)} %copy-done.17, s32[320]{0:T(512)} %sub.176.seg_src, s32[320]{0:T(512)} %get-tuple-element.55.seg_dst, s32[10]{0:T(128)} %get-tuple-element.49.tail_at, ...), custom_call_target="tpu_custom_call" | custom-call | flops 20000000000 | bytes 80000000 | tf_op jit(solution)/shard_map/dispatch_scaled/pallas_call | solution.py:100
  467.4 155.1 %inward_tiles.1 = (bf16[38400,512]{1,0:T(8,128)(2,1)}, bf16[38400,512]{1,0:T(8,128)(2,1)}, bf16[38400,1536]{1,0:T(8,128)(2,1)}) custom-call(s32[150]{0:T(256)} %get-tuple-element.135.tile_exp, s32[150]{0:T(256)} %copy-done.22, s32[150]{0:T(256)} %get-tuple-element.52.own_at, s32[150]{0:T(256)} %get-tuple-element.51.tile_kind, ...), custom_call_target="tpu_custom_call" | custom-call | flops 60000002048 | bytes 250000000 | tf_op jit(solution)/shard_map/inward_tiles/pallas_call | solution.py:325
  622.5 142.9 %grad_tiles.1 = (bf16[10,1536,512]{2,1,0:T(8,128)(2,1)}, bf16[10,1536,512]{2,1,0:T(8,128)(2,1)}, bf16[10,512,1536]{2,1,0:T(8,128)(2,1)}) custom-call(s32[80]{0:T(128)} %get-tuple-element.43.pair_tile, s32[80]{0:T(128)} %get-tuple-element.42.pair_next, s32[80]{0:T(128)} %copy-done.21, s32[80]{0:T(128)} %get-tuple-element.40.pair_kind, ...), custom_call_target="tpu_custom_call" | custom-call | flops 85000003584 | bytes 250000000 | tf_op jit(solution)/shard_map/grad_tiles/pallas_call | solution.py:354
  772.1 51.0 %combine.1 = f32[4096,1536]{1,0:T(8,128)} custom-call(s32[32]{0:T(128)} %add.318.order, s32[32]{0:T(128)} %get-tuple-element.119.n_mix, s32[320]{0:T(512)} %copy-done.17, s32[320]{0:T(512)} %sub.176.seg_src, s32[320]{0:T(512)} %get-tuple-element.55.seg_dst, bf16[38400,1536]{1,0:T(8,128)(2,1)} %get-tuple-element.23.rows, ...), custom_call_target="tpu_custom_call" | custom-call | flops 10000000000 | bytes 60000000 | tf_op jit(solution)/shard_map/combine/pallas_call | solution.py:196
  823.1 10.3 slice.188
  833.4 105.4 %combine_weighted.1 = (f32[4096,1536]{1,0:T(8,128)}, f32[16,256,8]{2,1,0:T(8,128)}) custom-call(s32[32]{0:T(128)} %add.318.order, s32[32]{0:T(128)} %get-tuple-element.119.n_mix, s32[320]{0:T(512)} %copy-done.17, s32[320]{0:T(512)} %sub.176.seg_src, s32[320]{0:T(512)} %get-tuple-element.55.seg_dst, bf16[38400,1536]{1,0:T(8,128)(2,1)} %get-tuple-element.19.rows, ...), custom_call_target="tpu_custom_call" | custom-call | flops 30000001024 | bytes 60000000 | tf_op jit(solution)/shard_map/combine_weighted/pallas_call | solution.py:196
  938.8 10.4 slice.102
  952.2 9.6 slice_add_fusion
  961.8 3.3 slice.190
  965.2 3.3 copy-done.4
  968.5 49.2 %collective-permute-start.3 = (f32[1024,1536]{1,0:T(8,128)}, f32[1024,1536]{1,0:T(8,128)}, u32[]{:S(2)}, u32[]{:S(2)}) collective-permute-start(f32[1024,1536]{1,0:T(8,128)} %slice.190), channel_id=1, source_target_pairs={{0,4},{4,0},{1,5},{5,1},{2,6},{6,2},{3,7},{7,3}} | collective-permute-start | bytes 18874376 | tf_op jit(solution)/shard_map/ppermute | solution.py:451
  1017.7 5.9 slice_add_fusion.1
  1023.7 3.1 slice.184
  1026.8 3.7 copy-done.3
  1046.5 253.0 %collective-permute-done.5 = f32[4,256,8]{2,1,0:T(8,128)} collective-permute-done((f32[4,256,8]{2,1,0:T(8,128)}, f32[4,256,8]{2,1,0:T(8,128)}, u32[]{:S(2)}, u32[]{:S(2)}) %collective-permute-start.5) | collective-permute-done | bytes 32800 | tf_op jit(solution)/shard_map/ppermute | solution.py:451
  1306.4 7.8 fusion.9
  1317.0 7.5 fusion.8
  1324.6 34.8 %all-reduce.3.cloned.1.call-done = f32[1536,40]{0,1:T(8,128)} async-done(((f32[1536,40]{0,1:T(8,128)}), f32[1536,40]{0,1:T(8,128)}) %all-reduce.3.cloned.1.call-update) | async-done | bytes 245776 | tf_op jit(solution)/shard_map/psum | solution.py:530
  1361.1 21.4 %copy.67 = bf16[20,1536,512]{2,1,0:T(8,128)(2,1)} copy(bf16[20,1536,512]{2,1,0:T(8,128)(2,1)} %all-gather.12.cloned.1.call-done) | data formatting | bytes 62914560
  1382.4 21.4 %copy.68 = bf16[20,1536,512]{2,1,0:T(8,128)(2,1)} copy(bf16[20,1536,512]{2,1,0:T(8,128)(2,1)} %all-gather.14.cloned.1.call-done) | data formatting | bytes 62914560
  1403.8 21.6 %copy.69 = bf16[20,512,1536]{2,1,0:T(8,128)(2,1)} copy(bf16[20,512,1536]{2,1,0:T(8,128)(2,1)} %all-gather.16.cloned.1.call-done) | data formatting | bytes 62914560
  (161 shorter events, 63.6 us)
Async XLA Ops:
  7.2 9.8 copy-start
  7.2 135.1 %all-gather.8.cloned.1.call-start = ((), (), s32[]{:S(2)}) async-start(), calls=%async_computation | async-start | bytes 28311552 | tf_op jit(solution)/shard_map/all_gather | solution.py:491
  16.1 1.9 copy-start.1
  16.1 3.3 copy-start.13
  16.1 362.5 %all-gather.10.cloned.1.call-start = ((), (), s32[]{:S(2)}) async-start(), calls=%async_computation.1 | async-start | bytes 28311552 | tf_op jit(solution)/shard_map/all_gather | solution.py:493
  16.9 1307.7 %all-gather.12.cloned.1.call-start = ((), (), s32[]{:S(2)}) async-start(), calls=%async_computation.3 | async-start | bytes 47185920 | tf_op jit(solution)/shard_map/all_gather | solution.py:524
  41.0 11.3 copy-start.7
  61.0 81.2 %copy-start.17 = (s32[320]{0:T(512)}, s32[320]{0:T(512)S(1)}, u32[]{:S(2)}) copy-start(s32[320]{0:T(512)S(1)} %get-tuple-element.56.seg_len) | copy-start | bytes 3844
  61.6 163.8 %copy-start.22 = (s32[150]{0:T(256)}, s32[150]{0:T(256)S(1)}, u32[]{:S(2)}) copy-start(s32[150]{0:T(256)S(1)} %iota_minimum_fusion.tile_at) | copy-start | bytes 1804
  69.7 155.7 %copy-start.21 = (s32[80]{0:T(128)}, s32[80]{0:T(128)S(1)}, u32[]{:S(2)}) copy-start(s32[80]{0:T(128)S(1)} %convert_reduce_fusion.4.pair_exp) | copy-start | bytes 964
  765.4 559.2 %all-gather.14.cloned.1.call-start = ((), (), s32[]{:S(2)}) async-start(), calls=%async_computation.4 | async-start | bytes 47185920 | tf_op jit(solution)/shard_map/all_gather | solution.py:524
  766.0 558.6 %all-gather.16.cloned.1.call-start = ((), (), s32[]{:S(2)}) async-start(), calls=%async_computation.5 | async-start | bytes 47185920 | tf_op jit(solution)/shard_map/all_gather | solution.py:524
  766.6 592.8 %all-reduce.3.cloned.1.call-start = ((), (), s32[]{:S(2)}) async-start(), calls=%async_computation.2 | async-start | bytes 491520 | tf_op jit(solution)/shard_map/psum | solution.py:530
  833.4 118.8 %collective-permute-start.2 = (f32[2048,1536]{1,0:T(8,128)}, f32[2048,1536]{1,0:T(8,128)}, u32[]{:S(2)}, u32[]{:S(2)}) collective-permute-start(f32[2048,1536]{1,0:T(8,128)} %slice.188), channel_id=1, source_target_pairs={{0,1},{1,0},{2,3},{3,2},{4,5},{5,4},{6,7},{7,6}} | collective-permute-start | bytes 37748744 | tf_op jit(solution)/shard_map/ppermute | solution.py:449
  949.2 68.5 %collective-permute-start = (f32[2048,1536]{1,0:T(8,128)}, f32[2048,1536]{1,0:T(8,128)S(1)}, u32[]{:S(2)}, u32[]{:S(2)}) collective-permute-start(f32[2048,1536]{1,0:T(8,128)} %slice.102), channel_id=1, source_target_pairs={{0,1},{1,0},{2,3},{3,2},{4,5},{5,4},{6,7},{7,6}} | collective-permute-start | bytes 37748744 | tf_op jit(solution)/shard_map/ppermute | solution.py:449
  961.8 6.7 copy-start.4
  968.5 337.1 %collective-permute-start.3 = (f32[1024,1536]{1,0:T(8,128)}, f32[1024,1536]{1,0:T(8,128)}, u32[]{:S(2)}, u32[]{:S(2)}) collective-permute-start(f32[1024,1536]{1,0:T(8,128)} %slice.190), channel_id=1, source_target_pairs={{0,4},{4,0},{1,5},{5,1},{2,6},{6,2},{3,7},{7,3}} | collective-permute-start | bytes 18874376 | tf_op jit(solution)/shard_map/ppermute | solution.py:451
  1023.7 6.8 copy-start.3
  1023.7 11.9 copy-start.12
  1030.5 272.3 %copy-start.14 = (s32[1024,8]{0,1:T(8,128)S(1)}, s32[1024,8]{0,1:T(8,128)}, u32[]{:S(2)}) copy-start(s32[1024,8]{0,1:T(8,128)} %param.10) | copy-start | bytes 98308
  1030.5 272.5 %copy-start.11 = (f32[1024,40]{0,1:T(8,128)S(1)}, f32[1024,40]{0,1:T(8,128)}, u32[]{:S(2)}) copy-start(f32[1024,40]{0,1:T(8,128)} %copy-done.10) | copy-start | bytes 491524
  1030.5 272.7 %copy-start.2 = (bf16[1024,1536]{1,0:T(8,128)(2,1)S(1)}, bf16[1024,1536]{1,0:T(8,128)(2,1)}, u32[]{:S(2)}) copy-start(bf16[1024,1536]{1,0:T(8,128)(2,1)} %fusion.2) | copy-start | bytes 9437188
  1030.5 283.7 %collective-permute-start.1 = (f32[1024,1536]{1,0:T(8,128)}, f32[1024,1536]{1,0:T(8,128)}, u32[]{:S(2)}, u32[]{:S(2)}) collective-permute-start(f32[1024,1536]{1,0:T(8,128)} %slice.184), channel_id=1, source_target_pairs={{0,4},{4,0},{1,5},{5,1},{2,6},{6,2},{3,7},{7,3}} | collective-permute-start | bytes 18874376 | tf_op jit(solution)/shard_map/ppermute | solution.py:451
  1038.1 1.2 collective-permute-start.4
  1045.0 254.4 %collective-permute-start.5 = (f32[4,256,8]{2,1,0:T(8,128)}, f32[4,256,8]{2,1,0:T(8,128)}, u32[]{:S(2)}, u32[]{:S(2)}) collective-permute-start(f32[4,256,8]{2,1,0:T(8,128)} %slice.192), channel_id=1, source_target_pairs={{0,4},{4,0},{1,5},{5,1},{2,6},{6,2},{3,7},{7,3}} | collective-permute-start | bytes 98312 | tf_op jit(solution)/shard_map/ppermute | solution.py:451
  1302.8 2.8 copy-start.16
  1304.5 9.7 slice-start
  1305.5 8.7 slice-start.1
  1305.5 10.6 slice-start.2
  1305.5 11.5 copy-start.6
  1305.5 11.5 copy-start.19
  1305.6 11.5 copy-start.20
  (6 other events, 5.8 us)
Sparse Core Ops, SparseCore 0:
  16.2 125.9 all-gather.7
  144.0 119.6 all-gather.9
  765.5 108.0 all-gather.11
  875.0 44.7 all-gather.13
  921.2 69.4 all-gather.15
  1304.6 54.7 all-reduce.2

commit v2 on v1

v2 whole, which is shorter than its diff:
```python
import functools

import jax
import jax.numpy as jnp
from jax import lax
from jax.experimental import pallas as pl
from jax.experimental.pallas import tpu as pltpu
from jax.sharding import PartitionSpec as P


AUX_COEF = 0.001
NORM_EPS = 1e-6
MAX_HITS = 416
BLOCK = 256
GROUP = 16
TILE = 512
HALF = TILE // 2
CHUNK = 256
MIX = 256
NT_DIMS = (((1,), (1,)), ((), ()))
TN_DIMS = (((0,), (0,)), ((), ()))
VMEM_LIMIT = 60 * 1024 * 1024


def norm_forward(tokens32, gain32):
    inv_rms = lax.rsqrt(jnp.mean(tokens32 * tokens32, axis=1, keepdims=True) + NORM_EPS)
    return inv_rms, (tokens32 * inv_rms * gain32).astype(jnp.bfloat16)


def norm_backward(tokens32, inv_rms, gain32, d_normed):
    d_scaled = d_normed * gain32
    return inv_rms * (d_scaled - tokens32 * (inv_rms * inv_rms) * jnp.mean(d_scaled * tokens32, axis=1, keepdims=True))


def dot32(left, right, dims=(((1,), (0,)), ((), ()))):
    return lax.dot_general(left, right, dims, preferred_element_type=jnp.float32)


def dispatch_kernel(scaled, n_exp, order, n_chunk, seg_len, seg_src, seg_dst, tail_at, tail_len, src, pos, gates, out, stack, blank, sems, tail_sem):
    step = pl.program_id(0)
    last = pl.num_programs(0) - 1
    slot = lax.rem(step, 2)

    def segment_copy(blk, buf, exp, grp):
        at = blk * n_exp + exp
        from_row = pl.multiple_of((seg_src[at] + grp) * GROUP, GROUP)
        to_row = pl.multiple_of((seg_dst[at] + grp) * GROUP, GROUP)
        return pltpu.make_async_copy(stack.at[buf, pl.ds(from_row, GROUP), :], out.at[pl.ds(to_row, GROUP), :], sems.at[buf])

    def each_segment(blk, buf, act):
        for exp in range(n_exp):
            @pl.loop(0, seg_len[blk * n_exp + exp])
            def _(grp):
                act(segment_copy(blk, buf, exp, grp))

    def each_tail(act):
        for exp in range(n_exp):
            @pl.loop(0, tail_len[exp])
            def _(grp):
                to_row = pl.multiple_of((tail_at[exp] + grp) * GROUP, GROUP)
                act(pltpu.make_async_copy(blank, out.at[pl.ds(to_row, GROUP), :], tail_sem))

    @pl.when(step == 0)
    def _():
        blank[...] = jnp.zeros_like(blank)
        each_tail(lambda copy: copy.start())

    @pl.when(step >= 2)
    def _():
        each_segment(step - 2, slot, lambda copy: copy.wait())

    @pl.loop(0, n_chunk[step])
    def _(chunk):
        row = lax.broadcasted_iota(jnp.int32, (CHUNK, BLOCK), 0) + chunk * CHUNK
        hit = pos[0, 0:1, :] == row
        if scaled:
            weight = jnp.where(hit, gates[0, 0:1, :], 0.0)
        for k in range(1, pos.shape[1]):
            here = pos[0, k:k + 1, :] == row
            hit = jnp.logical_or(hit, here)
            if scaled:
                weight = jnp.where(here, gates[0, k:k + 1, :], weight)
        picked = dot32(jnp.where(hit, 1.0, 0.0).astype(jnp.bfloat16), src[...])
        if scaled:
            picked = picked * jnp.sum(weight, axis=1, keepdims=True)
        stack[slot, pl.ds(pl.multiple_of(chunk * CHUNK, CHUNK), CHUNK), :] = picked.astype(jnp.bfloat16)

    each_segment(step, slot, lambda copy: copy.start())

    @pl.when(step == last)
    def _():
        each_segment(step - 1, 1 - slot, lambda copy: copy.wait())
        each_segment(step, slot, lambda copy: copy.wait())
        each_tail(lambda copy: copy.wait())


def dispatch(src, pos, gates, plan, rows, scaled):
    blocks, top_k, _ = pos.shape
    width = src.shape[1]
    n_exp = plan["tail_at"].shape[0]
    stack_rows = -(-(BLOCK * top_k + n_exp * (GROUP - 1)) // CHUNK) * CHUNK
    return pl.pallas_call(
        functools.partial(dispatch_kernel, scaled, n_exp),
        out_shape=jax.ShapeDtypeStruct((rows, width), jnp.bfloat16),
        grid_spec=pltpu.PrefetchScalarGridSpec(
            num_scalar_prefetch=7,
            grid=(blocks,),
            in_specs=[
                pl.BlockSpec((BLOCK, width), lambda i, order, *_: (order[i], 0)),
                pl.BlockSpec((1, top_k, BLOCK), lambda i, *_: (i, 0, 0)),
                pl.BlockSpec((1, top_k, BLOCK), lambda i, *_: (i, 0, 0)),
            ],
            out_specs=pl.BlockSpec(memory_space=pl.ANY),
            scratch_shapes=[
                pltpu.VMEM((2, stack_rows, width), jnp.bfloat16),
                pltpu.VMEM((GROUP, width), jnp.bfloat16),
                pltpu.SemaphoreType.DMA((2,)),
                pltpu.SemaphoreType.DMA,
            ],
        ),
        compiler_params=pltpu.CompilerParams(dimension_semantics=("arbitrary",), vmem_limit_bytes=VMEM_LIMIT),
        cost_estimate=pl.CostEstimate(flops=20_000_000_000, bytes_accessed=80_000_000, transcendentals=0),
        name="dispatch_scaled" if scaled else "dispatch",
    )(plan["order"], plan["n_chunk"], plan["seg_len"], plan["seg_src"], plan["seg_dst"], plan["tail_at"], plan["tail_len"], src, pos, gates)


def combine_kernel(weighted, n_exp, order, n_mix, seg_len, seg_src, seg_dst, rows, pos, gates, d_out, *rest):
    if weighted:
        away, far, near, d_gates, stack, total, sems = rest
    else:
        away, far, near, stack, total, sems = rest
    step = pl.program_id(0)
    blocks = pl.num_programs(0)
    slot = lax.rem(step, 2)

    def each_segment(blk, buf, act):
        for exp in range(n_exp):
            @pl.loop(0, seg_len[blk * n_exp + exp])
            def _(grp):
                at = blk * n_exp + exp
                to_row = pl.multiple_of((seg_src[at] + grp) * GROUP, GROUP)
                from_row = pl.multiple_of((seg_dst[at] + grp) * GROUP, GROUP)
                act(pltpu.make_async_copy(rows.at[pl.ds(from_row, GROUP), :], stack.at[buf, pl.ds(to_row, GROUP), :], sems.at[buf]))

    @pl.when(step == 0)
    def _():
        @pl.loop(0, stack.shape[1] // MIX)
        def _(part):
            stack[:, pl.ds(pl.multiple_of(part * MIX, MIX), MIX), :] = jnp.zeros((2, MIX, stack.shape[2]), stack.dtype)

        each_segment(0, 0, lambda copy: copy.start())

    @pl.when(step < blocks - 1)
    def _():
        each_segment(step + 1, 1 - slot, lambda copy: copy.start())

    each_segment(step, slot, lambda copy: copy.wait())
    total[...] = jnp.zeros_like(total)
    if weighted:
        d_gates[...] = jnp.zeros_like(d_gates)

    @pl.loop(0, n_mix[step])
    def _(part):
        col = lax.broadcasted_iota(jnp.int32, (BLOCK, MIX), 1) + part * MIX
        part_rows = stack[slot, pl.ds(pl.multiple_of(part * MIX, MIX), MIX), :]
        top_k = pos.shape[2]
        if weighted:
            cross = dot32(d_out[...], part_rows, NT_DIMS)
            weight = jnp.zeros((BLOCK, MIX), jnp.float32)
            d_cols = []
            for k in range(top_k):
                here = pos[0, :, k:k + 1] == col
                weight = jnp.where(here, gates[0, :, k:k + 1], weight)
                d_cols.append(jnp.sum(jnp.where(here, cross, 0.0), axis=1, keepdims=True))
            d_gates[0] += jnp.concatenate(d_cols, axis=1)
            high = weight.astype(jnp.bfloat16)
            left = weight - high.astype(jnp.float32)
            mid = left.astype(jnp.bfloat16)
            low = (left - mid.astype(jnp.float32)).astype(jnp.bfloat16)
            mixed = dot32(jnp.concatenate([high, mid, low], axis=0), part_rows)
            total[...] += mixed[:BLOCK] + mixed[BLOCK:2 * BLOCK] + mixed[2 * BLOCK:]
        else:
            hit = pos[0, :, 0:1] == col
            for k in range(1, top_k):
                hit = jnp.logical_or(hit, pos[0, :, k:k + 1] == col)
            total[...] += dot32(jnp.where(hit, 1.0, 0.0).astype(jnp.bfloat16), part_rows)

    half, quarter = blocks // 2, blocks // 4

    @pl.when(step < half)
    def _():
        away[...] = total[...]

    @pl.when((step >= half) & (step < half + quarter))
    def _():
        far[...] = total[...]

    @pl.when(step >= half + quarter)
    def _():
        near[...] = total[...]


def combine(rows, pos_t, gates_t, d_out, plan, weighted):
    blocks, _, top_k = pos_t.shape
    width = rows.shape[1]
    n_exp = plan["tail_at"].shape[0]
    stack_rows = -(-(BLOCK * top_k + n_exp * (GROUP - 1)) // MIX) * MIX
    half, quarter = blocks // 2, blocks // 4
    out_shape, out_specs = [], []
    for first, count in ((0, half), (half, quarter), (half + quarter, quarter)):
        out_shape.append(jax.ShapeDtypeStruct((count * BLOCK, width), jnp.float32))
        out_specs.append(pl.BlockSpec((BLOCK, width), lambda i, *_, first=first, count=count: (jnp.clip(i - first, 0, count - 1), 0)))
    if weighted:
        out_shape.append(jax.ShapeDtypeStruct((blocks, BLOCK, top_k), jnp.float32))
        out_specs.append(pl.BlockSpec((1, BLOCK, top_k), lambda i, *_: (i, 0, 0)))
    d_spec = pl.BlockSpec((BLOCK, width), lambda i, order, *_: (order[i], 0)) if weighted else pl.BlockSpec((GROUP, width), lambda i, *_: (0, 0))
    return pl.pallas_call(
        functools.partial(combine_kernel, weighted, n_exp),
        out_shape=out_shape,
        grid_spec=pltpu.PrefetchScalarGridSpec(
            num_scalar_prefetch=5,
            grid=(blocks,),
            in_specs=[
                pl.BlockSpec(memory_space=pl.ANY),
                pl.BlockSpec((1, BLOCK, top_k), lambda i, *_: (i, 0, 0)),
                pl.BlockSpec((1, BLOCK, top_k), lambda i, *_: (i, 0, 0)),
                d_spec,
            ],
            out_specs=out_specs,
            scratch_shapes=[
                pltpu.VMEM((2, stack_rows, width), jnp.bfloat16),
                pltpu.VMEM((BLOCK, width), jnp.float32),
                pltpu.SemaphoreType.DMA((2,)),
            ],
        ),
        compiler_params=pltpu.CompilerParams(dimension_semantics=("arbitrary",), vmem_limit_bytes=VMEM_LIMIT),
        cost_estimate=pl.CostEstimate(flops=70_000_000_000 if weighted else 40_000_000_000, bytes_accessed=60_000_000, transcendentals=0),
        name="combine_weighted" if weighted else "combine",
    )(plan["order"], plan["n_mix"], plan["seg_len"], plan["seg_src"], plan["seg_dst"], rows, pos_t, gates_t, d_out)


def by_kind(kind, body):
    for code, rows in ((1, HALF), (2, TILE)):
        @pl.when(kind == code)
        def _():
            body(pl.ds(0, rows))


def forward_kernel(tile_exp, tile_at, own_at, tile_kind, own_kind, x, w_gate, w_up, w_down, act_gate, act_up, hidden, result):
    step = pl.program_id(0)

    def first(part):
        a = dot32(x[part], w_gate[0])
        b = dot32(x[part], w_up[0])
        act_gate[part] = a
        act_up[part] = b
        hidden[part] = (a * jax.nn.sigmoid(a) * b).astype(jnp.bfloat16)

    def second(part):
        result[part] = dot32(hidden[part], w_down[0]).astype(jnp.bfloat16)

    by_kind(tile_kind[step], first)
    by_kind(own_kind[step], second)


def inward_kernel(own, tile_exp, tile_at, tile_kind, d_rows, act_gate, act_up, *rest):
    if own:
        w_gate, w_up, w_down, d_gate, d_up, d_in = rest
    else:
        w_down, _, _, d_gate, d_up = rest

    def body(part):
        d_hidden = dot32(d_rows[part], w_down[0], NT_DIMS)
        a = act_gate[part]
        sig = jax.nn.sigmoid(a)
        d_a = (d_hidden * act_up[part] * sig * (1.0 + a * (1.0 - sig))).astype(jnp.bfloat16)
        d_b = (d_hidden * (a * sig)).astype(jnp.bfloat16)
        d_gate[part] = d_a
        d_up[part] = d_b
        if own:
            d_in[part] = (dot32(d_a, w_gate[0], NT_DIMS) + dot32(d_b, w_up[0], NT_DIMS)).astype(jnp.bfloat16)

    by_kind(tile_kind[pl.program_id(0)], body)


def grads_kernel(lefts, tile_exp, tile_at, tile_kind, tile_first, tile_last, base, *refs):
    n = len(lefts)
    left_refs, right_refs = refs[:max(lefts) + 1], refs[max(lefts) + 1:max(lefts) + 1 + n]
    outs, wholes, totals = refs[-3 * n:-2 * n], refs[-2 * n:-n], refs[-n:]
    step = pl.program_id(0)

    @pl.when(tile_first[step] > 0)
    def _():
        for total in totals:
            total[...] = jnp.zeros_like(total)

    def body(part):
        for which, right, total in zip(lefts, right_refs, totals):
            total[...] += dot32(left_refs[which][part], right[part], TN_DIMS)

    by_kind(tile_kind[step], body)

    @pl.when(tile_last[step] > 0)
    def _():
        for out, whole, total in zip(outs, wholes, totals):
            rounded = total[...].astype(jnp.bfloat16)
            out[0] = rounded
            whole[0] = rounded


def kernel_params():
    return pltpu.CompilerParams(dimension_semantics=("arbitrary",), vmem_limit_bytes=VMEM_LIMIT)


def forward_tiles(x, w_gate, w_up, w_down, plan):
    rows, width = x.shape
    mid = w_gate.shape[2]
    wide = pl.BlockSpec((TILE, width), lambda t, exp, at, own, *_: (at[t], 0))
    thin = pl.BlockSpec((TILE, mid), lambda t, exp, at, own, *_: (at[t], 0))
    owned = pl.BlockSpec((TILE, width), lambda t, exp, at, own, *_: (own[t], 0))
    w_in = pl.BlockSpec((1, width, mid), lambda t, exp, *_: (exp[t], 0, 0))
    w_out = pl.BlockSpec((1, mid, width), lambda t, exp, *_: (exp[t], 0, 0))
    return pl.pallas_call(
        forward_kernel,
        out_shape=[
            jax.ShapeDtypeStruct((rows, mid), jnp.float32),
            jax.ShapeDtypeStruct((rows, mid), jnp.float32),
            jax.ShapeDtypeStruct((rows, mid), jnp.bfloat16),
            jax.ShapeDtypeStruct((rows, width), jnp.bfloat16),
        ],
        grid_spec=pltpu.PrefetchScalarGridSpec(num_scalar_prefetch=5, grid=(rows // TILE,), in_specs=[wide, w_in, w_in, w_out], out_specs=[thin, thin, thin, owned]),
        compiler_params=kernel_params(),
        cost_estimate=pl.CostEstimate(flops=120_000_000_000, bytes_accessed=250_000_000, transcendentals=0),
        name="forward_tiles",
    )(plan["tile_weight"], plan["tile_at"], plan["own_at"], plan["tile_kind"], plan["own_kind"], x, w_gate, w_up, w_down)


def inward_tiles(d_rows, act_gate, act_up, w_gate, w_up, w_down, plan, begun):
    own = begun is None
    rows, width = d_rows.shape
    mid = w_gate.shape[2]
    wide = pl.BlockSpec((TILE, width), lambda t, exp, at, *_: (at[t], 0))
    thin = pl.BlockSpec((TILE, mid), lambda t, exp, at, *_: (at[t], 0))
    w_in = pl.BlockSpec((1, width, mid), lambda t, exp, *_: (exp[t], 0, 0))
    w_out = pl.BlockSpec((1, mid, width), lambda t, exp, *_: (exp[t], 0, 0))
    kept = pl.BlockSpec(memory_space=pl.ANY)
    thin_shape = jax.ShapeDtypeStruct((rows, mid), jnp.bfloat16)
    seq = plan["own_seq"] if own else plan["other_seq"]
    return pl.pallas_call(
        functools.partial(inward_kernel, own),
        out_shape=[thin_shape, thin_shape] + ([jax.ShapeDtypeStruct((rows, width), jnp.bfloat16)] if own else []),
        grid_spec=pltpu.PrefetchScalarGridSpec(
            num_scalar_prefetch=3,
            grid=(seq[0].shape[0],),
            in_specs=[wide, thin, thin] + ([w_in, w_in, w_out] if own else [w_out, kept, kept]),
            out_specs=[thin, thin] + ([wide] if own else []),
        ),
        input_output_aliases={} if own else {7: 0, 8: 1},
        compiler_params=kernel_params(),
        cost_estimate=pl.CostEstimate(flops=90_000_000_000 if own else 45_000_000_000, bytes_accessed=150_000_000, transcendentals=0),
        name="inward_own" if own else "inward_other",
    )(*seq, d_rows, act_gate, act_up, *((w_gate, w_up, w_down) if own else (w_down, *begun)))


def grad_tiles(lefts, left_arrays, right_arrays, plan):
    n_exp = plan["tail_at"].shape[0]
    rows = plan["tile_at"].shape[0] * TILE
    shapes = [(left_arrays[which].shape[1], right.shape[1]) for which, right in zip(lefts, right_arrays)]
    in_specs = [pl.BlockSpec((TILE, array.shape[1]), lambda t, exp, at, *_: (at[t], 0)) for array in (*left_arrays, *right_arrays)]
    alone = [pl.BlockSpec((1, *shape), lambda t, exp, *_: (exp[t], 0, 0)) for shape in shapes]
    whole = [pl.BlockSpec((1, *shape), lambda t, exp, at, kind, first, last, base: (base[0] + exp[t], 0, 0)) for shape in shapes]
    return pl.pallas_call(
        functools.partial(grads_kernel, lefts),
        out_shape=[jax.ShapeDtypeStruct((n_exp, *shape), jnp.bfloat16) for shape in shapes]
        + [jax.ShapeDtypeStruct((2 * n_exp, *shape), jnp.bfloat16) for shape in shapes],
        grid_spec=pltpu.PrefetchScalarGridSpec(
            num_scalar_prefetch=6,
            grid=(rows // TILE,),
            in_specs=in_specs,
            out_specs=alone + whole,
            scratch_shapes=[pltpu.VMEM(shape, jnp.float32) for shape in shapes],
        ),
        compiler_params=kernel_params(),
        cost_estimate=pl.CostEstimate(flops=45_000_000_000 * len(lefts), bytes_accessed=100_000_000 * len(lefts), transcendentals=0),
    )(plan["tile_exp"], plan["tile_at"], plan["tile_kind"], plan["tile_first"], plan["tile_last"], plan["base"], *left_arrays, *right_arrays)


def merge_kernel(base, whole_in, other, whole):
    whole[...] = other[...]


def merge(whole, other, other_base):
    n_exp, *shape = other.shape
    return pl.pallas_call(
        merge_kernel,
        out_shape=jax.ShapeDtypeStruct(whole.shape, whole.dtype),
        grid_spec=pltpu.PrefetchScalarGridSpec(
            num_scalar_prefetch=1,
            grid=(n_exp,),
            in_specs=[pl.BlockSpec(memory_space=pl.ANY), pl.BlockSpec((1, *shape), lambda i, base: (i, 0, 0))],
            out_specs=pl.BlockSpec((1, *shape), lambda i, base: (base[0] + i, 0, 0)),
        ),
        input_output_aliases={1: 0},
        compiler_params=pltpu.CompilerParams(dimension_semantics=("arbitrary",), vmem_limit_bytes=16 * 1024 * 1024),
        cost_estimate=pl.CostEstimate(flops=8_000_000_000, bytes_accessed=30_000_000, transcendentals=0),
        name="merge",
    )(other_base, whole, other)


def exclusive(values, axis=0):
    return jnp.cumsum(values, axis=axis) - values


def make_plan(local_ids, order, own_blocks, n_exp, max_tiles, weight_base):
    onehot = (local_ids[:, :, None, :] == jnp.arange(n_exp)[None, None, :, None]).astype(jnp.float32)
    hits = jnp.sum(onehot, axis=1)
    before = jnp.triu(jnp.ones((BLOCK, BLOCK), jnp.bfloat16), 1)
    rank = jnp.einsum("oet,ts->oes", hits.astype(jnp.bfloat16), before, preferred_element_type=jnp.float32)
    seg_len = (jnp.sum(hits, axis=2).astype(jnp.int32) + GROUP - 1) // GROUP
    seg_src = exclusive(seg_len, 1)
    per_tile, per_half = TILE // GROUP, HALF // GROUP
    groups = jnp.sum(seg_len, axis=0)
    tiles = (groups + per_tile - 1) // per_tile
    tile_base = exclusive(tiles)
    seg_dst = tile_base[None, :] * per_tile + exclusive(seg_len, 0)
    place = rank + (seg_src * GROUP).astype(jnp.float32)[:, :, None]
    pos = jnp.sum(onehot * (place[:, None] + 1.0), axis=2).astype(jnp.int32) - 1
    own_tiles = (jnp.sum(seg_len[:own_blocks], axis=0) + per_tile - 1) // per_tile
    exp_ids = jnp.arange(n_exp)

    def sequence(counts, length):
        ids = jnp.arange(length)
        at = jnp.minimum(ids, jnp.maximum(jnp.sum(counts) - 1, 0))
        ends = jnp.cumsum(counts)
        exp = jnp.minimum(jnp.sum((at[:, None] >= ends[None, :]).astype(jnp.int32), axis=1), n_exp - 1)
        is_exp = (exp[:, None] == exp_ids[None, :]).astype(jnp.int32)
        pick = lambda table: jnp.sum(is_exp * table[None, :], axis=1)
        return exp, at - pick(ends - counts), ids > at, pick

    def kind_of(pick, nth, past):
        left = pick(groups) - nth * per_tile
        return jnp.where(past, 0, jnp.where(left <= per_half, 1, 2))

    exp, nth, past, pick = sequence(tiles, max_tiles)
    kind = kind_of(pick, nth, past)
    own_count = pick(own_tiles)
    max_own = n_exp * (max_tiles // n_exp // 2 + 1)
    o_exp, o_nth, o_past, o_pick = sequence(own_tiles, max_own)
    r_exp, r_nth, r_past, r_pick = sequence(tiles - own_tiles, max_tiles)
    none = jnp.sum(tiles - own_tiles) == 0
    r_exp = jnp.where(none, 0, r_exp)
    r_nth = jnp.where(none, 0, r_nth + r_pick(own_tiles))
    r_kind = jnp.where(none, jnp.where(r_past, 0, jnp.where(groups[0] <= per_half, 1, 2)), kind_of(r_pick, r_nth, r_past))
    r_tile = jnp.where(none, 0, r_pick(tile_base) + r_nth)
    stack_rows = jnp.sum(seg_len, axis=1) * GROUP
    plan = {
        "order": order,
        "n_chunk": (stack_rows + CHUNK - 1) // CHUNK,
        "n_mix": (stack_rows + MIX - 1) // MIX,
        "seg_len": seg_len.reshape(-1),
        "seg_src": seg_src.reshape(-1),
        "seg_dst": seg_dst.reshape(-1),
        "tail_at": tile_base * per_tile + groups,
        "tail_len": (groups + per_half - 1) // per_half * per_half - groups,
        "base": weight_base.reshape(1),
        "tile_exp": exp,
        "tile_weight": exp + weight_base,
        "tile_at": pick(tile_base) + nth,
        "own_at": pick(tile_base) + jnp.minimum(nth, own_count - 1),
        "tile_kind": kind,
        "own_kind": jnp.where(nth < own_count, kind, 0),
        "tile_first": (nth == 0) & ~past,
        "tile_last": (nth == pick(tiles) - 1) & ~past,
        "own_seq": (o_exp + weight_base, o_pick(tile_base) + o_nth, kind_of(o_pick, o_nth, o_past)),
        "other_seq": (r_exp + weight_base, r_tile, r_kind),
    }
    return jax.tree.map(lambda value: value.astype(jnp.int32), plan), pos


def solution(mesh):
    ep_size = mesh.shape["ep"]
    dp_size = mesh.shape["dp"]
    devices = ep_size * dp_size
    cores = 2
    tok_spec = P(("dp", "ep"), None)
    exp_spec = P("ep", None, None)
    core_perm = [(i, i ^ 1) for i in range(dp_size)]
    ep_perm = [(i, i ^ 1) for i in range(ep_size)]

    def to_core(away):
        return lax.ppermute(away, "dp", core_perm)

    def to_ep(far):
        return lax.ppermute(far, "ep", ep_perm)

    def after(value, other):
        return lax.optimization_barrier((value, other))

    def device_step(tokens, d_out, expert_ids, norm_gain, router, w_gate, w_up, w_down):
        tok_rows, _ = tokens.shape
        top_k = expert_ids.shape[1]
        local_experts = w_gate.shape[0]
        experts = local_experts * ep_size
        total_tok = tok_rows * devices
        n_exp = local_experts // cores
        dev_blocks = tok_rows // BLOCK
        own_devs = devices // 2
        own_blocks = own_devs * dev_blocks
        seg_pad = devices * dev_blocks * (GROUP - 1)
        max_tiles = n_exp * -(-(devices * MAX_HITS + seg_pad) // TILE)

        ep_at = lax.axis_index("ep")
        dp_at = lax.axis_index("dp")
        core_at = lax.rem(dp_at, cores)
        x_at = lax.div(dp_at, cores)

        def dev_of(x, core, ep):
            return (x * cores + core) * ep_size + ep

        dev_order = jnp.stack(
            [dev_of(x_at, 1 - core_at, 1 - ep_at), dev_of(x_at, 1 - core_at, ep_at), dev_of(x_at, core_at, 1 - ep_at), dev_of(x_at, core_at, ep_at)]
            + [dev_of(1 - x_at, core, ep) for core in range(cores) for ep in range(ep_size)]
        )
        order = (dev_order[:, None] * dev_blocks + jnp.arange(dev_blocks)[None, :]).reshape(-1).astype(jnp.int32)

        tokens32 = tokens.astype(jnp.float32)
        gain32 = norm_gain.astype(jnp.float32)
        inv_rms, normed = norm_forward(tokens32, gain32)
        logits = jnp.dot(normed, router, preferred_element_type=jnp.float32)
        router_probs = jax.nn.softmax(logits, axis=1)
        expert_hits = expert_ids[:, :, None] == jnp.arange(experts)[None, None, :]
        gate_vals = jnp.sum(jnp.where(expert_hits, router_probs[:, None, :], 0.0), axis=2)

        prob_sums = jnp.pad(jnp.sum(router_probs, axis=0), (0, tok_rows - experts))
        packet = jnp.concatenate([expert_ids.astype(jnp.float32).T, gate_vals.T, prob_sums[None]], axis=0)
        packets = lax.all_gather(packet, ("dp", "ep"))
        all_normed = lax.all_gather(normed, ("dp", "ep"), tiled=True)
        d_out_late, _ = lax.optimization_barrier((d_out, all_normed[:8]))
        all_d_out = lax.all_gather(d_out_late, ("dp", "ep"), tiled=True)

        all_ids = packets[:, :top_k].astype(jnp.int32)
        counts = jnp.sum((all_ids[..., None] == jnp.arange(experts)).astype(jnp.float32), axis=(0, 1, 2))
        expert_frac = counts / (total_tok * top_k)
        aux_loss = AUX_COEF * experts * jnp.sum(expert_frac * jnp.sum(packets[:, 2 * top_k, :experts], axis=0)) / total_tok

        turned = jnp.take(packets, dev_order, axis=0)

        def by_block(rows):
            return rows.reshape(devices, top_k, dev_blocks, BLOCK).transpose(0, 2, 1, 3).reshape(devices * dev_blocks, top_k, BLOCK)

        first_expert = ep_at * local_experts + core_at * n_exp
        block_ids = by_block(turned[:, :top_k]).astype(jnp.int32) - first_expert
        block_ids = jnp.where((block_ids >= 0) & (block_ids < n_exp), block_ids, n_exp)
        block_gates = by_block(turned[:, top_k:2 * top_k])
        plan, pos = make_plan(block_ids, order, own_blocks, n_exp, max_tiles, core_at * n_exp)
        pos_t = pos[:own_blocks].transpose(0, 2, 1)
        gates_t = block_gates[:own_blocks].transpose(0, 2, 1)

        rows = max_tiles * TILE
        x = dispatch(all_normed, pos, block_gates, plan, rows, False)
        act_gate, act_up, hidden, result = forward_tiles(x, w_gate, w_up, w_down, plan)
        away, far, near, d_gate_parts = combine(result, pos_t, gates_t, all_d_out, plan, True)
        all_d_out, away = after(all_d_out, away)
        met = to_core(away)
        half, quarter = own_blocks // 2, own_blocks // 4
        d_gate_met = to_core(d_gate_parts[:half])
        d_rows = dispatch(all_d_out, pos, block_gates, plan, rows, True)
        d_gate_mine = d_gate_parts[half:] + d_gate_met
        d_rows, (far, d_gate_far) = after(d_rows, (far + met[:tok_rows], d_gate_mine[:quarter]))
        crossed = to_ep(far)
        d_gate_crossed = to_ep(d_gate_far)
        d_act_gate, d_act_up, d_expert_in = inward_tiles(d_rows, act_gate, act_up, w_gate, w_up, w_down, plan, None)
        d_away, d_far, d_near = combine(d_expert_in, pos_t, gates_t, all_d_out, plan, False)
        d_act_gate, d_away = after(d_act_gate, d_away)
        d_met = to_core(d_away)
        d_gates = (d_gate_mine[quarter:] + d_gate_crossed).reshape(tok_rows, top_k)
        d_probs = jnp.sum(jnp.where(expert_hits, d_gates[:, :, None], 0.0), axis=1) + (AUX_COEF * experts / total_tok) * expert_frac[None, :]
        d_logits = (router_probs * (d_probs - jnp.sum(router_probs * d_probs, axis=1, keepdims=True))).astype(jnp.bfloat16)
        grad_router = lax.dot_general(normed, d_logits, TN_DIMS, preferred_element_type=jnp.float32)
        d_act_gate, d_act_up = inward_tiles(d_rows, act_gate, act_up, w_gate, w_up, w_down, plan, (d_act_gate, d_act_up))
        d_act_gate, (d_far, grad_router) = after(d_act_gate, (d_far + d_met[:tok_rows], grad_router))
        d_crossed = to_ep(d_far)
        grad_router = lax.psum(grad_router, ("ep", "dp"))
        grad_gate, grad_up, all_gate, all_up = grad_tiles((0, 0), (x,), (d_act_gate, d_act_up), plan)
        hidden, grad_gate = after(hidden, grad_gate)
        grad_down, all_down = grad_tiles((0,), (hidden,), (d_rows,), plan)
        other_base = (1 - core_at).reshape(1).astype(jnp.int32) * n_exp
        all_gate = merge(all_gate, to_core(grad_gate), other_base)
        all_up = merge(all_up, to_core(grad_up), other_base)
        all_down = merge(all_down, to_core(grad_down), other_base)
        layer_out = (tokens32 + (near + met[tok_rows:] + crossed)).astype(jnp.bfloat16)
        d_normed = (d_near + d_met[tok_rows:] + d_crossed) + lax.dot_general(d_logits, router, NT_DIMS, preferred_element_type=jnp.float32)
        d_tokens = (d_out.astype(jnp.float32) + norm_backward(tokens32, inv_rms, gain32, d_normed)).astype(jnp.bfloat16)
        return layer_out, aux_loss.reshape(1), d_tokens, grad_router, all_gate, all_up, all_down

    return jax.shard_map(device_step, mesh=mesh, in_specs=(tok_spec, tok_spec, tok_spec, P(None), P(None, None), exp_spec, exp_spec, exp_spec), out_specs=(tok_spec, P(None), tok_spec, P(None, None), exp_spec, exp_spec, exp_spec), check_vma=False)
```

time: 1440 us -> 1390 us (0.965)
  local copies, waits for them, and re-layouts: 131 us -> 22.4 us
  starting transfers between devices: 55.3 us -> 96.2 us
  Pallas kernels: 779 us -> 806 us
  other arithmetic: 94 us -> 67.5 us
    unnamed x56 -> x73, local copies, waits for them, and re-layouts: 79.9 us -> 4.7 us
    pallas_call x2 -> x7, Pallas kernels: 298 us -> 363 us  [the longest x2 174 us: grad_tiles(): pl.pallas_call(functools.partial(grads_kernel, lefts), out_shape=[jax.Sha...]
    ppermute x6 -> x9, starting transfers between devices: 55.1 us -> 96.1 us  [the longest x3 72.6 us: to_ep(): return lax.ppermute(far, 'ep', ep_perm)]
    psum x1, waiting for transfers between devices: 34.8 us -> 0.01 us  [device_step(): grad_router = lax.psum(grad_router, ('ep', 'dp'))]
    all_gather x1, waiting for transfers between devices: 41.4 us -> 72.2 us  [device_step(): all_normed = lax.all_gather(normed, ('dp', 'ep'), tiled=True)]
    slice x7 -> x3, local copies, waits for them, and re-layouts: 30.7 us -> 2.43 us  [the longest x2 1.59 us: device_step(): d_gate_met = to_core(d_gate_parts[:half])]
    pallas_call x2, Pallas kernels: 172 us -> 144 us  [dispatch(): pl.pallas_call(functools.partial(dispatch_kernel, scaled, n_exp), out_sha...]
    ppermute x6 -> x9, waiting for transfers between devices: 253 us -> 260 us  [the longest x3 260 us: to_ep(): return lax.ppermute(far, 'ep', ep_perm)]
  transfers between devices with their start and end apart: 12 -> 12, of which waited for: 4 -> 3; matrix products, arithmetic and copies ran while one was open for 10% -> 5% of each run, Pallas kernels for 27% -> 28%
where the time goes in v2:
time: 1390 us; the launch traced here: 1370 us
  Pallas kernels  806 us (58%)
  waiting for transfers between devices  333 us (24%)
  starting transfers between devices  96.2 us (7%)
  other arithmetic  67.5 us (5%)
  local copies, waits for them, and re-layouts  22.4 us (2%)
  blocking collectives  20.9 us (2%)
  between operations  19 us (1%)
    ppermute x3, waiting for transfers between devices, to_ep(): return lax.ppermute(far, 'ep', ep_perm)  260 us
    pallas_call x2, Pallas kernels, grad_tiles(): pl.pallas_call(functools.partial(grads_kernel, lefts), out_shape=[jax.Sha...  174 us
    pallas_call x2, Pallas kernels, combine(): pl.pallas_call(functools.partial(combine_kernel, weighted, n_exp), out_sh...  158 us
    pallas_call x2, Pallas kernels, inward_tiles(): pl.pallas_call(functools.partial(inward_kernel, own), out_shape=[thin_sha...  146 us
    pallas_call x2, Pallas kernels, dispatch(): pl.pallas_call(functools.partial(dispatch_kernel, scaled, n_exp), out_sha...  144 us
    pallas_call x1, Pallas kernels, forward_tiles(): pl.pallas_call(forward_kernel, out_shape=[jax.ShapeDtypeStruct((rows, mid...  141 us
    ppermute x3, starting transfers between devices, to_ep(): return lax.ppermute(far, 'ep', ep_perm)  72.6 us
    all_gather x1, waiting for transfers between devices, device_step(): all_normed = lax.all_gather(normed, ('dp', 'ep'), tiled=True)  72.2 us
  transfers between devices with their start and end apart: 12, of which 3 were waited for; matrix products, arithmetic and copies ran while one was open for 5% of the time, Pallas kernels for 28%

profile of v2, /device:TPU:0, one launch (start us, length us, event | category | flops | bytes accessed | tf_op | source)
XLA Modules:
  0.0 1370.6 jit_solution(12939992753109073163)
XLA Ops:
  7.2 2.6 fusion
  11.7 4.3 fusion.2
  19.9 20.9 %all-gather.1 = f32[8,17,1024]{2,1,0:T(8,128)S(1)} all-gather(f32[1,17,1024]{2,1,0:T(8,128)S(1)} %maximum_bitcast_fusion), channel_id=2, replica_groups=mesh['ep'=2,'dp'=4] {'dp','ep'}, dimensions={0}, use_global_device_ids=true | all-gather | bytes 626688 | tf_op jit(solution)/shard_map/all_gather | solution.py:536
  44.6 3.1 copy.55
  47.8 4.7 broadcast_add_fusion
  52.4 3.4 copy.57.pos
  61.3 1.9 copy.58
  66.9 3.1 slice_bitcast_fusion.pos
  70.1 72.2 %all-gather.5.cloned.1.call-done.src = bf16[8192,1536]{1,0:T(8,128)(2,1)} async-done(((bf16[1024,1536]{1,0:T(8,128)(2,1)}), bf16[8192,1536]{1,0:T(8,128)(2,1)}) %all-gather.5.cloned.1.call-update) | async-done | bytes 25165840 | tf_op jit(solution)/shard_map/all_gather | solution.py:537
  142.3 69.0 %dispatch.1.x.refs_0_ = bf16[40960,1536]{1,0:T(8,128)(2,1)} custom-call(s32[32]{0:T(128)} %add.360.order, s32[32]{0:T(128)} %and_select_fusion.6.n_chunk.n_mix, s32[320]{0:T(512)} %copy-done.15, s32[320]{0:T(512)} %sub.225.seg_src, s32[320]{0:T(512)} %get-tuple-element.103.seg_dst, s32[10]{0:T(128)} %get-tuple-element.136.tail_at, ...), custom_call_target="tpu_custom_call" | custom-call | flops 20000000000 | bytes 80000000 | tf_op jit(solution)/shard_map/dispatch/pallas_call | solution.py:102
  211.3 141.5 %forward_tiles.1 = (f32[40960,512]{1,0:T(8,128)}, f32[40960,512]{1,0:T(8,128)}, bf16[40960,512]{1,0:T(8,128)(2,1)}, bf16[40960,1536]{1,0:T(8,128)(2,1)}) custom-call(s32[80]{0:T(128)} %get-tuple-element.144.tile_exp, s32[80]{0:T(128)} %copy-done.33, s32[80]{0:T(128)} %get-tuple-element.123.own_at, s32[80]{0:T(128)} %get-tuple-element.98.tile_kind, ...), custom_call_target="tpu_custom_call" | custom-call | flops 120000004096 | bytes 250000000 | tf_op jit(solution)/shard_map/forward_tiles/pallas_call | solution.py:323
  352.8 105.1 %combine_weighted.1 = (f32[2048,1536]{1,0:T(8,128)}, f32[1024,1536]{1,0:T(8,128)}, f32[1024,1536]{1,0:T(8,128)}, f32[16,256,8]{2,1,0:T(8,128)}) custom-call(s32[32]{0:T(128)} %add.360.order, s32[32]{0:T(128)} %and_select_fusion.6.n_chunk.n_mix, s32[320]{0:T(512)} %copy-done.15, s32[320]{0:T(512)} %sub.225.seg_src, s32[320]{0:T(512)} %get-tuple-element.103.seg_dst, ...), custom_call_target="tpu_custom_call" | custom-call | flops 70000001024 | bytes 60000000 | tf_op jit(solution)/shard_map/combine_weighted/pallas_call | solution.py:217
  457.9 13.6 collective-permute-start
  475.1 74.7 %dispatch_scaled.1.d_rows.refs_1_ = bf16[40960,1536]{1,0:T(8,128)(2,1)} custom-call(s32[32]{0:T(128)} %add.360.order, s32[32]{0:T(128)} %and_select_fusion.6.n_chunk.n_mix, s32[320]{0:T(512)} %copy-done.15, s32[320]{0:T(512)} %sub.225.seg_src, s32[320]{0:T(512)} %get-tuple-element.103.seg_dst, s32[10]{0:T(128)} %get-tuple-element.136.tail_at, ...), custom_call_target="tpu_custom_call" | custom-call | flops 20000000000 | bytes 80000000 | tf_op jit(solution)/shard_map/dispatch_scaled/pallas_call | solution.py:102
  552.2 8.6 slice_add_fusion.2
  560.8 96.2 %inward_own.1 = (bf16[40960,512]{1,0:T(8,128)(2,1)}, bf16[40960,512]{1,0:T(8,128)(2,1)}, bf16[40960,1536]{1,0:T(8,128)(2,1)}) custom-call(s32[50]{0:T(128)} %get-tuple-element.129.tile_exp, s32[50]{0:T(128)} %get-tuple-element.127.tile_at, s32[50]{0:T(128)} %get-tuple-element.126.tile_kind, bf16[40960,1536]{1,0:T(8,128)(2,1)} %dispatch_scaled.1.d_rows.refs_1_, ...), custom_call_target="tpu_custom_call" | custom-call | flops 89999998976 | bytes 150000000 | tf_op jit(solution)/shard_map/inward_own/pallas_call | solution.py:349
  657.0 52.7 %combine.1 = (f32[2048,1536]{1,0:T(8,128)}, f32[1024,1536]{1,0:T(8,128)}, f32[1024,1536]{1,0:T(8,128)}) custom-call(s32[32]{0:T(128)} %add.360.order, s32[32]{0:T(128)} %and_select_fusion.6.n_chunk.n_mix, s32[320]{0:T(512)} %copy-done.15, s32[320]{0:T(512)} %sub.225.seg_src, s32[320]{0:T(512)} %get-tuple-element.103.seg_dst, ...), custom_call_target="tpu_custom_call" | custom-call | flops 40000000000 | bytes 60000000 | tf_op jit(solution)/shard_map/combine/pallas_call | solution.py:217
  709.7 9.4 collective-permute-start.3
  724.3 45.9 %collective-permute-start.4 = (f32[4,256,8]{2,1,0:T(8,128)}, f32[4,256,8]{2,1,0:T(8,128)S(1)}, u32[]{:S(2)}, u32[]{:S(2)}) collective-permute-start(f32[4,256,8]{2,1,0:T(8,128)} %slice.118), channel_id=1, source_target_pairs={{0,4},{4,0},{1,5},{5,1},{2,6},{6,2},{3,7},{7,3}} | collective-permute-start | bytes 98312 | tf_op jit(solution)/shard_map/ppermute | solution.py:494
  770.3 50.1 %inward_other.1 = (bf16[40960,512]{1,0:T(8,128)(2,1)}, bf16[40960,512]{1,0:T(8,128)(2,1)}) custom-call(s32[80]{0:T(128)} %get-tuple-element.130.tile_exp, s32[80]{0:T(128)} %get-tuple-element.122.tile_at, s32[80]{0:T(128)} %get-tuple-element.121.tile_kind, ...), custom_call_target="tpu_custom_call", output_to_operand_aliasing={{0}: (7, {}), {1}: (8, {})} | custom-call | flops 44999999488 | bytes 150000000 | tf_op jit(solution)/shard_map/inward_other/pallas_call | solution.py:349
  825.2 8.6 slice_add_fusion
  833.8 103.8 %shard_map.135 = (bf16[10,1536,512]{2,1,0:T(8,128)(2,1)}, bf16[10,1536,512]{2,1,0:T(8,128)(2,1)}, bf16[20,1536,512]{2,1,0:T(8,128)(2,1)}, bf16[20,1536,512]{2,1,0:T(8,128)(2,1)}) custom-call(s32[80]{0:T(128)} %copy-done.22, s32[80]{0:T(128)} %copy-done.33, s32[80]{0:T(128)} %get-tuple-element.98.tile_kind, s32[80]{0:T(128)} %get-tuple-element.125.tile_first, ...), custom_call_target="tpu_custom_call" | custom-call | flops 89999998976 | bytes 200000000 | tf_op jit(solution)/shard_map/pallas_call | solution.py:372
  937.6 70.1 %shard_map.136 = (bf16[10,512,1536]{2,1,0:T(8,128)(2,1)}, bf16[20,512,1536]{2,1,0:T(8,128)(2,1)}) custom-call(s32[80]{0:T(128)} %copy-done.22, s32[80]{0:T(128)} %copy-done.33, s32[80]{0:T(128)} %get-tuple-element.98.tile_kind, s32[80]{0:T(128)} %get-tuple-element.125.tile_first, s32[80]{0:T(128)} %get-tuple-element.124.tile_last, s32[1]{0:T(128)} %bitcast.36.base, ...), custom_call_target="tpu_custom_call" | custom-call | flops 44999999488 | bytes 100000000 | tf_op jit(solution)/shard_map/pallas_call | solution.py:372
  1008.3 26.6 %collective-permute-start.5 = (f32[1024,1536]{1,0:T(8,128)}, f32[1024,1536]{1,0:T(8,128)}, u32[]{:S(2)}, u32[]{:S(2)}) collective-permute-start(f32[1024,1536]{1,0:T(8,128)} %slice_add_fusion), channel_id=1, source_target_pairs={{0,4},{4,0},{1,5},{5,1},{2,6},{6,2},{3,7},{7,3}} | collective-permute-start | bytes 18874376 | tf_op jit(solution)/shard_map/ppermute | solution.py:494
  1035.6 3.6 fusion.45
  1039.2 135.2 %collective-permute-done.5 = f32[1024,1536]{1,0:T(8,128)} collective-permute-done((f32[1024,1536]{1,0:T(8,128)}, f32[1024,1536]{1,0:T(8,128)}, u32[]{:S(2)}, u32[]{:S(2)}) %collective-permute-start.5) | collective-permute-done | bytes 6291488 | tf_op jit(solution)/shard_map/ppermute | solution.py:494
  1174.4 9.3 fusion.9
  1183.8 124.8 %collective-permute-done.2 = f32[1024,1536]{1,0:T(8,128)} collective-permute-done((f32[1024,1536]{1,0:T(8,128)}, f32[1024,1536]{1,0:T(8,128)}, u32[]{:S(2)}, u32[]{:S(2)}) %collective-permute-start.2) | collective-permute-done | bytes 6291488 | tf_op jit(solution)/shard_map/ppermute | solution.py:494
  1308.6 10.2 fusion.8
  1318.8 14.1 %merge.5 = bf16[20,512,1536]{2,1,0:T(8,128)(2,1)} custom-call(s32[1]{0:T(128)} %bitcast.35.base, bf16[20,512,1536]{2,1,0:T(8,128)(2,1)} %get-tuple-element.73.whole_in, bf16[10,512,1536]{2,1,0:T(8,128)(2,1)} %collective-permute-done.8.other), custom_call_target="tpu_custom_call", output_to_operand_aliasing={{}: (1, {})} | custom-call | flops 8000000000 | bytes 30000000 | tf_op jit(solution)/shard_map/merge/pallas_call | solution.py:394
  1332.9 14.1 %merge.4 = bf16[20,1536,512]{2,1,0:T(8,128)(2,1)} custom-call(s32[1]{0:T(128)} %bitcast.35.base, bf16[20,1536,512]{2,1,0:T(8,128)(2,1)} %get-tuple-element.70.whole_in, bf16[10,1536,512]{2,1,0:T(8,128)(2,1)} %collective-permute-done.7.other), custom_call_target="tpu_custom_call", output_to_operand_aliasing={{}: (1, {})} | custom-call | flops 8000000000 | bytes 30000000 | tf_op jit(solution)/shard_map/merge/pallas_call | solution.py:394
  1347.0 14.1 %merge.3 = bf16[20,1536,512]{2,1,0:T(8,128)(2,1)} custom-call(s32[1]{0:T(128)} %bitcast.35.base, bf16[20,1536,512]{2,1,0:T(8,128)(2,1)} %get-tuple-element.66.whole_in, bf16[10,1536,512]{2,1,0:T(8,128)(2,1)} %collective-permute-done.6.other), custom_call_target="tpu_custom_call", output_to_operand_aliasing={{}: (1, {})} | custom-call | flops 8000000000 | bytes 30000000 | tf_op jit(solution)/shard_map/merge/pallas_call | solution.py:394
  (174 shorter events, 34.1 us)
Async XLA Ops:
  7.2 135.1 %all-gather.5.cloned.1.call-start = ((), (), s32[]{:S(2)}) async-start(), calls=%async_computation | async-start | bytes 28311552 | tf_op jit(solution)/shard_map/all_gather | solution.py:537
  16.1 336.7 %all-gather.7.cloned.1.call-start = ((), (), s32[]{:S(2)}) async-start(), calls=%async_computation.1 | async-start | bytes 28311552 | tf_op jit(solution)/shard_map/all_gather | solution.py:539
  16.9 1344.3 %all-reduce.3.cloned.1.call-start = ((), (), s32[]{:S(2)}) async-start(), calls=%async_computation.2 | async-start | bytes 491520 | tf_op jit(solution)/shard_map/psum | solution.py:583
  58.3 152.9 %copy-start.25 = (s32[10]{0:T(128)}, s32[10]{0:T(128)S(1)}, u32[]{:S(2)}) copy-start(s32[10]{0:T(128)S(1)} %get-tuple-element.137) | copy-start | bytes 124
  61.3 81.0 %copy-start.7 = (f32[8,32,256]{2,1,0:T(8,128)}, f32[8,32,256]{2,1,0:T(8,128)S(1)}, u32[]{:S(2)}) copy-start(f32[8,32,256]{2,1,0:T(8,128)S(1)} %pad_maximum_fusion) | copy-start | bytes 786436
  63.8 78.4 %copy-start.15 = (s32[320]{0:T(512)}, s32[320]{0:T(512)S(1)}, u32[]{:S(2)}) copy-start(s32[320]{0:T(512)S(1)} %get-tuple-element.104.seg_len) | copy-start | bytes 3844
  64.4 146.8 %copy-start.33 = (s32[80]{0:T(128)}, s32[80]{0:T(128)S(1)}, u32[]{:S(2)}) copy-start(s32[80]{0:T(128)S(1)} %iota_minimum_fusion.2.tile_at) | copy-start | bytes 964
  65.2 146.1 %copy-start.22 = (s32[80]{0:T(128)}, s32[80]{0:T(128)S(1)}, u32[]{:S(2)}) copy-start(s32[80]{0:T(128)S(1)} %get-tuple-element.145.tile_exp) | copy-start | bytes 964
  65.8 145.5 %copy-start.23 = (s32[80]{0:T(128)}, s32[80]{0:T(128)S(1)}, u32[]{:S(2)}) copy-start(s32[80]{0:T(128)S(1)} %get-tuple-element.86) | copy-start | bytes 964
  352.8 119.4 %copy-start.35 = (s32[10,1]{0,1:T(1,128)S(1)}, s32[10,1]{0,1:T(1,128)}, u32[]{:S(2)}) copy-start(s32[10,1]{0,1:T(1,128)} %copy-done.34) | copy-start | bytes 124
  352.8 120.1 %copy-start.19 = (s32[10]{0:T(128)S(1)}, s32[10]{0:T(128)}, u32[]{:S(2)}) copy-start(s32[10]{0:T(128)} %copy-done.18) | copy-start | bytes 124
  352.8 120.0 %copy-start.26 = (s32[10]{0:T(128)S(1)}, s32[10]{0:T(128)}, u32[]{:S(2)}) copy-start(s32[10]{0:T(128)} %copy-done.25) | copy-start | bytes 124
  352.8 120.0 %copy-start.27 = (s32[10]{0:T(128)S(1)}, s32[10]{0:T(128)}, u32[]{:S(2)}) copy-start(s32[10]{0:T(128)} %get-tuple-element.95) | copy-start | bytes 124
  457.9 94.4 %collective-permute-start = (f32[2048,1536]{1,0:T(8,128)}, f32[2048,1536]{1,0:T(8,128)}, u32[]{:S(2)}, u32[]{:S(2)}) collective-permute-start(f32[2048,1536]{1,0:T(8,128)} %get-tuple-element.44), channel_id=1, source_target_pairs={{0,1},{1,0},{2,3},{3,2},{4,5},{5,4},{6,7},{7,6}} | collective-permute-start | bytes 37748744 | tf_op jit(solution)/shard_map/ppermute | solution.py:491
  475.1 75.1 %copy-start.10 = (f32[16,256,8]{2,1,0:T(8,128)S(1)}, f32[16,256,8]{2,1,0:T(8,128)}, u32[]{:S(2)}) copy-start(f32[16,256,8]{2,1,0:T(8,128)} %get-tuple-element.47) | copy-start | bytes 393220
  475.1 74.8 %collective-permute-start.1 = (f32[8,256,8]{1,2,0:T(8,128)S(1)}, f32[8,256,8]{1,2,0:T(8,128)S(1)}, u32[]{:S(2)}, u32[]{:S(2)}) collective-permute-start(f32[8,256,8]{1,2,0:T(8,128)S(1)} %copy.60), channel_id=1, source_target_pairs={{0,1},{1,0},{2,3},{3,2},{4,5},{5,4},{6,7},{7,6}} | collective-permute-start | bytes 196616 | tf_op jit(solution)/shard_map/ppermute | solution.py:491
  657.0 66.7 %copy-start.28 = (s32[80]{0:T(128)S(1)}, s32[80]{0:T(128)}, u32[]{:S(2)}) copy-start(s32[80]{0:T(128)} %get-tuple-element.81) | copy-start | bytes 964
  657.0 66.7 %copy-start.29 = (s32[80]{0:T(128)S(1)}, s32[80]{0:T(128)}, u32[]{:S(2)}) copy-start(s32[80]{0:T(128)} %get-tuple-element.82) | copy-start | bytes 964
  657.0 66.7 %copy-start.30 = (s32[80]{0:T(128)S(1)}, s32[80]{0:T(128)}, u32[]{:S(2)}) copy-start(s32[80]{0:T(128)} %get-tuple-element.84) | copy-start | bytes 964
  657.0 66.7 %copy-start.31 = (s32[80]{0:T(128)S(1)}, s32[80]{0:T(128)}, u32[]{:S(2)}) copy-start(s32[80]{0:T(128)} %get-tuple-element.85) | copy-start | bytes 964
  709.7 115.5 %collective-permute-start.3 = (f32[2048,1536]{1,0:T(8,128)}, f32[2048,1536]{1,0:T(8,128)}, u32[]{:S(2)}, u32[]{:S(2)}) collective-permute-start(f32[2048,1536]{1,0:T(8,128)} %get-tuple-element.56), channel_id=1, source_target_pairs={{0,1},{1,0},{2,3},{3,2},{4,5},{5,4},{6,7},{7,6}} | collective-permute-start | bytes 37748744 | tf_op jit(solution)/shard_map/ppermute | solution.py:491
  724.3 96.1 %collective-permute-start.4 = (f32[4,256,8]{2,1,0:T(8,128)}, f32[4,256,8]{2,1,0:T(8,128)S(1)}, u32[]{:S(2)}, u32[]{:S(2)}) collective-permute-start(f32[4,256,8]{2,1,0:T(8,128)} %slice.118), channel_id=1, source_target_pairs={{0,4},{4,0},{1,5},{5,1},{2,6},{6,2},{3,7},{7,3}} | collective-permute-start | bytes 98312 | tf_op jit(solution)/shard_map/ppermute | solution.py:494
  1007.8 166.6 %copy-start.3 = (bf16[1024,1536]{1,0:T(8,128)(2,1)S(1)}, bf16[1024,1536]{1,0:T(8,128)(2,1)}, u32[]{:S(2)}) copy-start(bf16[1024,1536]{1,0:T(8,128)(2,1)} %param.8) | copy-start | bytes 9437188
  1007.8 166.6 %copy-start.14 = (f32[1536]{0:T(1024)S(1)}, f32[1536]{0:T(1024)}, u32[]{:S(2)}) copy-start(f32[1536]{0:T(1024)} %copy-done.13) | copy-start | bytes 18436
  1007.8 311.0 %collective-permute-start.8 = (bf16[10,512,1536]{2,1,0:T(8,128)(2,1)}, bf16[10,512,1536]{2,1,0:T(8,128)(2,1)}, u32[]{:S(2)}, u32[]{:S(2)}) collective-permute-start(bf16[10,512,1536]{2,1,0:T(8,128)(2,1)} %get-tuple-element.74), channel_id=1, source_target_pairs={{0,1},{1,0},{2,3},{3,2},{4,5},{5,4},{6,7},{7,6}} | collective-permute-start | bytes 47185928 | tf_op jit(solution)/shard_map/ppermute | solution.py:491
  1007.8 325.1 %collective-permute-start.7 = (bf16[10,1536,512]{2,1,0:T(8,128)(2,1)}, bf16[10,1536,512]{2,1,0:T(8,128)(2,1)}, u32[]{:S(2)}, u32[]{:S(2)}) collective-permute-start(bf16[10,1536,512]{2,1,0:T(8,128)(2,1)} %get-tuple-element.71), channel_id=1, source_target_pairs={{0,1},{1,0},{2,3},{3,2},{4,5},{5,4},{6,7},{7,6}} | collective-permute-start | bytes 47185928 | tf_op jit(solution)/shard_map/ppermute | solution.py:491
  1008.3 338.7 %collective-permute-start.6 = (bf16[10,1536,512]{2,1,0:T(8,128)(2,1)}, bf16[10,1536,512]{2,1,0:T(8,128)(2,1)}, u32[]{:S(2)}, u32[]{:S(2)}) collective-permute-start(bf16[10,1536,512]{2,1,0:T(8,128)(2,1)} %get-tuple-element.69), channel_id=1, source_target_pairs={{0,1},{1,0},{2,3},{3,2},{4,5},{5,4},{6,7},{7,6}} | collective-permute-start | bytes 47185928 | tf_op jit(solution)/shard_map/ppermute | solution.py:491
  1008.3 166.1 %collective-permute-start.5 = (f32[1024,1536]{1,0:T(8,128)}, f32[1024,1536]{1,0:T(8,128)}, u32[]{:S(2)}, u32[]{:S(2)}) collective-permute-start(f32[1024,1536]{1,0:T(8,128)} %slice_add_fusion), channel_id=1, source_target_pairs={{0,4},{4,0},{1,5},{5,1},{2,6},{6,2},{3,7},{7,3}} | collective-permute-start | bytes 18874376 | tf_op jit(solution)/shard_map/ppermute | solution.py:494
  1035.0 273.6 %collective-permute-start.2 = (f32[1024,1536]{1,0:T(8,128)}, f32[1024,1536]{1,0:T(8,128)}, u32[]{:S(2)}, u32[]{:S(2)}) collective-permute-start(f32[1024,1536]{1,0:T(8,128)} %slice_add_fusion.2), channel_id=1, source_target_pairs={{0,4},{4,0},{1,5},{5,1},{2,6},{6,2},{3,7},{7,3}} | collective-permute-start | bytes 18874376 | tf_op jit(solution)/shard_map/ppermute | solution.py:494
  1174.4 134.2 %copy-start.4 = (bf16[1024,1536]{1,0:T(8,128)(2,1)S(1)}, bf16[1024,1536]{1,0:T(8,128)(2,1)}, u32[]{:S(2)}) copy-start(bf16[1024,1536]{1,0:T(8,128)(2,1)} %param.9) | copy-start | bytes 9437188
  1174.4 134.2 %copy-start.17 = (f32[1024]{0:T(1024)S(1)}, f32[1024]{0:T(1024)}, u32[]{:S(2)}) copy-start(f32[1024]{0:T(1024)} %copy-done.16) | copy-start | bytes 12292
  1174.4 134.2 %copy-start.21 = (f32[1024]{0:T(1024)S(1)}, f32[1024]{0:T(1024)}, u32[]{:S(2)}) copy-start(f32[1024]{0:T(1024)} %get-tuple-element.119) | copy-start | bytes 12292
  (16 other events, 403.7 us)
Sparse Core Ops, SparseCore 0:
  16.2 126.0 all-gather.4
  144.1 119.6 all-gather.6
  1039.4 54.0 all-reduce.2

commit v3 on v2

v3 whole, which is shorter than its diff:
```python
import functools

import jax
import jax.numpy as jnp
from jax import lax
from jax.experimental import pallas as pl
from jax.experimental.pallas import tpu as pltpu
from jax.sharding import PartitionSpec as P


AUX_COEF = 0.001
NORM_EPS = 1e-6
MAX_HITS = 416
BLOCK = 256
GROUP = 16
TILE = 512
HALF = TILE // 2
CHUNK = 256
MIX = 256
NT_DIMS = (((1,), (1,)), ((), ()))
TN_DIMS = (((0,), (0,)), ((), ()))
VMEM_LIMIT = 60 * 1024 * 1024


def norm_forward(tokens32, gain32):
    inv_rms = lax.rsqrt(jnp.mean(tokens32 * tokens32, axis=1, keepdims=True) + NORM_EPS)
    return inv_rms, (tokens32 * inv_rms * gain32).astype(jnp.bfloat16)


def norm_backward(tokens32, inv_rms, gain32, d_normed):
    d_scaled = d_normed * gain32
    return inv_rms * (d_scaled - tokens32 * (inv_rms * inv_rms) * jnp.mean(d_scaled * tokens32, axis=1, keepdims=True))


def dot32(left, right, dims=(((1,), (0,)), ((), ()))):
    return lax.dot_general(left, right, dims, preferred_element_type=jnp.float32)


def dispatch_kernel(scaled, begun, n_exp, src_blk, ordinal, n_chunk, seg_len, seg_src, seg_dst, tail_at, tail_len, src, pos, gates, *rest):
    out, stack, blank, sems, tail_sem = rest[1:] if begun else rest
    step = pl.program_id(0)
    last = pl.num_programs(0) - 1
    slot = lax.rem(step, 2)

    def segment_copy(blk, buf, exp, grp):
        at = blk * n_exp + exp
        from_row = pl.multiple_of((seg_src[at] + grp) * GROUP, GROUP)
        to_row = pl.multiple_of((seg_dst[at] + grp) * GROUP, GROUP)
        return pltpu.make_async_copy(stack.at[buf, pl.ds(from_row, GROUP), :], out.at[pl.ds(to_row, GROUP), :], sems.at[buf])

    def each_segment(blk, buf, act):
        for exp in range(n_exp):
            @pl.loop(0, seg_len[blk * n_exp + exp])
            def _(grp):
                act(segment_copy(blk, buf, exp, grp))

    def each_tail(act):
        for exp in range(n_exp):
            @pl.loop(0, tail_len[exp])
            def _(grp):
                to_row = pl.multiple_of((tail_at[exp] + grp) * GROUP, GROUP)
                act(pltpu.make_async_copy(blank, out.at[pl.ds(to_row, GROUP), :], tail_sem))

    if not begun:
        @pl.when(step == 0)
        def _():
            blank[...] = jnp.zeros_like(blank)
            each_tail(lambda copy: copy.start())

    @pl.when(step >= 2)
    def _():
        each_segment(ordinal[step - 2], slot, lambda copy: copy.wait())

    @pl.loop(0, n_chunk[ordinal[step]])
    def _(chunk):
        row = lax.broadcasted_iota(jnp.int32, (CHUNK, BLOCK), 0) + chunk * CHUNK
        hit = pos[0, 0:1, :] == row
        if scaled:
            weight = jnp.where(hit, gates[0, 0:1, :], 0.0)
        for k in range(1, pos.shape[1]):
            here = pos[0, k:k + 1, :] == row
            hit = jnp.logical_or(hit, here)
            if scaled:
                weight = jnp.where(here, gates[0, k:k + 1, :], weight)
        picked = dot32(jnp.where(hit, 1.0, 0.0).astype(jnp.bfloat16), src[...])
        if scaled:
            picked = picked * jnp.sum(weight, axis=1, keepdims=True)
        stack[slot, pl.ds(pl.multiple_of(chunk * CHUNK, CHUNK), CHUNK), :] = picked.astype(jnp.bfloat16)

    each_segment(ordinal[step], slot, lambda copy: copy.start())

    @pl.when(step == last)
    def _():
        each_segment(ordinal[step - 1], 1 - slot, lambda copy: copy.wait())
        each_segment(ordinal[step], slot, lambda copy: copy.wait())
        if not begun:
            each_tail(lambda copy: copy.wait())


def dispatch(src, pos, gates, plan, part, out, rows, scaled):
    top_k = pos.shape[1]
    src_blk, ordinal = plan["parts"][part]
    begun = out is not None
    width = src.shape[1]
    n_exp = plan["tail_at"].shape[0]
    stack_rows = -(-(BLOCK * top_k + n_exp * (GROUP - 1)) // CHUNK) * CHUNK
    return pl.pallas_call(
        functools.partial(dispatch_kernel, scaled, begun, n_exp),
        out_shape=jax.ShapeDtypeStruct((rows, width), jnp.bfloat16),
        grid_spec=pltpu.PrefetchScalarGridSpec(
            num_scalar_prefetch=8,
            grid=(ordinal.shape[0],),
            in_specs=[
                pl.BlockSpec((BLOCK, width), lambda i, blk, *_: (blk[i], 0)),
                pl.BlockSpec((1, top_k, BLOCK), lambda i, blk, ordinal, *_: (ordinal[i], 0, 0)),
                pl.BlockSpec((1, top_k, BLOCK), lambda i, blk, ordinal, *_: (ordinal[i], 0, 0)),
            ]
            + [pl.BlockSpec(memory_space=pl.ANY)] * begun,
            out_specs=pl.BlockSpec(memory_space=pl.ANY),
            scratch_shapes=[
                pltpu.VMEM((2, stack_rows, width), jnp.bfloat16),
                pltpu.VMEM((GROUP, width), jnp.bfloat16),
                pltpu.SemaphoreType.DMA((2,)),
                pltpu.SemaphoreType.DMA,
            ],
        ),
        compiler_params=pltpu.CompilerParams(dimension_semantics=("arbitrary",), vmem_limit_bytes=VMEM_LIMIT),
        input_output_aliases={11: 0} if begun else {},
        cost_estimate=pl.CostEstimate(flops=20_000_000_000, bytes_accessed=80_000_000, transcendentals=0),
        name="dispatch_scaled" if scaled else "dispatch",
    )(src_blk, ordinal, plan["n_chunk"], plan["seg_len"], plan["seg_src"], plan["seg_dst"], plan["tail_at"], plan["tail_len"], src, pos, gates, *([out] * begun))


def combine_kernel(weighted, first, counts, dev_blocks, n_exp, at0, at1, n_mix, seg_len, seg_src, seg_dst, rows, pos, gates, *rest):
    if weighted:
        d_out0, d_out1, *outs, d_gates, stack, total, sems = rest
    else:
        *outs, stack, total, sems = rest
    step = pl.program_id(0)
    blocks = pl.num_programs(0)
    slot = lax.rem(step, 2)

    def each_segment(blk, buf, act):
        for exp in range(n_exp):
            @pl.loop(0, seg_len[blk * n_exp + exp])
            def _(grp):
                at = blk * n_exp + exp
                to_row = pl.multiple_of((seg_src[at] + grp) * GROUP, GROUP)
                from_row = pl.multiple_of((seg_dst[at] + grp) * GROUP, GROUP)
                act(pltpu.make_async_copy(rows.at[pl.ds(from_row, GROUP), :], stack.at[buf, pl.ds(to_row, GROUP), :], sems.at[buf]))

    @pl.when(step == 0)
    def _():
        @pl.loop(0, stack.shape[1] // MIX)
        def _(part):
            stack[:, pl.ds(pl.multiple_of(part * MIX, MIX), MIX), :] = jnp.zeros((2, MIX, stack.shape[2]), stack.dtype)

        each_segment(first, 0, lambda copy: copy.start())

    @pl.when(step < blocks - 1)
    def _():
        each_segment(first + step + 1, 1 - slot, lambda copy: copy.start())

    each_segment(first + step, slot, lambda copy: copy.wait())
    total[...] = jnp.zeros_like(total)
    if weighted:
        d_gates[...] = jnp.zeros_like(d_gates)

    @pl.loop(0, n_mix[first + step])
    def _(part):
        col = lax.broadcasted_iota(jnp.int32, (BLOCK, MIX), 1) + part * MIX
        part_rows = stack[slot, pl.ds(pl.multiple_of(part * MIX, MIX), MIX), :]
        top_k = pos.shape[2]
        if weighted:
            late = lax.rem(step, dev_blocks) >= dev_blocks // 2
            cross = dot32(jnp.where(late, d_out1[...], d_out0[...]), part_rows, NT_DIMS)
            weight = jnp.zeros((BLOCK, MIX), jnp.float32)
            d_cols = []
            for k in range(top_k):
                here = pos[0, :, k:k + 1] == col
                weight = jnp.where(here, gates[0, :, k:k + 1], weight)
                d_cols.append(jnp.sum(jnp.where(here, cross, 0.0), axis=1, keepdims=True))
            d_gates[0] += jnp.concatenate(d_cols, axis=1)
            high = weight.astype(jnp.bfloat16)
            left = weight - high.astype(jnp.float32)
            mid = left.astype(jnp.bfloat16)
            low = (left - mid.astype(jnp.float32)).astype(jnp.bfloat16)
            mixed = dot32(jnp.concatenate([high, mid, low], axis=0), part_rows)
            total[...] += mixed[:BLOCK] + mixed[BLOCK:2 * BLOCK] + mixed[2 * BLOCK:]
        else:
            hit = pos[0, :, 0:1] == col
            for k in range(1, top_k):
                hit = jnp.logical_or(hit, pos[0, :, k:k + 1] == col)
            total[...] += dot32(jnp.where(hit, 1.0, 0.0).astype(jnp.bfloat16), part_rows)

    begin = 0
    for out, count in zip(outs, counts):
        @pl.when((step >= begin) & (step < begin + count))
        def _():
            out[...] = total[...]

        begin += count


def combine(rows, pos_t, gates_t, d_outs, plan, first, counts, weighted):
    _, _, top_k = pos_t.shape
    width = rows.shape[1]
    n_exp = plan["tail_at"].shape[0]
    blocks = sum(counts)
    stack_rows = -(-(BLOCK * top_k + n_exp * (GROUP - 1)) // MIX) * MIX
    out_shape, out_specs, begin = [], [], 0
    for count in counts:
        out_shape.append(jax.ShapeDtypeStruct((count * BLOCK, width), jnp.float32))
        out_specs.append(pl.BlockSpec((BLOCK, width), lambda i, *_, begin=begin, count=count: (jnp.clip(i - begin, 0, count - 1), 0)))
        begin += count
    d_specs = []
    if weighted:
        out_shape.append(jax.ShapeDtypeStruct((blocks, BLOCK, top_k), jnp.float32))
        out_specs.append(pl.BlockSpec((1, BLOCK, top_k), lambda i, *_: (i, 0, 0)))
        d_specs = [
            pl.BlockSpec((BLOCK, width), lambda i, at0, at1, *_: (at0[first + i], 0)),
            pl.BlockSpec((BLOCK, width), lambda i, at0, at1, *_: (at1[first + i], 0)),
        ]
    return pl.pallas_call(
        functools.partial(combine_kernel, weighted, first, counts, plan["dev_blocks"], n_exp),
        out_shape=out_shape,
        grid_spec=pltpu.PrefetchScalarGridSpec(
            num_scalar_prefetch=6,
            grid=(blocks,),
            in_specs=[
                pl.BlockSpec(memory_space=pl.ANY),
                pl.BlockSpec((1, BLOCK, top_k), lambda i, *_: (first + i, 0, 0)),
                pl.BlockSpec((1, BLOCK, top_k), lambda i, *_: (first + i, 0, 0)),
            ]
            + d_specs,
            out_specs=out_specs,
            scratch_shapes=[
                pltpu.VMEM((2, stack_rows, width), jnp.bfloat16),
                pltpu.VMEM((BLOCK, width), jnp.float32),
                pltpu.SemaphoreType.DMA((2,)),
            ],
        ),
        compiler_params=pltpu.CompilerParams(dimension_semantics=("arbitrary",), vmem_limit_bytes=VMEM_LIMIT),
        cost_estimate=pl.CostEstimate(flops=5_000_000_000 * blocks, bytes_accessed=60_000_000, transcendentals=0),
        name="combine_weighted" if weighted else "combine",
    )(*plan["d_at"], plan["n_mix"], plan["seg_len"], plan["seg_src"], plan["seg_own"], rows, pos_t, gates_t, *(d_outs if weighted else ()))


def by_kind(kind, body):
    for code, rows in ((1, HALF), (2, TILE)):
        @pl.when(kind == code)
        def _():
            body(pl.ds(0, rows))


def activations(x, w_gate, w_up):
    a = dot32(x, w_gate)
    b = dot32(x, w_up)
    sig = jax.nn.sigmoid(a)
    return a, b, sig, (a * sig * b).astype(jnp.bfloat16)


def cotangents(d_rows, w_down, a, b, sig):
    d_hidden = dot32(d_rows, w_down, NT_DIMS)
    d_a = (d_hidden * b * sig * (1.0 + a * (1.0 - sig))).astype(jnp.bfloat16)
    return d_a, (d_hidden * (a * sig)).astype(jnp.bfloat16)


def own_kernel(tile_exp, tile_at, own_at, tile_kind, x, d_rows, w_gate, w_up, w_down, hidden, d_gate, d_up, result, d_in):
    @pl.loop(0, tile_kind[pl.program_id(0)])
    def _(half):
        part = pl.ds(pl.multiple_of(half * HALF, HALF), HALF)
        a, b, sig, u = activations(x[part], w_gate[0], w_up[0])
        hidden[part] = u
        result[part] = dot32(u, w_down[0]).astype(jnp.bfloat16)
        d_a, d_b = cotangents(d_rows[part], w_down[0], a, b, sig)
        d_gate[part] = d_a
        d_up[part] = d_b
        d_in[part] = (dot32(d_a, w_gate[0], NT_DIMS) + dot32(d_b, w_up[0], NT_DIMS)).astype(jnp.bfloat16)


def rest_kernel(begun, tile_exp, tile_at, own_at, own_kind, other_kind, tile_first, tile_last, base, x, d_rows, w_gate, w_up, w_down, hidden, d_gate, d_up, *refs):
    g_gate, g_up, g_down, all_gate, all_up, all_down, s_gate, s_up, s_down, t_hidden, t_gate, t_up = refs[3:] if begun else refs
    step = pl.program_id(0)

    @pl.when(tile_first[step] > 0)
    def _():
        for total in (s_gate, s_up, s_down):
            total[...] = jnp.zeros_like(total)

    def add(u, d_a, d_b, part):
        s_gate[...] += dot32(x[part], d_a[part], TN_DIMS)
        s_up[...] += dot32(x[part], d_b[part], TN_DIMS)
        s_down[...] += dot32(u[part], d_rows[part], TN_DIMS)

    @pl.loop(0, other_kind[step])
    def _(half):
        part = pl.ds(pl.multiple_of(half * HALF, HALF), HALF)
        a, b, sig, u = activations(x[part], w_gate[0], w_up[0])
        t_hidden[part] = u
        t_gate[part], t_up[part] = cotangents(d_rows[part], w_down[0], a, b, sig)

    by_kind(own_kind[step], functools.partial(add, hidden, d_gate, d_up))
    by_kind(other_kind[step], functools.partial(add, t_hidden, t_gate, t_up))

    @pl.when(tile_last[step] > 0)
    def _():
        for out, whole, total in ((g_gate, all_gate, s_gate), (g_up, all_up, s_up), (g_down, all_down, s_down)):
            rounded = total[...].astype(jnp.bfloat16)
            out[0] = rounded
            whole[0] = rounded


def kernel_params():
    return pltpu.CompilerParams(dimension_semantics=("arbitrary",), vmem_limit_bytes=VMEM_LIMIT)


def own_tiles(x, d_rows, w_gate, w_up, w_down, plan):
    width = x.shape[1]
    mid = w_gate.shape[2]
    wide = pl.BlockSpec((TILE, width), lambda t, exp, at, *_: (at[t], 0))
    thin = pl.BlockSpec((TILE, mid), lambda t, exp, at, own, *_: (own[t], 0))
    wide_own = pl.BlockSpec((TILE, width), lambda t, exp, at, own, *_: (own[t], 0))
    w_in = pl.BlockSpec((1, width, mid), lambda t, exp, *_: (exp[t], 0, 0))
    w_out = pl.BlockSpec((1, mid, width), lambda t, exp, *_: (exp[t], 0, 0))
    seq = plan["own_seq"]
    own_rows = seq[0].shape[0] * TILE
    thin_shape = jax.ShapeDtypeStruct((own_rows, mid), jnp.bfloat16)
    wide_shape = jax.ShapeDtypeStruct((own_rows, width), jnp.bfloat16)
    return pl.pallas_call(
        own_kernel,
        out_shape=[thin_shape] * 3 + [wide_shape] * 2,
        grid_spec=pltpu.PrefetchScalarGridSpec(num_scalar_prefetch=4, grid=(seq[0].shape[0],), in_specs=[wide, wide, w_in, w_in, w_out], out_specs=[thin] * 3 + [wide_own] * 2),
        compiler_params=kernel_params(),
        cost_estimate=pl.CostEstimate(flops=120_000_000_000, bytes_accessed=250_000_000, transcendentals=0),
        name="own_tiles",
    )(*seq, x, d_rows, w_gate, w_up, w_down)


def rest_tiles(x, d_rows, w_gate, w_up, w_down, hidden, d_gate, d_up, plan, half, begun):
    width, mid = w_gate.shape[1:]
    n_half = plan["tail_at"].shape[0] // 2
    seq = plan["rest_seq"][half]
    shapes = [(width, mid), (width, mid), (mid, width)]
    wide = pl.BlockSpec((TILE, width), lambda t, exp, at, *_: (at[t], 0))
    kept = pl.BlockSpec((TILE, mid), lambda t, exp, at, own, *_: (own[t], 0))
    w_in = pl.BlockSpec((1, width, mid), lambda t, exp, at, own, k1, k2, first, last, base: (base[0] + exp[t], 0, 0))
    w_out = pl.BlockSpec((1, mid, width), lambda t, exp, at, own, k1, k2, first, last, base: (base[0] + exp[t], 0, 0))
    alone = [pl.BlockSpec((1, *shape), lambda t, exp, *_: (exp[t] - half * n_half, 0, 0)) for shape in shapes]
    return pl.pallas_call(
        functools.partial(rest_kernel, begun is not None),
        out_shape=[jax.ShapeDtypeStruct((n_half, *shape), jnp.bfloat16) for shape in shapes]
        + [jax.ShapeDtypeStruct((4 * n_half, *shape), jnp.bfloat16) for shape in shapes],
        grid_spec=pltpu.PrefetchScalarGridSpec(
            num_scalar_prefetch=8,
            grid=(seq[0].shape[0],),
            in_specs=[wide, wide, w_in, w_in, w_out, kept, kept, kept] + [pl.BlockSpec(memory_space=pl.ANY)] * (3 if begun else 0),
            out_specs=alone + [w_in, w_in, w_out],
            scratch_shapes=[pltpu.VMEM(shape, jnp.float32) for shape in shapes] + [pltpu.VMEM((TILE, mid), jnp.bfloat16)] * 3,
        ),
        input_output_aliases={16: 3, 17: 4, 18: 5} if begun else {},
        compiler_params=kernel_params(),
        cost_estimate=pl.CostEstimate(flops=80_000_000_000, bytes_accessed=150_000_000, transcendentals=0),
        name="rest_tiles",
    )(*seq, plan["base"], x, d_rows, w_gate, w_up, w_down, hidden, d_gate, d_up, *(begun or ()))


def merge_kernel(base, whole_in, other, whole):
    whole[...] = other[...]


def merge(whole, other, other_base):
    count, *shape = other.shape
    return pl.pallas_call(
        merge_kernel,
        out_shape=jax.ShapeDtypeStruct(whole.shape, whole.dtype),
        grid_spec=pltpu.PrefetchScalarGridSpec(
            num_scalar_prefetch=1,
            grid=(count,),
            in_specs=[pl.BlockSpec(memory_space=pl.ANY), pl.BlockSpec((1, *shape), lambda i, base: (i, 0, 0))],
            out_specs=pl.BlockSpec((1, *shape), lambda i, base: (base[0] + i, 0, 0)),
        ),
        input_output_aliases={1: 0},
        compiler_params=pltpu.CompilerParams(dimension_semantics=("arbitrary",), vmem_limit_bytes=16 * 1024 * 1024),
        cost_estimate=pl.CostEstimate(flops=8_000_000_000, bytes_accessed=30_000_000, transcendentals=0),
        name="merge",
    )(other_base, whole, other)


def exclusive(values, axis=0):
    return jnp.cumsum(values, axis=axis) - values


def make_plan(local_ids, dev_order, own_blocks, n_exp, max_tiles, max_own, weight_base):
    order = jnp.arange(local_ids.shape[0])
    onehot = (local_ids[:, :, None, :] == jnp.arange(n_exp)[None, None, :, None]).astype(jnp.float32)
    hits = jnp.sum(onehot, axis=1)
    before = jnp.triu(jnp.ones((BLOCK, BLOCK), jnp.bfloat16), 1)
    rank = jnp.einsum("oet,ts->oes", hits.astype(jnp.bfloat16), before, preferred_element_type=jnp.float32)
    seg_len = (jnp.sum(hits, axis=2).astype(jnp.int32) + GROUP - 1) // GROUP
    seg_src = exclusive(seg_len, 1)
    per_tile, per_half = TILE // GROUP, HALF // GROUP
    groups = jnp.sum(seg_len, axis=0)
    tiles = (groups + per_tile - 1) // per_tile
    tile_base = exclusive(tiles)
    seg_dst = tile_base[None, :] * per_tile + exclusive(seg_len, 0)
    place = rank + (seg_src * GROUP).astype(jnp.float32)[:, :, None]
    pos = jnp.sum(onehot * (place[:, None] + 1.0), axis=2).astype(jnp.int32) - 1
    own_tiles = (jnp.sum(seg_len[:own_blocks], axis=0) + per_tile - 1) // per_tile
    exp_ids = jnp.arange(n_exp)

    def sequence(counts, length):
        ids = jnp.arange(length)
        at = jnp.minimum(ids, jnp.maximum(jnp.sum(counts) - 1, 0))
        ends = jnp.cumsum(counts)
        exp = jnp.minimum(jnp.sum((at[:, None] >= ends[None, :]).astype(jnp.int32), axis=1), n_exp - 1)
        is_exp = (exp[:, None] == exp_ids[None, :]).astype(jnp.int32)
        pick = lambda table: jnp.sum(is_exp * table[None, :], axis=1)
        return exp, at - pick(ends - counts), ids > at, pick

    def kind_of(pick, nth, past):
        left = pick(groups) - nth * per_tile
        return jnp.where(past, 0, jnp.where(left <= per_half, 1, 2))

    o_exp, o_nth, o_past, o_pick = sequence(own_tiles, max_own)
    own_base = exclusive(own_tiles)

    def rest_seq(half):
        mine = exp_ids // (n_exp // 2) == half
        exp, nth, past, pick = sequence(jnp.where(mine, tiles, 0), max_tiles // 2)
        kind = kind_of(pick, nth, past)
        own_count = pick(own_tiles)
        is_own = nth < own_count
        seq = (
            exp,
            pick(tile_base) + nth,
            pick(own_base) + jnp.minimum(nth, own_count - 1),
            jnp.where(is_own, kind, 0),
            jnp.where(is_own, 0, kind),
            (nth == 0) & ~past,
            (nth == pick(tiles) - 1) & ~past,
        )
        return seq

    dev_blocks = order.shape[0] // dev_order.shape[0]
    part_blocks = dev_blocks // 2
    in_part = jnp.arange(part_blocks)

    def part_of(part):
        blk = dev_order[:, None] * part_blocks + in_part[None, :]
        ordinal = jnp.arange(dev_order.shape[0])[:, None] * dev_blocks + part * part_blocks + in_part[None, :]
        return blk.reshape(-1), ordinal.reshape(-1)

    d_at = dev_order[:, None] * part_blocks + jnp.arange(dev_blocks)[None, :] % part_blocks
    early = jnp.arange(dev_blocks)[None, :] < part_blocks
    d_at0 = jnp.where(early, d_at, d_at[:, part_blocks - 1:part_blocks])
    d_at1 = jnp.where(early, d_at[:, :1], d_at)
    stack_rows = jnp.sum(seg_len, axis=1) * GROUP
    plan = {
        "parts": (part_of(0), part_of(1)),
        "d_at": (d_at0.reshape(-1), d_at1.reshape(-1)),
        "n_chunk": (stack_rows + CHUNK - 1) // CHUNK,
        "n_mix": (stack_rows + MIX - 1) // MIX,
        "seg_len": seg_len.reshape(-1),
        "seg_src": seg_src.reshape(-1),
        "seg_dst": seg_dst.reshape(-1),
        "seg_own": (own_base[None, :] * per_tile + exclusive(seg_len, 0)).reshape(-1),
        "tail_at": tile_base * per_tile + groups,
        "tail_len": (groups + per_half - 1) // per_half * per_half - groups,
        "base": weight_base.reshape(1),
        "own_seq": (o_exp + weight_base, o_pick(tile_base) + o_nth, o_pick(own_base) + o_nth, kind_of(o_pick, o_nth, o_past)),
        "rest_seq": (rest_seq(0), rest_seq(1)),
    }
    return jax.tree.map(lambda value: value.astype(jnp.int32), plan), pos


def solution(mesh):
    ep_size = mesh.shape["ep"]
    dp_size = mesh.shape["dp"]
    devices = ep_size * dp_size
    cores = 2
    tok_spec = P(("dp", "ep"), None)
    exp_spec = P("ep", None, None)
    core_perm = [(i, i ^ 1) for i in range(dp_size)]
    ep_perm = [(i, i ^ 1) for i in range(ep_size)]

    def to_core(away):
        return lax.ppermute(away, "dp", core_perm)

    def to_ep(far):
        return lax.ppermute(far, "ep", ep_perm)

    def after(value, other):
        return lax.optimization_barrier((value, other))

    def device_step(tokens, d_out, expert_ids, norm_gain, router, w_gate, w_up, w_down):
        tok_rows, _ = tokens.shape
        top_k = expert_ids.shape[1]
        local_experts = w_gate.shape[0]
        experts = local_experts * ep_size
        total_tok = tok_rows * devices
        n_exp = local_experts // cores
        dev_blocks = tok_rows // BLOCK
        own_devs = devices // 2
        own_blocks = own_devs * dev_blocks
        seg_pad = devices * dev_blocks * (GROUP - 1)
        max_own = n_exp * -(-(own_devs * MAX_HITS + own_blocks * (GROUP - 1)) // TILE)
        max_tiles = n_exp * -(-(devices * MAX_HITS + seg_pad) // TILE)

        ep_at = lax.axis_index("ep")
        dp_at = lax.axis_index("dp")
        core_at = lax.rem(dp_at, cores)
        x_at = lax.div(dp_at, cores)

        def dev_of(x, core, ep):
            return (x * cores + core) * ep_size + ep

        dev_order = jnp.stack(
            [dev_of(x_at, 1 - core_at, 1 - ep_at), dev_of(x_at, 1 - core_at, ep_at), dev_of(x_at, core_at, 1 - ep_at), dev_of(x_at, core_at, ep_at)]
            + [dev_of(1 - x_at, core, ep) for core in range(cores) for ep in range(ep_size)]
        )
        tokens32 = tokens.astype(jnp.float32)
        gain32 = norm_gain.astype(jnp.float32)
        inv_rms, normed = norm_forward(tokens32, gain32)
        logits = jnp.dot(normed, router, preferred_element_type=jnp.float32)
        router_probs = jax.nn.softmax(logits, axis=1)
        expert_hits = expert_ids[:, :, None] == jnp.arange(experts)[None, None, :]
        gate_vals = jnp.sum(jnp.where(expert_hits, router_probs[:, None, :], 0.0), axis=2)

        prob_sums = jnp.pad(jnp.sum(router_probs, axis=0), (0, tok_rows - experts))
        packet = jnp.concatenate([expert_ids.astype(jnp.float32).T, gate_vals.T, prob_sums[None]], axis=0)
        packets = lax.all_gather(packet, ("dp", "ep"))
        half_rows = tok_rows // 2
        parts = [normed[:half_rows], normed[half_rows:], d_out[:half_rows], d_out[half_rows:]]
        gathered = [lax.all_gather(parts[0], ("dp", "ep"), tiled=True)]
        for part in parts[1:]:
            late, _ = lax.optimization_barrier((part, gathered[-1][:8]))
            gathered.append(lax.all_gather(late, ("dp", "ep"), tiled=True))
        all_normed, all_d_out = gathered[:2], gathered[2:]

        all_ids = packets[:, :top_k].astype(jnp.int32)
        counts = jnp.sum((all_ids[..., None] == jnp.arange(experts)).astype(jnp.float32), axis=(0, 1, 2))
        expert_frac = counts / (total_tok * top_k)
        aux_loss = AUX_COEF * experts * jnp.sum(expert_frac * jnp.sum(packets[:, 2 * top_k, :experts], axis=0)) / total_tok

        turned = jnp.take(packets, dev_order, axis=0)

        def by_block(rows):
            return rows.reshape(devices, top_k, dev_blocks, BLOCK).transpose(0, 2, 1, 3).reshape(devices * dev_blocks, top_k, BLOCK)

        first_expert = ep_at * local_experts + core_at * n_exp
        block_ids = by_block(turned[:, :top_k]).astype(jnp.int32) - first_expert
        block_ids = jnp.where((block_ids >= 0) & (block_ids < n_exp), block_ids, n_exp)
        block_gates = by_block(turned[:, top_k:2 * top_k])
        plan, pos = make_plan(block_ids, dev_order, own_blocks, n_exp, max_tiles, max_own, core_at * n_exp)
        plan["dev_blocks"] = dev_blocks
        pos_t = pos[:own_blocks].transpose(0, 2, 1)
        gates_t = block_gates[:own_blocks].transpose(0, 2, 1)

        rows = max_tiles * TILE
        x = dispatch(all_normed[0], pos, block_gates, plan, 0, None, rows, False)
        x = dispatch(all_normed[1], pos, block_gates, plan, 1, x, rows, False)
        d_rows = dispatch(all_d_out[0], pos, block_gates, plan, 0, None, rows, True)
        d_rows = dispatch(all_d_out[1], pos, block_gates, plan, 1, d_rows, rows, True)
        hidden, d_act_gate, d_act_up, result, d_expert_in = own_tiles(x, d_rows, w_gate, w_up, w_down, plan)
        half, quarter = own_blocks // 2, own_blocks // 4
        d_away, d_far, d_near = combine(d_expert_in, pos_t, gates_t, None, plan, 0, (half, quarter, quarter), False)
        result, d_away = after(result, d_away)
        d_met = to_core(d_away)
        away, d_gate_away = combine(result, pos_t, gates_t, all_d_out, plan, 0, (half,), True)
        result, (away, d_gate_away, d_far) = after(result, (away, d_gate_away, d_far + d_met[:tok_rows]))
        d_crossed = to_ep(d_far)
        met = to_core(away)
        d_gate_met = to_core(d_gate_away)
        far, near, d_gate_mine = combine(result, pos_t, gates_t, all_d_out, plan, half, (quarter, quarter), True)
        d_gate_mine = d_gate_mine + d_gate_met
        hidden, (far, d_gate_far) = after(hidden, (far + met[:tok_rows], d_gate_mine[:quarter]))
        crossed = to_ep(far)
        d_gate_crossed = to_ep(d_gate_far)
        grads, wholes = [None, None], None
        for part in range(2):
            *grads[part], all_gate, all_up, all_down = rest_tiles(x, d_rows, w_gate, w_up, w_down, hidden, d_act_gate, d_act_up, plan, part, wholes)
            wholes = (all_gate, all_up, all_down)
        d_gates = (d_gate_mine[quarter:] + d_gate_crossed).reshape(tok_rows, top_k)
        d_probs = jnp.sum(jnp.where(expert_hits, d_gates[:, :, None], 0.0), axis=1) + (AUX_COEF * experts / total_tok) * expert_frac[None, :]
        d_logits = (router_probs * (d_probs - jnp.sum(router_probs * d_probs, axis=1, keepdims=True))).astype(jnp.bfloat16)
        grad_router = lax.psum(lax.dot_general(normed, d_logits, TN_DIMS, preferred_element_type=jnp.float32), ("ep", "dp"))
        other_base = (1 - core_at).reshape(1).astype(jnp.int32) * n_exp
        wholes = list(wholes)
        for part in range(2):
            for i in range(3):
                wholes[i] = merge(wholes[i], to_core(grads[part][i]), other_base + part * (n_exp // 2))
        all_gate, all_up, all_down = wholes
        layer_out = (tokens32 + (near + met[tok_rows:] + crossed)).astype(jnp.bfloat16)
        d_normed = (d_near + d_met[tok_rows:] + d_crossed) + lax.dot_general(d_logits, router, NT_DIMS, preferred_element_type=jnp.float32)
        d_tokens = (d_out.astype(jnp.float32) + norm_backward(tokens32, inv_rms, gain32, d_normed)).astype(jnp.bfloat16)
        return layer_out, aux_loss.reshape(1), d_tokens, grad_router, all_gate, all_up, all_down

    return jax.shard_map(device_step, mesh=mesh, in_specs=(tok_spec, tok_spec, tok_spec, P(None), P(None, None), exp_spec, exp_spec, exp_spec), out_specs=(tok_spec, P(None), tok_spec, P(None, None), exp_spec, exp_spec, exp_spec), check_vma=False)
```

time: 1390 us -> 1060 us (0.76)
  waiting for transfers between devices: 333 us -> 120 us
  Pallas kernels: 806 us -> 709 us
  starting transfers between devices: 96.2 us -> 79 us
    ppermute x3, waiting for transfers between devices: 260 us -> 12.2 us  [to_ep(): return lax.ppermute(far, 'ep', ep_perm)]
    pallas_call x9 -> x10, Pallas kernels: 763 us -> 660 us  [the longest x2 211 us: rest_tiles(): pl.pallas_call(functools.partial(rest_kernel, begun is not None), out_sha...]
    all_gather x2 -> x4, waiting for transfers between devices: 72.2 us -> 107 us  [the longest x3 94.9 us: device_step(): gathered.append(lax.all_gather(late, ('dp', 'ep'), tiled=True))]
    pallas_call x3 -> x6, Pallas kernels: 42.3 us -> 48.8 us  [merge(): pl.pallas_call(merge_kernel, out_shape=jax.ShapeDtypeStruct(whole.shape,...]
  transfers between devices with their start and end apart: 12 -> 17, of which waited for: 3 -> 5; matrix products, arithmetic and copies ran while one was open for 5% -> 7% of each run, Pallas kernels for 28% -> 46%
where the time goes in v3:
time: 1060 us; the launch traced here: 1050 us
  Pallas kernels  709 us (67%)
  waiting for transfers between devices  120 us (11%)
  starting transfers between devices  79 us (7%)
  other arithmetic  66.8 us (6%)
  local copies, waits for them, and re-layouts  29 us (3%)
  blocking collectives  21.9 us (2%)
  between operations  18.7 us (2%)
    pallas_call x2, Pallas kernels, rest_tiles(): pl.pallas_call(functools.partial(rest_kernel, begun is not None), out_sha...  211 us
    pallas_call x3, Pallas kernels, combine(): pl.pallas_call(functools.partial(combine_kernel, weighted, first, counts,...  162 us
    pallas_call x4, Pallas kernels, dispatch(): pl.pallas_call(functools.partial(dispatch_kernel, scaled, begun, n_exp),...  148 us
    pallas_call x1, Pallas kernels, own_tiles(): pl.pallas_call(own_kernel, out_shape=[thin_shape] * 3 + [wide_shape] * 2,...  139 us
    all_gather x3, waiting for transfers between devices, device_step(): gathered.append(lax.all_gather(late, ('dp', 'ep'), tiled=True))  94.9 us
    ppermute x3, starting transfers between devices, to_ep(): return lax.ppermute(far, 'ep', ep_perm)  58.9 us
    pallas_call x6, Pallas kernels, merge(): pl.pallas_call(merge_kernel, out_shape=jax.ShapeDtypeStruct(whole.shape,...  48.8 us
    all_gather x1, blocking collectives, device_step(): packets = lax.all_gather(packet, ('dp', 'ep'))  21.9 us
  transfers between devices with their start and end apart: 17, of which 5 were waited for; matrix products, arithmetic and copies ran while one was open for 7% of the time, Pallas kernels for 46%

profile of v3, /device:TPU:0, one launch (start us, length us, event | category | flops | bytes accessed | tf_op | source)
XLA Modules:
  0.0 1048.1 jit_solution(7799325640882145083)
XLA Ops:
  22.9 21.9 %all-gather.1 = f32[8,17,1024]{2,1,0:T(8,128)S(1)} all-gather(f32[1,17,1024]{2,1,0:T(8,128)S(1)} %maximum_bitcast_fusion), channel_id=2, replica_groups=mesh['ep'=2,'dp'=4] {'dp','ep'}, dimensions={0}, use_global_device_ids=true | all-gather | bytes 626688 | tf_op jit(solution)/shard_map/all_gather | solution.py:532
  62.5 4.9 broadcast_add_fusion
  78.2 11.9 %all-gather.9.cloned.1.call-done.src = bf16[4096,1536]{1,0:T(8,128)(2,1)} async-done(((bf16[512,1536]{1,0:T(8,128)(2,1)}), bf16[4096,1536]{1,0:T(8,128)(2,1)}) %all-gather.9.cloned.1.call-update) | async-done | bytes 12582928 | tf_op jit(solution)/shard_map/all_gather | solution.py:535
  90.1 36.5 %dispatch.2.rest_0_ = bf16[40960,1536]{1,0:T(8,128)(2,1)} custom-call(s32[16]{0:T(128)} %add.509.src_blk, s32[16]{0:T(128)} %add.526.ordinal, s32[32]{0:T(128)} %and_select_fusion.8.n_chunk.n_mix, s32[320]{0:T(512)} %copy-done.14, s32[320]{0:T(512)} %get-tuple-element.129.seg_src, s32[320]{0:T(512)} %get-tuple-element.128.seg_dst, ...), custom_call_target="tpu_custom_call" | custom-call | flops 20000000000 | bytes 80000000 | tf_op jit(solution)/shard_map/dispatch/pallas_call | solution.py:107
  126.6 31.8 %all-gather.13.cloned.1.call-done.src.rest_0_ = bf16[4096,1536]{1,0:T(8,128)(2,1)} async-done(((bf16[512,1536]{1,0:T(8,128)(2,1)}), bf16[4096,1536]{1,0:T(8,128)(2,1)}) %all-gather.13.cloned.1.call-update) | async-done | bytes 12582928 | tf_op jit(solution)/shard_map/all_gather | solution.py:538
  158.4 39.0 %dispatch_scaled.2.rest_0_ = bf16[40960,1536]{1,0:T(8,128)(2,1)} custom-call(s32[16]{0:T(128)} %add.509.src_blk, s32[16]{0:T(128)} %add.526.ordinal, s32[32]{0:T(128)} %and_select_fusion.8.n_chunk.n_mix, s32[320]{0:T(512)} %copy-done.14, s32[320]{0:T(512)} %get-tuple-element.129.seg_src, s32[320]{0:T(512)} %get-tuple-element.128.seg_dst, ...), custom_call_target="tpu_custom_call" | custom-call | flops 20000000000 | bytes 80000000 | tf_op jit(solution)/shard_map/dispatch_scaled/pallas_call | solution.py:107
  197.4 29.8 %all-gather.7.cloned.1.call-done.src = bf16[4096,1536]{1,0:T(8,128)(2,1)} async-done(((bf16[512,1536]{1,0:T(8,128)(2,1)}), bf16[4096,1536]{1,0:T(8,128)(2,1)}) %all-gather.7.cloned.1.call-update) | async-done | bytes 12582928 | tf_op jit(solution)/shard_map/all_gather | solution.py:538
  227.2 34.8 %dispatch.3.x = bf16[40960,1536]{1,0:T(8,128)(2,1)} custom-call(s32[16]{0:T(128)} %add.509.src_blk, s32[16]{0:T(128)} %add.514.ordinal, s32[32]{0:T(128)} %and_select_fusion.8.n_chunk.n_mix, s32[320]{0:T(512)} %copy-done.14, s32[320]{0:T(512)} %get-tuple-element.129.seg_src, s32[320]{0:T(512)} %get-tuple-element.128.seg_dst, ...), custom_call_target="tpu_custom_call", output_to_operand_aliasing={{}: (11, {})} | custom-call | flops 20000000000 | bytes 80000000 | tf_op jit(solution)/shard_map/dispatch/pallas_call | solution.py:107
  262.0 33.3 %all-gather.11.cloned.1.call-done.src.rest_1_ = bf16[4096,1536]{1,0:T(8,128)(2,1)} async-done(((bf16[512,1536]{1,0:T(8,128)(2,1)}), bf16[4096,1536]{1,0:T(8,128)(2,1)}) %all-gather.11.cloned.1.call-update) | async-done | bytes 12582928 | tf_op jit(solution)/shard_map/all_gather | solution.py:538
  295.4 37.4 %dispatch_scaled.3.d_rows = bf16[40960,1536]{1,0:T(8,128)(2,1)} custom-call(s32[16]{0:T(128)} %add.509.src_blk, s32[16]{0:T(128)} %add.514.ordinal, s32[32]{0:T(128)} %and_select_fusion.8.n_chunk.n_mix, s32[320]{0:T(512)} %copy-done.14, s32[320]{0:T(512)} %get-tuple-element.129.seg_src, ...), custom_call_target="tpu_custom_call", output_to_operand_aliasing={{}: (11, {})} | custom-call | flops 20000000000 | bytes 80000000 | tf_op jit(solution)/shard_map/dispatch_scaled/pallas_call | solution.py:107
  332.8 139.3 %own_tiles.1 = (bf16[20480,512]{1,0:T(8,128)(2,1)}, bf16[20480,512]{1,0:T(8,128)(2,1)}, bf16[20480,512]{1,0:T(8,128)(2,1)}, bf16[20480,1536]{1,0:T(8,128)(2,1)}, bf16[20480,1536]{1,0:T(8,128)(2,1)}) custom-call(s32[40]{0:T(128)} %get-tuple-element.152.tile_exp, s32[40]{0:T(128)} %get-tuple-element.148.tile_at, s32[40]{0:T(128)} %copy-done.34, ...), custom_call_target="tpu_custom_call" | custom-call | flops 120000004096 | bytes 250000000 | tf_op jit(solution)/shard_map/own_tiles/pallas_call | solution.py:330
  472.1 52.7 %combine.1 = (f32[2048,1536]{1,0:T(8,128)}, f32[1024,1536]{1,0:T(8,128)}, f32[1024,1536]{1,0:T(8,128)}) custom-call(s32[32]{0:T(128)} %select_n.248.at0, s32[32]{0:T(128)} %select_n.250.at1, s32[32]{0:T(128)} %and_select_fusion.8.n_chunk.n_mix, s32[320]{0:T(512)} %copy-done.14, s32[320]{0:T(512)} %get-tuple-element.129.seg_src, ...), custom_call_target="tpu_custom_call" | custom-call | flops 80000000000 | bytes 60000000 | tf_op jit(solution)/shard_map/combine/pallas_call | solution.py:224
  524.8 7.6 collective-permute-start
  532.4 53.2 %combine_weighted.2 = (f32[2048,1536]{1,0:T(8,128)}, f32[8,256,8]{2,1,0:T(8,128)}) custom-call(s32[32]{0:T(128)} %select_n.248.at0, s32[32]{0:T(128)} %select_n.250.at1, s32[32]{0:T(128)} %and_select_fusion.8.n_chunk.n_mix, s32[320]{0:T(512)} %copy-done.14, s32[320]{0:T(512)} %get-tuple-element.129.seg_src, s32[320]{0:T(512)} %get-tuple-element.100.seg_dst, ...), custom_call_target="tpu_custom_call" | custom-call | flops 40000000000 | bytes 60000000 | tf_op jit(solution)/shard_map/combine_weighted/pallas_call | solution.py:224
  585.8 8.7 slice_add_fusion.3
  594.5 8.5 collective-permute-start.1
  605.7 19.8 %collective-permute-start.4 = (f32[1024,1536]{1,0:T(8,128)}, f32[1024,1536]{1,0:T(8,128)}, u32[]{:S(2)}, u32[]{:S(2)}) collective-permute-start(f32[1024,1536]{1,0:T(8,128)} %slice_add_fusion.3), channel_id=1, source_target_pairs={{0,4},{4,0},{1,5},{5,1},{2,6},{6,2},{3,7},{7,3}} | collective-permute-start | bytes 18874376 | tf_op jit(solution)/shard_map/ppermute | solution.py:491
  625.5 56.0 %combine_weighted.3 = (f32[1024,1536]{1,0:T(8,128)}, f32[1024,1536]{1,0:T(8,128)}, f32[8,256,8]{2,1,0:T(8,128)}) custom-call(s32[32]{0:T(128)} %select_n.248.at0, s32[32]{0:T(128)} %select_n.250.at1, s32[32]{0:T(128)} %and_select_fusion.8.n_chunk.n_mix, s32[320]{0:T(512)} %copy-done.14, s32[320]{0:T(512)} %get-tuple-element.129.seg_src, ...), custom_call_target="tpu_custom_call" | custom-call | flops 40000000000 | bytes 60000000 | tf_op jit(solution)/shard_map/combine_weighted/pallas_call | solution.py:224
  685.1 8.8 slice_add_fusion.1
  693.9 6.0 collective-permute-start.3
  699.8 110.6 %rest_tiles.2 = (bf16[5,1536,512]{2,1,0:T(8,128)(2,1)}, bf16[5,1536,512]{2,1,0:T(8,128)(2,1)}, bf16[5,512,1536]{2,1,0:T(8,128)(2,1)}, bf16[20,1536,512]{2,1,0:T(...) custom-call(s32[40]{0:T(128)} %copy-done.23, s32[40]{0:T(128)} %get-tuple-element.140.tile_at, ...), custom_call_target="tpu_custom_call" | custom-call | flops 80000000000 | bytes 150000000 | tf_op jit(solution)/shard_map/rest_tiles/pallas_call | solution.py:350
  810.9 100.2 %rest_tiles.3 = (bf16[5,1536,512]{2,1,0:T(8,128)(2,1)}, bf16[5,1536,512]{2,1,0:T(8,128)(2,1)}, bf16[5,512,1536]{2,1,0:T(8,128)(2,1)}, bf16[20,1536,512]{2,1,0:T(...) custom-call(s32[40]{0:T(128)} %copy-done.22, ...), custom_call_target="tpu_custom_call", output_to_operand_aliasing={{3}: (16, {}), {4}: (17, {}), {5}: (18, {})} | custom-call | flops 80000000000 | bytes 150000000 | tf_op jit(solution)/shard_map/rest_tiles/pallas_call | solution.py:350
  913.9 33.2 %collective-permute-start.5 = (f32[4,256,8]{2,1,0:T(8,128)S(1)}, f32[4,256,8]{2,1,0:T(8,128)}, u32[]{:S(2)}, u32[]{:S(2)}) collective-permute-start(f32[4,256,8]{2,1,0:T(8,128)S(1)} %copy-done.11), channel_id=1, source_target_pairs={{0,4},{4,0},{1,5},{5,1},{2,6},{6,2},{3,7},{7,3}} | collective-permute-start | bytes 98312 | tf_op jit(solution)/shard_map/ppermute | solution.py:491
  947.1 12.2 %collective-permute-done.5 = f32[4,256,8]{2,1,0:T(8,128)} collective-permute-done((f32[4,256,8]{2,1,0:T(8,128)S(1)}, f32[4,256,8]{2,1,0:T(8,128)}, u32[]{:S(2)}, u32[]{:S(2)}) %collective-permute-start.5) | collective-permute-done | bytes 32800 | tf_op jit(solution)/shard_map/ppermute | solution.py:491
  971.4 7.7 fusion.9
  979.1 10.3 fusion.8
  989.4 8.1 merge.6.whole_in
  997.5 8.2 merge.8.whole_in
  1005.7 8.1 merge.7
  1013.8 8.1 merge.9
  1022.0 8.1 merge.10.whole_in
  1030.1 8.1 merge.11
  (207 shorter events, 64.5 us)
Async XLA Ops:
  7.2 82.9 %all-gather.9.cloned.1.call-start = ((), (), s32[]{:S(2)}) async-start(), calls=%async_computation.1 | async-start | bytes 14155776 | tf_op jit(solution)/shard_map/all_gather | solution.py:535
  15.8 142.6 %all-gather.13.cloned.1.call-start = ((), (), s32[]{:S(2)}) async-start(), calls=%async_computation.3 | async-start | bytes 14155776 | tf_op jit(solution)/shard_map/all_gather | solution.py:538
  19.6 207.6 %all-gather.7.cloned.1.call-start = ((), (), s32[]{:S(2)}) async-start(), calls=%async_computation | async-start | bytes 14155776 | tf_op jit(solution)/shard_map/all_gather | solution.py:538
  20.3 275.0 %all-gather.11.cloned.1.call-start = ((), (), s32[]{:S(2)}) async-start(), calls=%async_computation.2 | async-start | bytes 14155776 | tf_op jit(solution)/shard_map/all_gather | solution.py:538
  20.9 1017.3 %all-reduce.3.cloned.1.call-start = ((), (), s32[]{:S(2)}) async-start(), calls=%async_computation.4 | async-start | bytes 491520 | tf_op jit(solution)/shard_map/psum | solution.py:587
  71.4 55.1 %copy-start.23 = (s32[40]{0:T(128)}, s32[40]{0:T(128)S(1)}, u32[]{:S(2)}) copy-start(s32[40]{0:T(128)S(1)} %broadcast_minimum_fusion.tile_exp) | copy-start | bytes 484
  71.4 55.1 %copy-start.22 = (s32[40]{0:T(128)}, s32[40]{0:T(128)S(1)}, u32[]{:S(2)}) copy-start(s32[40]{0:T(128)S(1)} %broadcast_minimum_fusion.1.tile_exp) | copy-start | bytes 484
  524.8 60.8 %collective-permute-start = (f32[2048,1536]{1,0:T(8,128)}, f32[2048,1536]{1,0:T(8,128)}, u32[]{:S(2)}, u32[]{:S(2)}) collective-permute-start(f32[2048,1536]{1,0:T(8,128)} %get-tuple-element.48), channel_id=1, source_target_pairs={{0,1},{1,0},{2,3},{3,2},{4,5},{5,4},{6,7},{7,6}} | collective-permute-start | bytes 37748744 | tf_op jit(solution)/shard_map/ppermute | solution.py:488
  585.7 18.5 %copy-start.28 = (s32[40]{0:T(128)S(1)}, s32[40]{0:T(128)}, u32[]{:S(2)}) copy-start(s32[40]{0:T(128)} %get-tuple-element.84) | copy-start | bytes 484
  585.7 18.5 %copy-start.29 = (s32[40]{0:T(128)S(1)}, s32[40]{0:T(128)}, u32[]{:S(2)}) copy-start(s32[40]{0:T(128)} %get-tuple-element.88) | copy-start | bytes 484
  585.7 18.5 %copy-start.30 = (s32[40]{0:T(128)S(1)}, s32[40]{0:T(128)}, u32[]{:S(2)}) copy-start(s32[40]{0:T(128)} %get-tuple-element.91) | copy-start | bytes 484
  585.7 18.5 %copy-start.31 = (s32[40]{0:T(128)S(1)}, s32[40]{0:T(128)}, u32[]{:S(2)}) copy-start(s32[40]{0:T(128)} %get-tuple-element.93) | copy-start | bytes 484
  585.7 19.1 %copy-start.24 = (s32[40]{0:T(128)S(1)}, s32[40]{0:T(128)}, u32[]{:S(2)}) copy-start(s32[40]{0:T(128)} %get-tuple-element.83) | copy-start | bytes 484
  585.7 19.1 %copy-start.25 = (s32[40]{0:T(128)S(1)}, s32[40]{0:T(128)}, u32[]{:S(2)}) copy-start(s32[40]{0:T(128)} %get-tuple-element.87) | copy-start | bytes 484
  585.7 19.1 %copy-start.26 = (s32[40]{0:T(128)S(1)}, s32[40]{0:T(128)}, u32[]{:S(2)}) copy-start(s32[40]{0:T(128)} %get-tuple-element.90) | copy-start | bytes 484
  585.7 19.0 %copy-start.27 = (s32[40]{0:T(128)S(1)}, s32[40]{0:T(128)}, u32[]{:S(2)}) copy-start(s32[40]{0:T(128)} %get-tuple-element.92) | copy-start | bytes 484
  585.8 19.6 %copy-start.10 = (f32[8,256,8]{2,1,0:T(8,128)S(1)}, f32[8,256,8]{2,1,0:T(8,128)}, u32[]{:S(2)}) copy-start(f32[8,256,8]{2,1,0:T(8,128)} %get-tuple-element.55) | copy-start | bytes 196612
  594.5 90.6 %collective-permute-start.1 = (f32[2048,1536]{1,0:T(8,128)}, f32[2048,1536]{1,0:T(8,128)}, u32[]{:S(2)}, u32[]{:S(2)}) collective-permute-start(f32[2048,1536]{1,0:T(8,128)} %get-tuple-element.51), channel_id=1, source_target_pairs={{0,1},{1,0},{2,3},{3,2},{4,5},{5,4},{6,7},{7,6}} | collective-permute-start | bytes 37748744 | tf_op jit(solution)/shard_map/ppermute | solution.py:488
  605.7 75.8 %collective-permute-start.2 = (f32[8,256,8]{1,2,0:T(8,128)S(1)}, f32[8,256,8]{1,2,0:T(8,128)S(1)}, u32[]{:S(2)}, u32[]{:S(2)}) collective-permute-start(f32[8,256,8]{1,2,0:T(8,128)S(1)} %copy.76), channel_id=1, source_target_pairs={{0,1},{1,0},{2,3},{3,2},{4,5},{5,4},{6,7},{7,6}} | collective-permute-start | bytes 196616 | tf_op jit(solution)/shard_map/ppermute | solution.py:488
  605.7 308.2 %collective-permute-start.4 = (f32[1024,1536]{1,0:T(8,128)}, f32[1024,1536]{1,0:T(8,128)}, u32[]{:S(2)}, u32[]{:S(2)}) collective-permute-start(f32[1024,1536]{1,0:T(8,128)} %slice_add_fusion.3), channel_id=1, source_target_pairs={{0,4},{4,0},{1,5},{5,1},{2,6},{6,2},{3,7},{7,3}} | collective-permute-start | bytes 18874376 | tf_op jit(solution)/shard_map/ppermute | solution.py:491
  693.9 268.8 %collective-permute-start.3 = (f32[1024,1536]{1,0:T(8,128)}, f32[1024,1536]{1,0:T(8,128)}, u32[]{:S(2)}, u32[]{:S(2)}) collective-permute-start(f32[1024,1536]{1,0:T(8,128)} %slice_add_fusion.1), channel_id=1, source_target_pairs={{0,4},{4,0},{1,5},{5,1},{2,6},{6,2},{3,7},{7,3}} | collective-permute-start | bytes 18874376 | tf_op jit(solution)/shard_map/ppermute | solution.py:491
  810.4 157.6 %collective-permute-start.6 = (bf16[5,1536,512]{2,1,0:T(8,128)(2,1)}, bf16[5,1536,512]{2,1,0:T(8,128)(2,1)}, u32[]{:S(2)}, u32[]{:S(2)}) collective-permute-start(bf16[5,1536,512]{2,1,0:T(8,128)(2,1)} %get-tuple-element.67), channel_id=1, source_target_pairs={{0,1},{1,0},{2,3},{3,2},{4,5},{5,4},{6,7},{7,6}} | collective-permute-start | bytes 23592968 | tf_op jit(solution)/shard_map/ppermute | solution.py:488
  810.4 187.1 %collective-permute-start.8 = (bf16[5,1536,512]{2,1,0:T(8,128)(2,1)}, bf16[5,1536,512]{2,1,0:T(8,128)(2,1)}, u32[]{:S(2)}, u32[]{:S(2)}) collective-permute-start(bf16[5,1536,512]{2,1,0:T(8,128)(2,1)} %get-tuple-element.70), channel_id=1, source_target_pairs={{0,1},{1,0},{2,3},{3,2},{4,5},{5,4},{6,7},{7,6}} | collective-permute-start | bytes 23592968 | tf_op jit(solution)/shard_map/ppermute | solution.py:488
  810.9 103.0 %copy-start.11 = (f32[4,256,8]{2,1,0:T(8,128)S(1)}, f32[4,256,8]{2,1,0:T(8,128)}, u32[]{:S(2)}) copy-start(f32[4,256,8]{2,1,0:T(8,128)} %slice.135) | copy-start | bytes 98308
  810.9 156.8 %copy-start.13 = (s32[1024,8]{0,1:T(8,128)S(1)}, s32[1024,8]{0,1:T(8,128)}, u32[]{:S(2)}) copy-start(s32[1024,8]{0,1:T(8,128)} %param.10) | copy-start | bytes 98308
  810.9 157.0 %copy-start.9 = (f32[1024,40]{0,1:T(8,128)S(1)}, f32[1024,40]{0,1:T(8,128)}, u32[]{:S(2)}) copy-start(f32[1024,40]{0,1:T(8,128)} %copy-done.8) | copy-start | bytes 491524
  810.9 157.2 %copy-start.2 = (bf16[1024,1536]{1,0:T(8,128)(2,1)S(1)}, bf16[1024,1536]{1,0:T(8,128)(2,1)}, u32[]{:S(2)}) copy-start(bf16[1024,1536]{1,0:T(8,128)(2,1)} %copy-done.1) | copy-start | bytes 9437188
  911.1 94.5 %collective-permute-start.7 = (bf16[5,1536,512]{2,1,0:T(8,128)(2,1)}, bf16[5,1536,512]{2,1,0:T(8,128)(2,1)}, u32[]{:S(2)}, u32[]{:S(2)}) collective-permute-start(bf16[5,1536,512]{2,1,0:T(8,128)(2,1)} %get-tuple-element.68), channel_id=1, source_target_pairs={{0,1},{1,0},{2,3},{3,2},{4,5},{5,4},{6,7},{7,6}} | collective-permute-start | bytes 23592968 | tf_op jit(solution)/shard_map/ppermute | solution.py:488
  913.9 45.4 %collective-permute-start.5 = (f32[4,256,8]{2,1,0:T(8,128)S(1)}, f32[4,256,8]{2,1,0:T(8,128)}, u32[]{:S(2)}, u32[]{:S(2)}) collective-permute-start(f32[4,256,8]{2,1,0:T(8,128)S(1)} %copy-done.11), channel_id=1, source_target_pairs={{0,4},{4,0},{1,5},{5,1},{2,6},{6,2},{3,7},{7,3}} | collective-permute-start | bytes 98312 | tf_op jit(solution)/shard_map/ppermute | solution.py:491
  959.3 54.5 %collective-permute-start.9 = (bf16[5,1536,512]{2,1,0:T(8,128)(2,1)}, bf16[5,1536,512]{2,1,0:T(8,128)(2,1)}, u32[]{:S(2)}, u32[]{:S(2)}) collective-permute-start(bf16[5,1536,512]{2,1,0:T(8,128)(2,1)} %get-tuple-element.71), channel_id=1, source_target_pairs={{0,1},{1,0},{2,3},{3,2},{4,5},{5,4},{6,7},{7,6}} | collective-permute-start | bytes 23592968 | tf_op jit(solution)/shard_map/ppermute | solution.py:488
  962.7 59.3 %collective-permute-start.10 = (bf16[5,512,1536]{2,1,0:T(8,128)(2,1)}, bf16[5,512,1536]{2,1,0:T(8,128)(2,1)}, u32[]{:S(2)}, u32[]{:S(2)}) collective-permute-start(bf16[5,512,1536]{2,1,0:T(8,128)(2,1)} %get-tuple-element.73), channel_id=1, source_target_pairs={{0,1},{1,0},{2,3},{3,2},{4,5},{5,4},{6,7},{7,6}} | collective-permute-start | bytes 23592968 | tf_op jit(solution)/shard_map/ppermute | solution.py:488
  968.0 62.1 %collective-permute-start.11 = (bf16[5,512,1536]{2,1,0:T(8,128)(2,1)}, bf16[5,512,1536]{2,1,0:T(8,128)(2,1)}, u32[]{:S(2)}, u32[]{:S(2)}) collective-permute-start(bf16[5,512,1536]{2,1,0:T(8,128)(2,1)} %get-tuple-element.74), channel_id=1, source_target_pairs={{0,1},{1,0},{2,3},{3,2},{4,5},{5,4},{6,7},{7,6}} | collective-permute-start | bytes 23592968 | tf_op jit(solution)/shard_map/ppermute | solution.py:488
  (20 other events, 172.5 us)
Sparse Core Ops, SparseCore 0:
  15.9 74.1 all-gather.8
  91.9 66.4 all-gather.12
  160.8 66.4 all-gather.6
  228.9 66.4 all-gather.10
  969.6 51.8 all-reduce.2

commit v4 on v3

--- a/solution.py
+++ b/solution.py
@@ -36,9 +36,10 @@
     return lax.dot_general(left, right, dims, preferred_element_type=jnp.float32)
 
 
-def dispatch_kernel(scaled, begun, n_exp, src_blk, ordinal, n_chunk, seg_len, seg_src, seg_dst, tail_at, tail_len, src, pos, gates, *rest):
-    out, stack, blank, sems, tail_sem = rest[1:] if begun else rest
+def dispatch_kernel(scaled, begun, first, n_exp, n_chunk, seg_len, seg_src, seg_dst, tail_at, tail_len, pos, gates, *rest):
+    *srcs, out, stack, blank, src, sems, src_sems, tail_sem = rest[1:] if begun else rest
     step = pl.program_id(0)
+    src_blocks = srcs[0].shape[0] // BLOCK
     last = pl.num_programs(0) - 1
     slot = lax.rem(step, 2)
 
@@ -55,11 +56,30 @@
                 act(segment_copy(blk, buf, exp, grp))
 
     def each_tail(act):
-        for exp in range(n_exp):
-            @pl.loop(0, tail_len[exp])
+        @pl.loop(0, 2 * n_exp)
+        def _(tail):
+            @pl.loop(0, tail_len[tail])
             def _(grp):
-                to_row = pl.multiple_of((tail_at[exp] + grp) * GROUP, GROUP)
+                to_row = pl.multiple_of((tail_at[tail] + grp) * GROUP, GROUP)
                 act(pltpu.make_async_copy(blank, out.at[pl.ds(to_row, GROUP), :], tail_sem))
+
+    def start_source(blk, buf):
+        which = lax.div(blk, src_blocks)
+        at = pl.ds(pl.multiple_of(lax.rem(blk, src_blocks) * BLOCK, BLOCK), BLOCK)
+        for k, ref in enumerate(srcs):
+            @pl.when(which == k)
+            def _():
+                pltpu.make_async_copy(ref.at[at, :], src.at[buf], src_sems.at[buf]).start()
+
+    @pl.when(step == 0)
+    def _():
+        start_source(step, 0)
+
+    @pl.when(step < last)
+    def _():
+        start_source(step + 1, 1 - slot)
+
+    pltpu.make_async_copy(srcs[0].at[pl.ds(0, BLOCK), :], src.at[slot], src_sems.at[slot]).wait()
 
     if not begun:
         @pl.when(step == 0)
@@ -69,9 +89,9 @@
 
     @pl.when(step >= 2)
     def _():
-        each_segment(ordinal[step - 2], slot, lambda copy: copy.wait())
-
-    @pl.loop(0, n_chunk[ordinal[step]])
+        each_segment(first + step - 2, slot, lambda copy: copy.wait())
+
+    @pl.loop(0, n_chunk[first + step])
     def _(chunk):
         row = lax.broadcasted_iota(jnp.int32, (CHUNK, BLOCK), 0) + chunk * CHUNK
         hit = pos[0, 0:1, :] == row
@@ -82,56 +102,57 @@
             hit = jnp.logical_or(hit, here)
             if scaled:
                 weight = jnp.where(here, gates[0, k:k + 1, :], weight)
-        picked = dot32(jnp.where(hit, 1.0, 0.0).astype(jnp.bfloat16), src[...])
+        picked = dot32(jnp.where(hit, 1.0, 0.0).astype(jnp.bfloat16), src[slot])
         if scaled:
             picked = picked * jnp.sum(weight, axis=1, keepdims=True)
         stack[slot, pl.ds(pl.multiple_of(chunk * CHUNK, CHUNK), CHUNK), :] = picked.astype(jnp.bfloat16)
 
-    each_segment(ordinal[step], slot, lambda copy: copy.start())
+    each_segment(first + step, slot, lambda copy: copy.start())
 
     @pl.when(step == last)
     def _():
-        each_segment(ordinal[step - 1], 1 - slot, lambda copy: copy.wait())
-        each_segment(ordinal[step], slot, lambda copy: copy.wait())
+        each_segment(first + step - 1, 1 - slot, lambda copy: copy.wait())
+        each_segment(first + step, slot, lambda copy: copy.wait())
         if not begun:
             each_tail(lambda copy: copy.wait())
 
 
-def dispatch(src, pos, gates, plan, part, out, rows, scaled):
+def dispatch(srcs, pos, gates, plan, first, out, rows, scaled):
     top_k = pos.shape[1]
-    src_blk, ordinal = plan["parts"][part]
     begun = out is not None
-    width = src.shape[1]
-    n_exp = plan["tail_at"].shape[0]
+    width = srcs[0].shape[1]
+    n_exp = plan["n_exp"]
     stack_rows = -(-(BLOCK * top_k + n_exp * (GROUP - 1)) // CHUNK) * CHUNK
+    any_spec = pl.BlockSpec(memory_space=pl.ANY)
     return pl.pallas_call(
-        functools.partial(dispatch_kernel, scaled, begun, n_exp),
+        functools.partial(dispatch_kernel, scaled, begun, first, n_exp),
         out_shape=jax.ShapeDtypeStruct((rows, width), jnp.bfloat16),
         grid_spec=pltpu.PrefetchScalarGridSpec(
-            num_scalar_prefetch=8,
-            grid=(ordinal.shape[0],),
+            num_scalar_prefetch=6,
+            grid=(sum(src.shape[0] for src in srcs) // BLOCK,),
             in_specs=[
-                pl.BlockSpec((BLOCK, width), lambda i, blk, *_: (blk[i], 0)),
-                pl.BlockSpec((1, top_k, BLOCK), lambda i, blk, ordinal, *_: (ordinal[i], 0, 0)),
-                pl.BlockSpec((1, top_k, BLOCK), lambda i, blk, ordinal, *_: (ordinal[i], 0, 0)),
+                pl.BlockSpec((1, top_k, BLOCK), lambda i, *_: (first + i, 0, 0)),
+                pl.BlockSpec((1, top_k, BLOCK), lambda i, *_: (first + i, 0, 0)),
             ]
-            + [pl.BlockSpec(memory_space=pl.ANY)] * begun,
-            out_specs=pl.BlockSpec(memory_space=pl.ANY),
+            + [any_spec] * (begun + len(srcs)),
+            out_specs=any_spec,
             scratch_shapes=[
                 pltpu.VMEM((2, stack_rows, width), jnp.bfloat16),
                 pltpu.VMEM((GROUP, width), jnp.bfloat16),
+                pltpu.VMEM((2, BLOCK, width), jnp.bfloat16),
+                pltpu.SemaphoreType.DMA((2,)),
                 pltpu.SemaphoreType.DMA((2,)),
                 pltpu.SemaphoreType.DMA,
             ],
         ),
         compiler_params=pltpu.CompilerParams(dimension_semantics=("arbitrary",), vmem_limit_bytes=VMEM_LIMIT),
-        input_output_aliases={11: 0} if begun else {},
-        cost_estimate=pl.CostEstimate(flops=20_000_000_000, bytes_accessed=80_000_000, transcendentals=0),
+        input_output_aliases={8: 0} if begun else {},
+        cost_estimate=pl.CostEstimate(flops=40_000_000_000, bytes_accessed=80_000_000, transcendentals=0),
         name="dispatch_scaled" if scaled else "dispatch",
-    )(src_blk, ordinal, plan["n_chunk"], plan["seg_len"], plan["seg_src"], plan["seg_dst"], plan["tail_at"], plan["tail_len"], src, pos, gates, *([out] * begun))
-
-
-def combine_kernel(weighted, first, counts, dev_blocks, n_exp, at0, at1, n_mix, seg_len, seg_src, seg_dst, rows, pos, gates, *rest):
+    )(plan["n_chunk"], plan["seg_len"], plan["seg_src"], plan["seg_dst"], plan["tail_at"], plan["tail_len"], pos, gates, *([out] * begun), *srcs)
+
+
+def combine_kernel(weighted, first, counts, dev_blocks, n_exp, n_mix, seg_len, seg_src, seg_dst, rows, pos, gates, *rest):
     if weighted:
         d_out0, d_out1, *outs, d_gates, stack, total, sems = rest
     else:
@@ -172,7 +193,7 @@
         part_rows = stack[slot, pl.ds(pl.multiple_of(part * MIX, MIX), MIX), :]
         top_k = pos.shape[2]
         if weighted:
-            late = lax.rem(step, dev_blocks) >= dev_blocks // 2
+            late = step >= dev_blocks
             cross = dot32(jnp.where(late, d_out1[...], d_out0[...]), part_rows, NT_DIMS)
             weight = jnp.zeros((BLOCK, MIX), jnp.float32)
             d_cols = []
@@ -205,8 +226,9 @@
 def combine(rows, pos_t, gates_t, d_outs, plan, first, counts, weighted):
     _, _, top_k = pos_t.shape
     width = rows.shape[1]
-    n_exp = plan["tail_at"].shape[0]
+    n_exp = plan["n_exp"]
     blocks = sum(counts)
+    dev_blocks = plan["dev_blocks"]
     stack_rows = -(-(BLOCK * top_k + n_exp * (GROUP - 1)) // MIX) * MIX
     out_shape, out_specs, begin = [], [], 0
     for count in counts:
@@ -218,14 +240,14 @@
         out_shape.append(jax.ShapeDtypeStruct((blocks, BLOCK, top_k), jnp.float32))
         out_specs.append(pl.BlockSpec((1, BLOCK, top_k), lambda i, *_: (i, 0, 0)))
         d_specs = [
-            pl.BlockSpec((BLOCK, width), lambda i, at0, at1, *_: (at0[first + i], 0)),
-            pl.BlockSpec((BLOCK, width), lambda i, at0, at1, *_: (at1[first + i], 0)),
+            pl.BlockSpec((BLOCK, width), lambda i, *_: (jnp.minimum(i, dev_blocks - 1), 0)),
+            pl.BlockSpec((BLOCK, width), lambda i, *_: (jnp.maximum(i - dev_blocks, 0), 0)),
         ]
     return pl.pallas_call(
-        functools.partial(combine_kernel, weighted, first, counts, plan["dev_blocks"], n_exp),
+        functools.partial(combine_kernel, weighted, first, counts, dev_blocks, n_exp),
         out_shape=out_shape,
         grid_spec=pltpu.PrefetchScalarGridSpec(
-            num_scalar_prefetch=6,
+            num_scalar_prefetch=4,
             grid=(blocks,),
             in_specs=[
                 pl.BlockSpec(memory_space=pl.ANY),
@@ -243,7 +265,7 @@
         compiler_params=pltpu.CompilerParams(dimension_semantics=("arbitrary",), vmem_limit_bytes=VMEM_LIMIT),
         cost_estimate=pl.CostEstimate(flops=5_000_000_000 * blocks, bytes_accessed=60_000_000, transcendentals=0),
         name="combine_weighted" if weighted else "combine",
-    )(*plan["d_at"], plan["n_mix"], plan["seg_len"], plan["seg_src"], plan["seg_own"], rows, pos_t, gates_t, *(d_outs if weighted else ()))
+    )(plan["n_mix"], plan["seg_len"], plan["seg_src"], plan["seg_own"], rows, pos_t, gates_t, *(d_outs if weighted else ()))
 
 
 def by_kind(kind, body):
@@ -339,7 +361,7 @@
 
 def rest_tiles(x, d_rows, w_gate, w_up, w_down, hidden, d_gate, d_up, plan, half, begun):
     width, mid = w_gate.shape[1:]
-    n_half = plan["tail_at"].shape[0] // 2
+    n_half = plan["n_exp"] // 2
     seq = plan["rest_seq"][half]
     shapes = [(width, mid), (width, mid), (mid, width)]
     wide = pl.BlockSpec((TILE, width), lambda t, exp, at, *_: (at[t], 0))
@@ -391,8 +413,7 @@
     return jnp.cumsum(values, axis=axis) - values
 
 
-def make_plan(local_ids, dev_order, own_blocks, n_exp, max_tiles, max_own, weight_base):
-    order = jnp.arange(local_ids.shape[0])
+def make_plan(local_ids, own_blocks, n_exp, max_tiles, max_own, weight_base):
     onehot = (local_ids[:, :, None, :] == jnp.arange(n_exp)[None, None, :, None]).astype(jnp.float32)
     hits = jnp.sum(onehot, axis=1)
     before = jnp.triu(jnp.ones((BLOCK, BLOCK), jnp.bfloat16), 1)
@@ -400,13 +421,15 @@
     seg_len = (jnp.sum(hits, axis=2).astype(jnp.int32) + GROUP - 1) // GROUP
     seg_src = exclusive(seg_len, 1)
     per_tile, per_half = TILE // GROUP, HALF // GROUP
-    groups = jnp.sum(seg_len, axis=0)
-    tiles = (groups + per_tile - 1) // per_tile
+    groups = jnp.stack([jnp.sum(seg_len[:own_blocks], axis=0), jnp.sum(seg_len[own_blocks:], axis=0)])
+    both_tiles = (groups + per_tile - 1) // per_tile
+    own_tiles, other_tiles = both_tiles
+    tiles = own_tiles + other_tiles
     tile_base = exclusive(tiles)
-    seg_dst = tile_base[None, :] * per_tile + exclusive(seg_len, 0)
+    begins = jnp.stack([tile_base, tile_base + own_tiles]) * per_tile
+    seg_dst = jnp.concatenate([begins[0] + exclusive(seg_len[:own_blocks], 0), begins[1] + exclusive(seg_len[own_blocks:], 0)])
     place = rank + (seg_src * GROUP).astype(jnp.float32)[:, :, None]
     pos = jnp.sum(onehot * (place[:, None] + 1.0), axis=2).astype(jnp.int32) - 1
-    own_tiles = (jnp.sum(seg_len[:own_blocks], axis=0) + per_tile - 1) // per_tile
     exp_ids = jnp.arange(n_exp)
 
     def sequence(counts, length):
@@ -418,8 +441,7 @@
         pick = lambda table: jnp.sum(is_exp * table[None, :], axis=1)
         return exp, at - pick(ends - counts), ids > at, pick
 
-    def kind_of(pick, nth, past):
-        left = pick(groups) - nth * per_tile
+    def kind_of(left, past):
         return jnp.where(past, 0, jnp.where(left <= per_half, 1, 2))
 
     o_exp, o_nth, o_past, o_pick = sequence(own_tiles, max_own)
@@ -428,9 +450,9 @@
     def rest_seq(half):
         mine = exp_ids // (n_exp // 2) == half
         exp, nth, past, pick = sequence(jnp.where(mine, tiles, 0), max_tiles // 2)
-        kind = kind_of(pick, nth, past)
         own_count = pick(own_tiles)
         is_own = nth < own_count
+        kind = kind_of(jnp.where(is_own, pick(groups[0]) - nth * per_tile, pick(groups[1]) - (nth - own_count) * per_tile), past)
         seq = (
             exp,
             pick(tile_base) + nth,
@@ -442,33 +464,18 @@
         )
         return seq
 
-    dev_blocks = order.shape[0] // dev_order.shape[0]
-    part_blocks = dev_blocks // 2
-    in_part = jnp.arange(part_blocks)
-
-    def part_of(part):
-        blk = dev_order[:, None] * part_blocks + in_part[None, :]
-        ordinal = jnp.arange(dev_order.shape[0])[:, None] * dev_blocks + part * part_blocks + in_part[None, :]
-        return blk.reshape(-1), ordinal.reshape(-1)
-
-    d_at = dev_order[:, None] * part_blocks + jnp.arange(dev_blocks)[None, :] % part_blocks
-    early = jnp.arange(dev_blocks)[None, :] < part_blocks
-    d_at0 = jnp.where(early, d_at, d_at[:, part_blocks - 1:part_blocks])
-    d_at1 = jnp.where(early, d_at[:, :1], d_at)
     stack_rows = jnp.sum(seg_len, axis=1) * GROUP
     plan = {
-        "parts": (part_of(0), part_of(1)),
-        "d_at": (d_at0.reshape(-1), d_at1.reshape(-1)),
         "n_chunk": (stack_rows + CHUNK - 1) // CHUNK,
         "n_mix": (stack_rows + MIX - 1) // MIX,
         "seg_len": seg_len.reshape(-1),
         "seg_src": seg_src.reshape(-1),
         "seg_dst": seg_dst.reshape(-1),
         "seg_own": (own_base[None, :] * per_tile + exclusive(seg_len, 0)).reshape(-1),
-        "tail_at": tile_base * per_tile + groups,
-        "tail_len": (groups + per_half - 1) // per_half * per_half - groups,
+        "tail_at": (begins + groups).reshape(-1),
+        "tail_len": ((groups + per_half - 1) // per_half * per_half - groups).reshape(-1),
         "base": weight_base.reshape(1),
-        "own_seq": (o_exp + weight_base, o_pick(tile_base) + o_nth, o_pick(own_base) + o_nth, kind_of(o_pick, o_nth, o_past)),
+        "own_seq": (o_exp + weight_base, o_pick(tile_base) + o_nth, o_pick(own_base) + o_nth, kind_of(o_pick(groups[0]) - o_nth * per_tile, o_past)),
         "rest_seq": (rest_seq(0), rest_seq(1)),
     }
     return jax.tree.map(lambda value: value.astype(jnp.int32), plan), pos
@@ -482,6 +489,7 @@
     tok_spec = P(("dp", "ep"), None)
     exp_spec = P("ep", None, None)
     core_perm = [(i, i ^ 1) for i in range(dp_size)]
+    x_perm = [(i, i ^ cores) for i in range(dp_size)]
     ep_perm = [(i, i ^ 1) for i in range(ep_size)]
 
     def to_core(away):
@@ -489,6 +497,15 @@
 
     def to_ep(far):
         return lax.ppermute(far, "ep", ep_perm)
+
+    def to_x(block):
+        return lax.ppermute(block, "dp", x_perm)
+
+    def spread(block):
+        ep_block = to_ep(block)
+        core_block = to_core(block)
+        own = (to_core(ep_block), core_block, ep_block, block)
+        return own, (to_x(block), to_x(ep_block))
 
     def after(value, other):
         return lax.optimization_barrier((value, other))
@@ -503,9 +520,8 @@
         dev_blocks = tok_rows // BLOCK
         own_devs = devices // 2
         own_blocks = own_devs * dev_blocks
-        seg_pad = devices * dev_blocks * (GROUP - 1)
         max_own = n_exp * -(-(own_devs * MAX_HITS + own_blocks * (GROUP - 1)) // TILE)
-        max_tiles = n_exp * -(-(devices * MAX_HITS + seg_pad) // TILE)
+        max_tiles = 2 * max_own
 
         ep_at = lax.axis_index("ep")
         dp_at = lax.axis_index("dp")
@@ -517,7 +533,7 @@
 
         dev_order = jnp.stack(
             [dev_of(x_at, 1 - core_at, 1 - ep_at), dev_of(x_at, 1 - core_at, ep_at), dev_of(x_at, core_at, 1 - ep_at), dev_of(x_at, core_at, ep_at)]
-            + [dev_of(1 - x_at, core, ep) for core in range(cores) for ep in range(ep_size)]
+            + [dev_of(1 - x_at, core_at, ep_at), dev_of(1 - x_at, core_at, 1 - ep_at), dev_of(1 - x_at, 1 - core_at, ep_at), dev_of(1 - x_at, 1 - core_at, 1 - ep_at)]
         )
         tokens32 = tokens.astype(jnp.float32)
         gain32 = norm_gain.astype(jnp.float32)
@@ -530,13 +546,8 @@
         prob_sums = jnp.pad(jnp.sum(router_probs, axis=0), (0, tok_rows - experts))
         packet = jnp.concatenate([expert_ids.astype(jnp.float32).T, gate_vals.T, prob_sums[None]], axis=0)
         packets = lax.all_gather(packet, ("dp", "ep"))
-        half_rows = tok_rows // 2
-        parts = [normed[:half_rows], normed[half_rows:], d_out[:half_rows], d_out[half_rows:]]
-        gathered = [lax.all_gather(parts[0], ("dp", "ep"), tiled=True)]
-        for part in parts[1:]:
-            late, _ = lax.optimization_barrier((part, gathered[-1][:8]))
-            gathered.append(lax.all_gather(late, ("dp", "ep"), tiled=True))
-        all_normed, all_d_out = gathered[:2], gathered[2:]
+        own_d_out, x_d_out = spread(d_out)
+        own_normed, x_normed = spread(normed)
 
         all_ids = packets[:, :top_k].astype(jnp.int32)
         counts = jnp.sum((all_ids[..., None] == jnp.arange(experts)).astype(jnp.float32), axis=(0, 1, 2))
@@ -552,31 +563,37 @@
         block_ids = by_block(turned[:, :top_k]).astype(jnp.int32) - first_expert
         block_ids = jnp.where((block_ids >= 0) & (block_ids < n_exp), block_ids, n_exp)
         block_gates = by_block(turned[:, top_k:2 * top_k])
-        plan, pos = make_plan(block_ids, dev_order, own_blocks, n_exp, max_tiles, max_own, core_at * n_exp)
-        plan["dev_blocks"] = dev_blocks
+        plan, pos = make_plan(block_ids, own_blocks, n_exp, max_tiles, max_own, core_at * n_exp)
+        plan.update(dev_blocks=dev_blocks, n_exp=n_exp)
         pos_t = pos[:own_blocks].transpose(0, 2, 1)
         gates_t = block_gates[:own_blocks].transpose(0, 2, 1)
 
         rows = max_tiles * TILE
-        x = dispatch(all_normed[0], pos, block_gates, plan, 0, None, rows, False)
-        x = dispatch(all_normed[1], pos, block_gates, plan, 1, x, rows, False)
-        d_rows = dispatch(all_d_out[0], pos, block_gates, plan, 0, None, rows, True)
-        d_rows = dispatch(all_d_out[1], pos, block_gates, plan, 1, d_rows, rows, True)
+        d_rows = dispatch(own_d_out, pos, block_gates, plan, 0, None, rows, True)
+        x = dispatch(own_normed, pos, block_gates, plan, 0, None, rows, False)
         hidden, d_act_gate, d_act_up, result, d_expert_in = own_tiles(x, d_rows, w_gate, w_up, w_down, plan)
+        d_rows, result = after(d_rows, result)
+        x_d_out, result = after(x_d_out, result)
+        x_normed, result = after(x_normed, result)
+        x_d_out = (*x_d_out, *(to_core(block) for block in x_d_out))
+        x_normed = (*x_normed, *(to_core(block) for block in x_normed))
         half, quarter = own_blocks // 2, own_blocks // 4
         d_away, d_far, d_near = combine(d_expert_in, pos_t, gates_t, None, plan, 0, (half, quarter, quarter), False)
         result, d_away = after(result, d_away)
         d_met = to_core(d_away)
-        away, d_gate_away = combine(result, pos_t, gates_t, all_d_out, plan, 0, (half,), True)
+        away, d_gate_away = combine(result, pos_t, gates_t, own_d_out[:2], plan, 0, (half,), True)
         result, (away, d_gate_away, d_far) = after(result, (away, d_gate_away, d_far + d_met[:tok_rows]))
         d_crossed = to_ep(d_far)
         met = to_core(away)
         d_gate_met = to_core(d_gate_away)
-        far, near, d_gate_mine = combine(result, pos_t, gates_t, all_d_out, plan, half, (quarter, quarter), True)
+        far, near, d_gate_mine = combine(result, pos_t, gates_t, own_d_out[2:], plan, half, (quarter, quarter), True)
         d_gate_mine = d_gate_mine + d_gate_met
         hidden, (far, d_gate_far) = after(hidden, (far + met[:tok_rows], d_gate_mine[:quarter]))
         crossed = to_ep(far)
         d_gate_crossed = to_ep(d_gate_far)
+        d_rows, hidden = after(d_rows, hidden)
+        d_rows = dispatch(x_d_out, pos, block_gates, plan, own_blocks, d_rows, rows, True)
+        x = dispatch(x_normed, pos, block_gates, plan, own_blocks, x, rows, False)
         grads, wholes = [None, None], None
         for part in range(2):
             *grads[part], all_gate, all_up, all_down = rest_tiles(x, d_rows, w_gate, w_up, w_down, hidden, d_act_gate, d_act_up, plan, part, wholes)

time: 1060 us -> 1130 us (1.066)
  blocking collectives: 21.9 us -> 139 us
  waiting for transfers between devices: 120 us -> 35.3 us
  Pallas kernels: 709 us -> 736 us
  starting transfers between devices: 79 us -> 105 us
  local copies, waits for them, and re-layouts: 29 us -> 12.3 us
    all_gather x1, blocking collectives: 21.9 us -> 139 us  [device_step(): packets = lax.all_gather(packet, ('dp', 'ep'))]
    all_gather x4 -> x0, waiting for transfers between devices: 107 us -> none  [the longest x3 94.9 us: device_step(): gathered.append(lax.all_gather(late, ('dp', 'ep'), tiled=True))]
    ppermute x9 -> x17, waiting for transfers between devices: 0.02 us -> 23.1 us  [to_core(): return lax.ppermute(away, 'dp', core_perm)]
    pallas_call x2, Pallas kernels: 211 us -> 231 us  [rest_tiles(): pl.pallas_call(functools.partial(rest_kernel, begun is not None), out_sha...]
    ppermute x3 -> x5, starting transfers between devices: 58.9 us -> 71.6 us  [to_ep(): return lax.ppermute(far, 'ep', ep_perm)]
    ppermute x9 -> x17, starting transfers between devices: 19.9 us -> 29.4 us  [to_core(): return lax.ppermute(away, 'dp', core_perm)]
  transfers between devices with their start and end apart: 17 -> 27, of which waited for: 5 -> 3; matrix products, arithmetic and copies ran while one was open for 7% -> 6% of each run, Pallas kernels for 46% -> 61%
where the time goes in v4:
time: 1130 us; the launch traced here: 1120 us
  Pallas kernels  736 us (65%)
  blocking collectives  139 us (12%)
  starting transfers between devices  105 us (9%)
  other arithmetic  64 us (6%)
  waiting for transfers between devices  35.3 us (3%)
  between operations  19 us (2%)
  local copies, waits for them, and re-layouts  12.3 us (1%)
    pallas_call x2, Pallas kernels, rest_tiles(): pl.pallas_call(functools.partial(rest_kernel, begun is not None), out_sha...  231 us
    pallas_call x3, Pallas kernels, combine(): pl.pallas_call(functools.partial(combine_kernel, weighted, first, counts,...  162 us
    pallas_call x4, Pallas kernels, dispatch(): pl.pallas_call(functools.partial(dispatch_kernel, scaled, begun, first, n...  155 us
    pallas_call x1, Pallas kernels, own_tiles(): pl.pallas_call(own_kernel, out_shape=[thin_shape] * 3 + [wide_shape] * 2,...  140 us
    all_gather x1, blocking collectives, device_step(): packets = lax.all_gather(packet, ('dp', 'ep'))  139 us
    ppermute x5, starting transfers between devices, to_ep(): return lax.ppermute(far, 'ep', ep_perm)  71.6 us
    pallas_call x6, Pallas kernels, merge(): pl.pallas_call(merge_kernel, out_shape=jax.ShapeDtypeStruct(whole.shape,...  48.8 us
    ppermute x17, starting transfers between devices, to_core(): return lax.ppermute(away, 'dp', core_perm)  29.4 us
  transfers between devices with their start and end apart: 27, of which 3 were waited for; matrix products, arithmetic and copies ran while one was open for 6% of the time, Pallas kernels for 61%

profile of v4, /device:TPU:0, one launch (start us, length us, event | category | flops | bytes accessed | tf_op | source)
XLA Modules:
  0.0 1117.5 jit_solution(4329193526413554954)
XLA Ops:
  11.1 4.3 fusion.2.rest_3_
  24.9 138.9 %all-gather.1 = f32[8,17,1024]{2,1,0:T(8,128)S(1)} all-gather(f32[1,17,1024]{2,1,0:T(8,128)S(1)} %maximum_bitcast_fusion), channel_id=2, replica_groups=mesh['ep'=2,'dp'=4] {'dp','ep'}, dimensions={0}, use_global_device_ids=true | all-gather | bytes 626688 | tf_op jit(solution)/shard_map/all_gather | solution.py:548
  183.6 39.7 %dispatch.2.x.rest_0_ = bf16[40960,1536]{1,0:T(8,128)(2,1)} custom-call(s32[32]{0:T(128)} %and_select_fusion.6.n_chunk.n_mix, s32[320]{0:T(512)} %copy-done.17, s32[320]{0:T(512)} %sub.230.seg_src, s32[320]{0:T(512)} %reshape.643.seg_dst, s32[20]{0:T(128)} %get-tuple-element.178.tail_at, s32[20]{0:T(128)} %get-tuple-element.177.tail_len, ...), custom_call_target="tpu_custom_call" | custom-call | flops 40000000000 | bytes 80000000 | tf_op jit(solution)/shard_map/dispatch/pallas_call | solution.py:127
  223.5 42.0 %dispatch_scaled.2.d_rows.rest_0_ = bf16[40960,1536]{1,0:T(8,128)(2,1)} custom-call(s32[32]{0:T(128)} %and_select_fusion.6.n_chunk.n_mix, s32[320]{0:T(512)} %copy-done.17, s32[320]{0:T(512)} %sub.230.seg_src, s32[320]{0:T(512)} %reshape.643.seg_dst, s32[20]{0:T(128)} %get-tuple-element.178.tail_at, s32[20]{0:T(128)} %get-tuple-element.177.tail_len, ...), custom_call_target="tpu_custom_call" | custom-call | flops 40000000000 | bytes 80000000 | tf_op jit(solution)/shard_map/dispatch_scaled/pallas_call | solution.py:127
  265.5 139.5 %own_tiles.1 = (bf16[20480,512]{1,0:T(8,128)(2,1)}, bf16[20480,512]{1,0:T(8,128)(2,1)}, bf16[20480,512]{1,0:T(8,128)(2,1)}, bf16[20480,1536]{1,0:T(8,128)(2,1)}, bf16[20480,1536]{1,0:T(8,128)(2,1)}) custom-call(s32[40]{0:T(128)} %get-tuple-element.182.tile_exp, s32[40]{0:T(128)} %get-tuple-element.180.tile_at, s32[40]{0:T(128)} %copy-done.35, ...), custom_call_target="tpu_custom_call" | custom-call | flops 120000004096 | bytes 250000000 | tf_op jit(solution)/shard_map/own_tiles/pallas_call | solution.py:352
  405.1 52.7 %combine.1 = (f32[2048,1536]{1,0:T(8,128)}, f32[1024,1536]{1,0:T(8,128)}, f32[1024,1536]{1,0:T(8,128)}) custom-call(s32[32]{0:T(128)} %and_select_fusion.6.n_chunk.n_mix, s32[320]{0:T(512)} %copy-done.17, s32[320]{0:T(512)} %sub.230.seg_src, s32[320]{0:T(512)} %get-tuple-element.128.seg_dst, bf16[20480,1536]{1,0:T(8,128)(2,1)} %get-tuple-element.55.rows, ...), custom_call_target="tpu_custom_call" | custom-call | flops 80000000000 | bytes 60000000 | tf_op jit(solution)/shard_map/combine/pallas_call | solution.py:246
  457.8 11.9 %collective-permute-start.10 = (f32[2048,1536]{1,0:T(8,128)}, f32[2048,1536]{1,0:T(8,128)}, u32[]{:S(2)}, u32[]{:S(2)}) collective-permute-start(f32[2048,1536]{1,0:T(8,128)} %get-tuple-element.61), channel_id=1, source_target_pairs={{0,1},{1,0},{2,3},{3,2},{4,5},{5,4},{6,7},{7,6}} | collective-permute-start | bytes 37748744 | tf_op jit(solution)/shard_map/ppermute | solution.py:496
  469.7 52.9 %combine_weighted.2 = (f32[2048,1536]{1,0:T(8,128)}, f32[8,256,8]{2,1,0:T(8,128)}) custom-call(s32[32]{0:T(128)} %and_select_fusion.6.n_chunk.n_mix, s32[320]{0:T(512)} %copy-done.17, s32[320]{0:T(512)} %sub.230.seg_src, s32[320]{0:T(512)} %get-tuple-element.128.seg_dst, bf16[20480,1536]{1,0:T(8,128)(2,1)} %get-tuple-element.62.rows, ...), custom_call_target="tpu_custom_call" | custom-call | flops 40000000000 | bytes 60000000 | tf_op jit(solution)/shard_map/combine_weighted/pallas_call | solution.py:246
  522.8 8.7 slice_add_fusion.3
  531.4 8.5 collective-permute-start.11
  545.0 18.4 %collective-permute-done.16.rest_3_ = bf16[1024,1536]{1,0:T(8,128)(2,1)S(1)} collective-permute-done((bf16[1024,1536]{1,0:T(8,128)(2,1)}, bf16[1024,1536]{1,0:T(8,128)(2,1)S(1)}, u32[]{:S(2)}, u32[]{:S(2)}) %collective-permute-start.16) | collective-permute-done | bytes 3145760 | tf_op jit(solution)/shard_map/ppermute | solution.py:496
  563.4 4.6 collective-permute-done.17.rest_4_
  568.1 35.2 %dispatch.3.x = bf16[40960,1536]{1,0:T(8,128)(2,1)} custom-call(s32[32]{0:T(128)} %and_select_fusion.6.n_chunk.n_mix, s32[320]{0:T(512)} %copy-done.17, s32[320]{0:T(512)} %sub.230.seg_src, s32[320]{0:T(512)} %reshape.643.seg_dst, s32[20]{0:T(128)} %get-tuple-element.178.tail_at, s32[20]{0:T(128)} %get-tuple-element.177.tail_len, ...), custom_call_target="tpu_custom_call", output_to_operand_aliasing={{}: (8, {})} | custom-call | flops 40000000000 | bytes 80000000 | tf_op jit(solution)/shard_map/dispatch/pallas_call | solution.py:127
  605.6 27.6 %collective-permute-start.14 = (f32[1024,1536]{1,0:T(8,128)}, f32[1024,1536]{1,0:T(8,128)}, u32[]{:S(2)}, u32[]{:S(2)}) collective-permute-start(f32[1024,1536]{1,0:T(8,128)} %slice_add_fusion.3), channel_id=1, source_target_pairs={{0,4},{4,0},{1,5},{5,1},{2,6},{6,2},{3,7},{7,3}} | collective-permute-start | bytes 18874376 | tf_op jit(solution)/shard_map/ppermute | solution.py:499
  633.3 56.0 %combine_weighted.3 = (f32[1024,1536]{1,0:T(8,128)}, f32[1024,1536]{1,0:T(8,128)}, f32[8,256,8]{2,1,0:T(8,128)}) custom-call(s32[32]{0:T(128)} %and_select_fusion.6.n_chunk.n_mix, s32[320]{0:T(512)} %copy-done.17, s32[320]{0:T(512)} %sub.230.seg_src, s32[320]{0:T(512)} %get-tuple-element.128.seg_dst, bf16[20480,1536]{1,0:T(8,128)(2,1)} %get-tuple-element.62.rows, ...), custom_call_target="tpu_custom_call" | custom-call | flops 40000000000 | bytes 60000000 | tf_op jit(solution)/shard_map/combine_weighted/pallas_call | solution.py:246
  692.8 8.6 slice_add_fusion.1
  701.4 5.9 collective-permute-start.13
  707.3 37.9 %dispatch_scaled.3.d_rows = bf16[40960,1536]{1,0:T(8,128)(2,1)} custom-call(s32[32]{0:T(128)} %and_select_fusion.6.n_chunk.n_mix, s32[320]{0:T(512)} %copy-done.17, s32[320]{0:T(512)} %sub.230.seg_src, s32[320]{0:T(512)} %reshape.643.seg_dst, s32[20]{0:T(128)} %get-tuple-element.178.tail_at, ...), custom_call_target="tpu_custom_call", output_to_operand_aliasing={{}: (8, {})} | custom-call | flops 40000000000 | bytes 80000000 | tf_op jit(solution)/shard_map/dispatch_scaled/pallas_call | solution.py:127
  745.2 125.0 %rest_tiles.2 = (bf16[5,1536,512]{2,1,0:T(8,128)(2,1)}, bf16[5,1536,512]{2,1,0:T(8,128)(2,1)}, bf16[5,512,1536]{2,1,0:T(8,128)(2,1)}, bf16[20,1536,512]{2,1,0:T(...) custom-call(s32[40]{0:T(128)} %copy-done.22, s32[40]{0:T(128)} %get-tuple-element.173.tile_at, ...), custom_call_target="tpu_custom_call" | custom-call | flops 80000000000 | bytes 150000000 | tf_op jit(solution)/shard_map/rest_tiles/pallas_call | solution.py:372
  870.7 106.0 %rest_tiles.3 = (bf16[5,1536,512]{2,1,0:T(8,128)(2,1)}, bf16[5,1536,512]{2,1,0:T(8,128)(2,1)}, bf16[5,512,1536]{2,1,0:T(8,128)(2,1)}, bf16[20,1536,512]{2,1,0:T(...) custom-call(s32[40]{0:T(128)} %copy-done.21, ...), custom_call_target="tpu_custom_call", output_to_operand_aliasing={{3}: (16, {}), {4}: (17, {}), {5}: (18, {})} | custom-call | flops 80000000000 | bytes 150000000 | tf_op jit(solution)/shard_map/rest_tiles/pallas_call | solution.py:372
  976.7 5.5 collective-permute-start.21
  982.2 34.7 %collective-permute-start.15 = (f32[4,256,8]{2,1,0:T(8,128)S(1)}, f32[4,256,8]{2,1,0:T(8,128)S(1)}, u32[]{:S(2)}, u32[]{:S(2)}) collective-permute-start(f32[4,256,8]{2,1,0:T(8,128)S(1)} %copy-done.10), channel_id=1, source_target_pairs={{0,4},{4,0},{1,5},{5,1},{2,6},{6,2},{3,7},{7,3}} | collective-permute-start | bytes 98312 | tf_op jit(solution)/shard_map/ppermute | solution.py:499
  1016.9 12.1 %collective-permute-done.15 = f32[4,256,8]{2,1,0:T(8,128)S(1)} collective-permute-done((f32[4,256,8]{2,1,0:T(8,128)S(1)}, f32[4,256,8]{2,1,0:T(8,128)S(1)}, u32[]{:S(2)}, u32[]{:S(2)}) %collective-permute-start.15) | collective-permute-done | bytes 32800 | tf_op jit(solution)/shard_map/ppermute | solution.py:499
  1034.8 3.4 fusion.53
  1039.3 7.6 fusion.9
  1047.0 11.7 %fusion.8 = (bf16[1024,1536]{1,0:T(8,128)(2,1)}, bf16[1024,1536]{1,0:T(8,128)(2,1)}) fusion(f32[1024,1536]{1,0:T(8,128)S(1)} %get-tuple-element.127, bf16[1024,1536]{1,0:T(8,128)(2,1)S(1)} %copy-done.1, bf16[1024,1536]{1,0:T(8,128)(2,1)} %rest_1_.1, f32[1024]{0:T(1024)S(1)} %broadcast_multiply_fusion, f32[1024]{0:T(1024)S(1)} %copy-done.18, ...), kind=kLoop, calls=%fused_computation.16 | loop fusion | flops 18874368 | bytes 37761024 | tf_op jit(solution)/shard_map/convert_element_type | solution.py:613
  1058.6 8.2 merge.6.whole_in
  1066.8 8.1 merge.8.whole_in
  1074.9 8.1 merge.7
  1083.1 8.1 merge.9
  1091.2 8.1 merge.10.whole_in
  1099.3 8.1 merge.11
  (215 shorter events, 50.3 us)
Async XLA Ops:
  7.2 1100.3 %all-reduce.3.cloned.1.call-start = ((), (), s32[]{:S(2)}) async-start(), calls=%async_computation | async-start | bytes 491520 | tf_op jit(solution)/shard_map/psum | solution.py:604
  15.5 157.2 %collective-permute-start.1 = (bf16[1024,1536]{1,0:T(8,128)(2,1)}, bf16[1024,1536]{1,0:T(8,128)(2,1)}, u32[]{:S(2)}, u32[]{:S(2)}) collective-permute-start(bf16[1024,1536]{1,0:T(8,128)(2,1)} %fusion.2.rest_3_), channel_id=1, source_target_pairs={{0,4},{4,0},{1,5},{5,1},{2,6},{6,2},{3,7},{7,3}} | collective-permute-start | bytes 9437192 | tf_op jit(solution)/shard_map/ppermute | solution.py:499
  18.8 162.7 %collective-permute-start.9 = (bf16[1024,1536]{1,0:T(8,128)(2,1)}, bf16[1024,1536]{1,0:T(8,128)(2,1)}, u32[]{:S(2)}, u32[]{:S(2)}) collective-permute-start(bf16[1024,1536]{1,0:T(8,128)(2,1)} %fusion.2.rest_3_), channel_id=1, source_target_pairs={{0,1},{1,0},{2,3},{3,2},{4,5},{5,4},{6,7},{7,6}} | collective-permute-start | bytes 9437192 | tf_op jit(solution)/shard_map/ppermute | solution.py:496
  18.8 163.2 %collective-permute-start.4 = (bf16[1024,1536]{1,0:T(8,128)(2,1)}, bf16[1024,1536]{1,0:T(8,128)(2,1)}, u32[]{:S(2)}, u32[]{:S(2)}) collective-permute-start(bf16[1024,1536]{1,0:T(8,128)(2,1)} %rest_1_.1), channel_id=1, source_target_pairs={{0,4},{4,0},{1,5},{5,1},{2,6},{6,2},{3,7},{7,3}} | collective-permute-start | bytes 9437192 | tf_op jit(solution)/shard_map/ppermute | solution.py:499
  18.9 204.5 %collective-permute-start.7 = (bf16[1024,1536]{1,0:T(8,128)(2,1)}, bf16[1024,1536]{1,0:T(8,128)(2,1)}, u32[]{:S(2)}, u32[]{:S(2)}) collective-permute-start(bf16[1024,1536]{1,0:T(8,128)(2,1)} %rest_1_.1), channel_id=1, source_target_pairs={{0,1},{1,0},{2,3},{3,2},{4,5},{5,4},{6,7},{7,6}} | collective-permute-start | bytes 9437192 | tf_op jit(solution)/shard_map/ppermute | solution.py:496
  19.3 385.7 %collective-permute-start = (bf16[1024,1536]{1,0:T(8,128)(2,1)}, bf16[1024,1536]{1,0:T(8,128)(2,1)}, u32[]{:S(2)}, u32[]{:S(2)}) collective-permute-start(bf16[1024,1536]{1,0:T(8,128)(2,1)} %fusion.2.rest_3_), channel_id=1, source_target_pairs={{0,2},{1,3},{2,0},{3,1},{4,6},{5,7},{6,4},{7,5}} | collective-permute-start | bytes 9437192 | tf_op jit(solution)/shard_map/ppermute | solution.py:502
  172.7 10.9 collective-permute-start.8
  178.3 45.0 %copy-start.35 = (s32[40]{0:T(128)}, s32[40]{0:T(128)S(1)}, u32[]{:S(2)}) copy-start(s32[40]{0:T(128)S(1)} %iota_minimum_fusion.2.own_at) | copy-start | bytes 484
  181.6 223.5 %collective-permute-start.3 = (bf16[1024,1536]{1,0:T(8,128)(2,1)}, bf16[1024,1536]{1,0:T(8,128)(2,1)}, u32[]{:S(2)}, u32[]{:S(2)}) collective-permute-start(bf16[1024,1536]{1,0:T(8,128)(2,1)} %rest_1_.1), channel_id=1, source_target_pairs={{0,2},{1,3},{2,0},{3,1},{4,6},{5,7},{6,4},{7,5}} | collective-permute-start | bytes 9437192 | tf_op jit(solution)/shard_map/ppermute | solution.py:502
  182.0 223.1 %collective-permute-start.2 = (bf16[1024,1536]{1,0:T(8,128)(2,1)}, bf16[1024,1536]{1,0:T(8,128)(2,1)}, u32[]{:S(2)}, u32[]{:S(2)}) collective-permute-start(bf16[1024,1536]{1,0:T(8,128)(2,1)} %collective-permute-done.1.rest_2_), channel_id=1, source_target_pairs={{0,2},{1,3},{2,0},{3,1},{4,6},{5,7},{6,4},{7,5}} | collective-permute-start | bytes 9437192 | tf_op jit(solution)/shard_map/ppermute | solution.py:502
  183.6 39.8 %collective-permute-start.6 = (bf16[1024,1536]{1,0:T(8,128)(2,1)}, bf16[1024,1536]{1,0:T(8,128)(2,1)}, u32[]{:S(2)}, u32[]{:S(2)}) collective-permute-start(bf16[1024,1536]{1,0:T(8,128)(2,1)} %collective-permute-done.4.rest_2_.rest_0_), channel_id=1, source_target_pairs={{0,1},{1,0},{2,3},{3,2},{4,5},{5,4},{6,7},{7,6}} | collective-permute-start | bytes 9437192 | tf_op jit(solution)/shard_map/ppermute | solution.py:496
  223.4 181.6 %collective-permute-start.5 = (bf16[1024,1536]{1,0:T(8,128)(2,1)}, bf16[1024,1536]{1,0:T(8,128)(2,1)}, u32[]{:S(2)}, u32[]{:S(2)}) collective-permute-start(bf16[1024,1536]{1,0:T(8,128)(2,1)} %collective-permute-done.4.rest_2_.rest_0_), channel_id=1, source_target_pairs={{0,2},{1,3},{2,0},{3,1},{4,6},{5,7},{6,4},{7,5}} | collective-permute-start | bytes 9437192 | tf_op jit(solution)/shard_map/ppermute | solution.py:502
  457.8 64.8 %collective-permute-start.10 = (f32[2048,1536]{1,0:T(8,128)}, f32[2048,1536]{1,0:T(8,128)}, u32[]{:S(2)}, u32[]{:S(2)}) collective-permute-start(f32[2048,1536]{1,0:T(8,128)} %get-tuple-element.61), channel_id=1, source_target_pairs={{0,1},{1,0},{2,3},{3,2},{4,5},{5,4},{6,7},{7,6}} | collective-permute-start | bytes 37748744 | tf_op jit(solution)/shard_map/ppermute | solution.py:496
  531.4 161.4 %collective-permute-start.11 = (f32[2048,1536]{1,0:T(8,128)}, f32[2048,1536]{1,0:T(8,128)}, u32[]{:S(2)}, u32[]{:S(2)}) collective-permute-start(f32[2048,1536]{1,0:T(8,128)} %get-tuple-element.64), channel_id=1, source_target_pairs={{0,1},{1,0},{2,3},{3,2},{4,5},{5,4},{6,7},{7,6}} | collective-permute-start | bytes 37748744 | tf_op jit(solution)/shard_map/ppermute | solution.py:496
  539.9 23.5 %collective-permute-start.16 = (bf16[1024,1536]{1,0:T(8,128)(2,1)}, bf16[1024,1536]{1,0:T(8,128)(2,1)S(1)}, u32[]{:S(2)}, u32[]{:S(2)}) collective-permute-start(bf16[1024,1536]{1,0:T(8,128)(2,1)} %collective-permute-done.rest_1_), channel_id=1, source_target_pairs={{0,1},{1,0},{2,3},{3,2},{4,5},{5,4},{6,7},{7,6}} | collective-permute-start | bytes 9437192 | tf_op jit(solution)/shard_map/ppermute | solution.py:496
  539.9 28.1 %collective-permute-start.17 = (bf16[1024,1536]{1,0:T(8,128)(2,1)}, bf16[1024,1536]{1,0:T(8,128)(2,1)}, u32[]{:S(2)}, u32[]{:S(2)}) collective-permute-start(bf16[1024,1536]{1,0:T(8,128)(2,1)} %collective-permute-done.2.rest_2_), channel_id=1, source_target_pairs={{0,1},{1,0},{2,3},{3,2},{4,5},{5,4},{6,7},{7,6}} | collective-permute-start | bytes 9437192 | tf_op jit(solution)/shard_map/ppermute | solution.py:496
  544.5 162.8 %collective-permute-start.18 = (bf16[1024,1536]{1,0:T(8,128)(2,1)}, bf16[1024,1536]{1,0:T(8,128)(2,1)}, u32[]{:S(2)}, u32[]{:S(2)}) collective-permute-start(bf16[1024,1536]{1,0:T(8,128)(2,1)} %collective-permute-done.3.rest_1_), channel_id=1, source_target_pairs={{0,1},{1,0},{2,3},{3,2},{4,5},{5,4},{6,7},{7,6}} | collective-permute-start | bytes 9437192 | tf_op jit(solution)/shard_map/ppermute | solution.py:496
  544.5 162.8 %collective-permute-start.19 = (bf16[1024,1536]{1,0:T(8,128)(2,1)}, bf16[1024,1536]{1,0:T(8,128)(2,1)}, u32[]{:S(2)}, u32[]{:S(2)}) collective-permute-start(bf16[1024,1536]{1,0:T(8,128)(2,1)} %collective-permute-done.5.rest_2_), channel_id=1, source_target_pairs={{0,1},{1,0},{2,3},{3,2},{4,5},{5,4},{6,7},{7,6}} | collective-permute-start | bytes 9437192 | tf_op jit(solution)/shard_map/ppermute | solution.py:496
  604.8 84.5 %collective-permute-start.12 = (f32[8,256,8]{1,2,0:T(8,128)S(1)}, f32[8,256,8]{1,2,0:T(8,128)S(1)}, u32[]{:S(2)}, u32[]{:S(2)}) collective-permute-start(f32[8,256,8]{1,2,0:T(8,128)S(1)} %copy.68), channel_id=1, source_target_pairs={{0,1},{1,0},{2,3},{3,2},{4,5},{5,4},{6,7},{7,6}} | collective-permute-start | bytes 196616 | tf_op jit(solution)/shard_map/ppermute | solution.py:496
  605.6 376.5 %collective-permute-start.14 = (f32[1024,1536]{1,0:T(8,128)}, f32[1024,1536]{1,0:T(8,128)}, u32[]{:S(2)}, u32[]{:S(2)}) collective-permute-start(f32[1024,1536]{1,0:T(8,128)} %slice_add_fusion.3), channel_id=1, source_target_pairs={{0,4},{4,0},{1,5},{5,1},{2,6},{6,2},{3,7},{7,3}} | collective-permute-start | bytes 18874376 | tf_op jit(solution)/shard_map/ppermute | solution.py:499
  701.4 331.0 %collective-permute-start.13 = (f32[1024,1536]{1,0:T(8,128)}, f32[1024,1536]{1,0:T(8,128)}, u32[]{:S(2)}, u32[]{:S(2)}) collective-permute-start(f32[1024,1536]{1,0:T(8,128)} %slice_add_fusion.1), channel_id=1, source_target_pairs={{0,4},{4,0},{1,5},{5,1},{2,6},{6,2},{3,7},{7,3}} | collective-permute-start | bytes 18874376 | tf_op jit(solution)/shard_map/ppermute | solution.py:499
  870.2 164.5 %collective-permute-start.20 = (bf16[5,1536,512]{2,1,0:T(8,128)(2,1)}, bf16[5,1536,512]{2,1,0:T(8,128)(2,1)}, u32[]{:S(2)}, u32[]{:S(2)}) collective-permute-start(bf16[5,1536,512]{2,1,0:T(8,128)(2,1)} %get-tuple-element.87), channel_id=1, source_target_pairs={{0,1},{1,0},{2,3},{3,2},{4,5},{5,4},{6,7},{7,6}} | collective-permute-start | bytes 23592968 | tf_op jit(solution)/shard_map/ppermute | solution.py:496
  870.2 196.6 %collective-permute-start.22 = (bf16[5,1536,512]{2,1,0:T(8,128)(2,1)}, bf16[5,1536,512]{2,1,0:T(8,128)(2,1)}, u32[]{:S(2)}, u32[]{:S(2)}) collective-permute-start(bf16[5,1536,512]{2,1,0:T(8,128)(2,1)} %get-tuple-element.90), channel_id=1, source_target_pairs={{0,1},{1,0},{2,3},{3,2},{4,5},{5,4},{6,7},{7,6}} | collective-permute-start | bytes 23592968 | tf_op jit(solution)/shard_map/ppermute | solution.py:496
  870.7 111.4 %copy-start.10 = (f32[4,256,8]{2,1,0:T(8,128)S(1)}, f32[4,256,8]{2,1,0:T(8,128)}, u32[]{:S(2)}) copy-start(f32[4,256,8]{2,1,0:T(8,128)} %slice.121) | copy-start | bytes 98308
  870.7 163.5 %copy-start.4 = (f32[8,256,8]{2,1,0:T(8,128)S(1)}, f32[8,256,8]{2,1,0:T(8,128)}, u32[]{:S(2)}) copy-start(f32[8,256,8]{2,1,0:T(8,128)} %copy-done.3) | copy-start | bytes 196612
  870.7 163.7 %copy-start.12 = (s32[1024,8]{0,1:T(8,128)S(1)}, s32[1024,8]{0,1:T(8,128)}, u32[]{:S(2)}) copy-start(s32[1024,8]{0,1:T(8,128)} %param.10) | copy-start | bytes 98308
  870.7 163.8 %copy-start.9 = (f32[1024,40]{0,1:T(8,128)S(1)}, f32[1024,40]{0,1:T(8,128)}, u32[]{:S(2)}) copy-start(f32[1024,40]{0,1:T(8,128)} %copy-done.8) | copy-start | bytes 491524
  976.7 98.3 %collective-permute-start.21 = (bf16[5,1536,512]{2,1,0:T(8,128)(2,1)}, bf16[5,1536,512]{2,1,0:T(8,128)(2,1)}, u32[]{:S(2)}, u32[]{:S(2)}) collective-permute-start(bf16[5,1536,512]{2,1,0:T(8,128)(2,1)} %get-tuple-element.88), channel_id=1, source_target_pairs={{0,1},{1,0},{2,3},{3,2},{4,5},{5,4},{6,7},{7,6}} | collective-permute-start | bytes 23592968 | tf_op jit(solution)/shard_map/ppermute | solution.py:496
  982.2 46.9 %collective-permute-start.15 = (f32[4,256,8]{2,1,0:T(8,128)S(1)}, f32[4,256,8]{2,1,0:T(8,128)S(1)}, u32[]{:S(2)}, u32[]{:S(2)}) collective-permute-start(f32[4,256,8]{2,1,0:T(8,128)S(1)} %copy-done.10), channel_id=1, source_target_pairs={{0,4},{4,0},{1,5},{5,1},{2,6},{6,2},{3,7},{7,3}} | collective-permute-start | bytes 98312 | tf_op jit(solution)/shard_map/ppermute | solution.py:499
  1029.0 54.1 %collective-permute-start.23 = (bf16[5,1536,512]{2,1,0:T(8,128)(2,1)}, bf16[5,1536,512]{2,1,0:T(8,128)(2,1)}, u32[]{:S(2)}, u32[]{:S(2)}) collective-permute-start(bf16[5,1536,512]{2,1,0:T(8,128)(2,1)} %get-tuple-element.91), channel_id=1, source_target_pairs={{0,1},{1,0},{2,3},{3,2},{4,5},{5,4},{6,7},{7,6}} | collective-permute-start | bytes 23592968 | tf_op jit(solution)/shard_map/ppermute | solution.py:496
  1032.4 58.8 %collective-permute-start.24 = (bf16[5,512,1536]{2,1,0:T(8,128)(2,1)}, bf16[5,512,1536]{2,1,0:T(8,128)(2,1)}, u32[]{:S(2)}, u32[]{:S(2)}) collective-permute-start(bf16[5,512,1536]{2,1,0:T(8,128)(2,1)} %get-tuple-element.93), channel_id=1, source_target_pairs={{0,1},{1,0},{2,3},{3,2},{4,5},{5,4},{6,7},{7,6}} | collective-permute-start | bytes 23592968 | tf_op jit(solution)/shard_map/ppermute | solution.py:496
  1034.7 64.7 %collective-permute-start.25 = (bf16[5,512,1536]{2,1,0:T(8,128)(2,1)}, bf16[5,512,1536]{2,1,0:T(8,128)(2,1)}, u32[]{:S(2)}, u32[]{:S(2)}) collective-permute-start(bf16[5,512,1536]{2,1,0:T(8,128)(2,1)} %get-tuple-element.94), channel_id=1, source_target_pairs={{0,1},{1,0},{2,3},{3,2},{4,5},{5,4},{6,7},{7,6}} | collective-permute-start | bytes 23592968 | tf_op jit(solution)/shard_map/ppermute | solution.py:496
  (31 other events, 465.3 us)
Sparse Core Ops, SparseCore 0:
  1038.4 44.8 all-reduce.2

commit v5 on v4

--- a/solution.py
+++ b/solution.py
@@ -1,4 +1,5 @@
 import functools
+from typing import Any, NamedTuple
 
 import jax
 import jax.numpy as jnp
@@ -36,24 +37,48 @@
     return lax.dot_general(left, right, dims, preferred_element_type=jnp.float32)
 
 
-def dispatch_kernel(scaled, begun, first, n_exp, n_chunk, seg_len, seg_src, seg_dst, tail_at, tail_len, pos, gates, *rest):
+def sized_copies(groups, copy):
+    fours = lax.div(groups, 4)
+
+    @pl.loop(0, fours)
+    def _(i):
+        copy(4 * i, 4)
+
+    left = groups - 4 * fours
+
+    @pl.when(left >= 2)
+    def _():
+        copy(4 * fours, 2)
+
+    @pl.when(lax.rem(left, 2) == 1)
+    def _():
+        copy(groups - 1, 1)
+
+
+def dispatch_kernel(scaled, begun, first, n_exp, n_chunk, n_group, seg_len, seg_src, seg_dst, tail_at, tail_len, pos, gates, *rest):
     *srcs, out, stack, blank, src, sems, src_sems, tail_sem = rest[1:] if begun else rest
     step = pl.program_id(0)
     src_blocks = srcs[0].shape[0] // BLOCK
     last = pl.num_programs(0) - 1
     slot = lax.rem(step, 2)
 
-    def segment_copy(blk, buf, exp, grp):
-        at = blk * n_exp + exp
-        from_row = pl.multiple_of((seg_src[at] + grp) * GROUP, GROUP)
-        to_row = pl.multiple_of((seg_dst[at] + grp) * GROUP, GROUP)
-        return pltpu.make_async_copy(stack.at[buf, pl.ds(from_row, GROUP), :], out.at[pl.ds(to_row, GROUP), :], sems.at[buf])
-
-    def each_segment(blk, buf, act):
-        for exp in range(n_exp):
-            @pl.loop(0, seg_len[blk * n_exp + exp])
-            def _(grp):
-                act(segment_copy(blk, buf, exp, grp))
+    def send_segments(blk, buf):
+        @pl.loop(0, n_exp)
+        def _(exp):
+            at = blk * n_exp + exp
+
+            def send(grp, count):
+                from_row = pl.multiple_of((seg_src[at] + grp) * GROUP, GROUP)
+                to_row = pl.multiple_of((seg_dst[at] + grp) * GROUP, GROUP)
+                pltpu.make_async_copy(stack.at[buf, pl.ds(from_row, count * GROUP), :], out.at[pl.ds(to_row, count * GROUP), :], sems.at[buf]).start()
+
+            sized_copies(seg_len[at], send)
+
+    def await_segments(blk, buf):
+        def wait(grp, count):
+            pltpu.make_async_copy(stack.at[buf, pl.ds(0, count * GROUP), :], out.at[pl.ds(0, count * GROUP), :], sems.at[buf]).wait()
+
+        sized_copies(n_group[blk], wait)
 
     def each_tail(act):
         @pl.loop(0, 2 * n_exp)
@@ -89,7 +114,7 @@
 
     @pl.when(step >= 2)
     def _():
-        each_segment(first + step - 2, slot, lambda copy: copy.wait())
+        await_segments(first + step - 2, slot)
 
     @pl.loop(0, n_chunk[first + step])
     def _(chunk):
@@ -107,12 +132,12 @@
             picked = picked * jnp.sum(weight, axis=1, keepdims=True)
         stack[slot, pl.ds(pl.multiple_of(chunk * CHUNK, CHUNK), CHUNK), :] = picked.astype(jnp.bfloat16)
 
-    each_segment(first + step, slot, lambda copy: copy.start())
+    send_segments(first + step, slot)
 
     @pl.when(step == last)
     def _():
-        each_segment(first + step - 1, 1 - slot, lambda copy: copy.wait())
-        each_segment(first + step, slot, lambda copy: copy.wait())
+        await_segments(first + step - 1, 1 - slot)
+        await_segments(first + step, slot)
         if not begun:
             each_tail(lambda copy: copy.wait())
 
@@ -121,14 +146,14 @@
     top_k = pos.shape[1]
     begun = out is not None
     width = srcs[0].shape[1]
-    n_exp = plan["n_exp"]
+    n_exp = plan.n_exp
     stack_rows = -(-(BLOCK * top_k + n_exp * (GROUP - 1)) // CHUNK) * CHUNK
     any_spec = pl.BlockSpec(memory_space=pl.ANY)
     return pl.pallas_call(
         functools.partial(dispatch_kernel, scaled, begun, first, n_exp),
         out_shape=jax.ShapeDtypeStruct((rows, width), jnp.bfloat16),
         grid_spec=pltpu.PrefetchScalarGridSpec(
-            num_scalar_prefetch=6,
+            num_scalar_prefetch=7,
             grid=(sum(src.shape[0] for src in srcs) // BLOCK,),
             in_specs=[
                 pl.BlockSpec((1, top_k, BLOCK), lambda i, *_: (first + i, 0, 0)),
@@ -146,13 +171,13 @@
             ],
         ),
         compiler_params=pltpu.CompilerParams(dimension_semantics=("arbitrary",), vmem_limit_bytes=VMEM_LIMIT),
-        input_output_aliases={8: 0} if begun else {},
+        input_output_aliases={9: 0} if begun else {},
         cost_estimate=pl.CostEstimate(flops=40_000_000_000, bytes_accessed=80_000_000, transcendentals=0),
         name="dispatch_scaled" if scaled else "dispatch",
-    )(plan["n_chunk"], plan["seg_len"], plan["seg_src"], plan["seg_dst"], plan["tail_at"], plan["tail_len"], pos, gates, *([out] * begun), *srcs)
-
-
-def combine_kernel(weighted, first, counts, dev_blocks, n_exp, n_mix, seg_len, seg_src, seg_dst, rows, pos, gates, *rest):
+    )(plan.n_chunk, plan.n_group, plan.seg_len, plan.seg_src, plan.seg_dst, plan.tail_at, plan.tail_len, pos, gates, *([out] * begun), *srcs)
+
+
+def combine_kernel(weighted, first, counts, dev_blocks, n_exp, n_mix, n_group, seg_len, seg_src, seg_dst, rows, pos, gates, *rest):
     if weighted:
         d_out0, d_out1, *outs, d_gates, stack, total, sems = rest
     else:
@@ -161,14 +186,23 @@
     blocks = pl.num_programs(0)
     slot = lax.rem(step, 2)
 
-    def each_segment(blk, buf, act):
-        for exp in range(n_exp):
-            @pl.loop(0, seg_len[blk * n_exp + exp])
-            def _(grp):
-                at = blk * n_exp + exp
+    def fetch_segments(blk, buf):
+        @pl.loop(0, n_exp)
+        def _(exp):
+            at = blk * n_exp + exp
+
+            def fetch(grp, count):
                 to_row = pl.multiple_of((seg_src[at] + grp) * GROUP, GROUP)
                 from_row = pl.multiple_of((seg_dst[at] + grp) * GROUP, GROUP)
-                act(pltpu.make_async_copy(rows.at[pl.ds(from_row, GROUP), :], stack.at[buf, pl.ds(to_row, GROUP), :], sems.at[buf]))
+                pltpu.make_async_copy(rows.at[pl.ds(from_row, count * GROUP), :], stack.at[buf, pl.ds(to_row, count * GROUP), :], sems.at[buf]).start()
+
+            sized_copies(seg_len[at], fetch)
+
+    def await_segments(blk, buf):
+        def wait(grp, count):
+            pltpu.make_async_copy(rows.at[pl.ds(0, count * GROUP), :], stack.at[buf, pl.ds(0, count * GROUP), :], sems.at[buf]).wait()
+
+        sized_copies(n_group[blk], wait)
 
     @pl.when(step == 0)
     def _():
@@ -176,13 +210,13 @@
         def _(part):
             stack[:, pl.ds(pl.multiple_of(part * MIX, MIX), MIX), :] = jnp.zeros((2, MIX, stack.shape[2]), stack.dtype)
 
-        each_segment(first, 0, lambda copy: copy.start())
+        fetch_segments(first, 0)
 
     @pl.when(step < blocks - 1)
     def _():
-        each_segment(first + step + 1, 1 - slot, lambda copy: copy.start())
-
-    each_segment(first + step, slot, lambda copy: copy.wait())
+        fetch_segments(first + step + 1, 1 - slot)
+
+    await_segments(first + step, slot)
     total[...] = jnp.zeros_like(total)
     if weighted:
         d_gates[...] = jnp.zeros_like(d_gates)
@@ -226,9 +260,9 @@
 def combine(rows, pos_t, gates_t, d_outs, plan, first, counts, weighted):
     _, _, top_k = pos_t.shape
     width = rows.shape[1]
-    n_exp = plan["n_exp"]
+    n_exp = plan.n_exp
     blocks = sum(counts)
-    dev_blocks = plan["dev_blocks"]
+    dev_blocks = plan.dev_blocks
     stack_rows = -(-(BLOCK * top_k + n_exp * (GROUP - 1)) // MIX) * MIX
     out_shape, out_specs, begin = [], [], 0
     for count in counts:
@@ -247,7 +281,7 @@
         functools.partial(combine_kernel, weighted, first, counts, dev_blocks, n_exp),
         out_shape=out_shape,
         grid_spec=pltpu.PrefetchScalarGridSpec(
-            num_scalar_prefetch=4,
+            num_scalar_prefetch=5,
             grid=(blocks,),
             in_specs=[
                 pl.BlockSpec(memory_space=pl.ANY),
@@ -265,7 +299,7 @@
         compiler_params=pltpu.CompilerParams(dimension_semantics=("arbitrary",), vmem_limit_bytes=VMEM_LIMIT),
         cost_estimate=pl.CostEstimate(flops=5_000_000_000 * blocks, bytes_accessed=60_000_000, transcendentals=0),
         name="combine_weighted" if weighted else "combine",
-    )(plan["n_mix"], plan["seg_len"], plan["seg_src"], plan["seg_own"], rows, pos_t, gates_t, *(d_outs if weighted else ()))
+    )(plan.n_mix, plan.n_group, plan.seg_len, plan.seg_src, plan.seg_own, rows, pos_t, gates_t, *(d_outs if weighted else ()))
 
 
 def by_kind(kind, body):
@@ -345,7 +379,7 @@
     wide_own = pl.BlockSpec((TILE, width), lambda t, exp, at, own, *_: (own[t], 0))
     w_in = pl.BlockSpec((1, width, mid), lambda t, exp, *_: (exp[t], 0, 0))
     w_out = pl.BlockSpec((1, mid, width), lambda t, exp, *_: (exp[t], 0, 0))
-    seq = plan["own_seq"]
+    seq = plan.own_seq
     own_rows = seq[0].shape[0] * TILE
     thin_shape = jax.ShapeDtypeStruct((own_rows, mid), jnp.bfloat16)
     wide_shape = jax.ShapeDtypeStruct((own_rows, width), jnp.bfloat16)
@@ -361,8 +395,8 @@
 
 def rest_tiles(x, d_rows, w_gate, w_up, w_down, hidden, d_gate, d_up, plan, half, begun):
     width, mid = w_gate.shape[1:]
-    n_half = plan["n_exp"] // 2
-    seq = plan["rest_seq"][half]
+    n_half = plan.n_exp // 2
+    seq = plan.rest_seq[half]
     shapes = [(width, mid), (width, mid), (mid, width)]
     wide = pl.BlockSpec((TILE, width), lambda t, exp, at, *_: (at[t], 0))
     kept = pl.BlockSpec((TILE, mid), lambda t, exp, at, own, *_: (own[t], 0))
@@ -384,7 +418,7 @@
         compiler_params=kernel_params(),
         cost_estimate=pl.CostEstimate(flops=80_000_000_000, bytes_accessed=150_000_000, transcendentals=0),
         name="rest_tiles",
-    )(*seq, plan["base"], x, d_rows, w_gate, w_up, w_down, hidden, d_gate, d_up, *(begun or ()))
+    )(*seq, plan.base, x, d_rows, w_gate, w_up, w_down, hidden, d_gate, d_up, *(begun or ()))
 
 
 def merge_kernel(base, whole_in, other, whole):
@@ -407,6 +441,23 @@
         cost_estimate=pl.CostEstimate(flops=8_000_000_000, bytes_accessed=30_000_000, transcendentals=0),
         name="merge",
     )(other_base, whole, other)
+
+
+class Plan(NamedTuple):
+    n_chunk: Any
+    n_group: Any
+    n_mix: Any
+    seg_len: Any
+    seg_src: Any
+    seg_dst: Any
+    seg_own: Any
+    tail_at: Any
+    tail_len: Any
+    base: Any
+    own_seq: Any
+    rest_seq: Any
+    dev_blocks: int = 0
+    n_exp: int = 0
 
 
 def exclusive(values, axis=0):
@@ -465,20 +516,21 @@
         return seq
 
     stack_rows = jnp.sum(seg_len, axis=1) * GROUP
-    plan = {
-        "n_chunk": (stack_rows + CHUNK - 1) // CHUNK,
-        "n_mix": (stack_rows + MIX - 1) // MIX,
-        "seg_len": seg_len.reshape(-1),
-        "seg_src": seg_src.reshape(-1),
-        "seg_dst": seg_dst.reshape(-1),
-        "seg_own": (own_base[None, :] * per_tile + exclusive(seg_len, 0)).reshape(-1),
-        "tail_at": (begins + groups).reshape(-1),
-        "tail_len": ((groups + per_half - 1) // per_half * per_half - groups).reshape(-1),
-        "base": weight_base.reshape(1),
-        "own_seq": (o_exp + weight_base, o_pick(tile_base) + o_nth, o_pick(own_base) + o_nth, kind_of(o_pick(groups[0]) - o_nth * per_tile, o_past)),
-        "rest_seq": (rest_seq(0), rest_seq(1)),
-    }
-    return jax.tree.map(lambda value: value.astype(jnp.int32), plan), pos
+    plan = Plan(
+        n_chunk=(stack_rows + CHUNK - 1) // CHUNK,
+        n_group=jnp.sum(seg_len, axis=1),
+        n_mix=(stack_rows + MIX - 1) // MIX,
+        seg_len=seg_len.reshape(-1),
+        seg_src=seg_src.reshape(-1),
+        seg_dst=seg_dst.reshape(-1),
+        seg_own=(own_base[None, :] * per_tile + exclusive(seg_len, 0)).reshape(-1),
+        tail_at=(begins + groups).reshape(-1),
+        tail_len=((groups + per_half - 1) // per_half * per_half - groups).reshape(-1),
+        base=weight_base.reshape(1),
+        own_seq=(o_exp + weight_base, o_pick(tile_base) + o_nth, o_pick(own_base) + o_nth, kind_of(o_pick(groups[0]) - o_nth * per_tile, o_past)),
+        rest_seq=(rest_seq(0), rest_seq(1)),
+    )
+    return jax.tree.map(lambda value: jnp.asarray(value, jnp.int32), plan), pos
 
 
 def solution(mesh):
@@ -543,31 +595,33 @@
         expert_hits = expert_ids[:, :, None] == jnp.arange(experts)[None, None, :]
         gate_vals = jnp.sum(jnp.where(expert_hits, router_probs[:, None, :], 0.0), axis=2)
 
-        prob_sums = jnp.pad(jnp.sum(router_probs, axis=0), (0, tok_rows - experts))
-        packet = jnp.concatenate([expert_ids.astype(jnp.float32).T, gate_vals.T, prob_sums[None]], axis=0)
-        packets = lax.all_gather(packet, ("dp", "ep"))
-        own_d_out, x_d_out = spread(d_out)
-        own_normed, x_normed = spread(normed)
-
-        all_ids = packets[:, :top_k].astype(jnp.int32)
+        id_packets = lax.all_gather(expert_ids.astype(jnp.float32).T, ("dp", "ep"))
+        d_out_late, id_packets = after(d_out, id_packets)
+        own_d_out, x_d_out = spread(d_out_late)
+        all_ids = id_packets.astype(jnp.int32)
         counts = jnp.sum((all_ids[..., None] == jnp.arange(experts)).astype(jnp.float32), axis=(0, 1, 2))
         expert_frac = counts / (total_tok * top_k)
-        aux_loss = AUX_COEF * experts * jnp.sum(expert_frac * jnp.sum(packets[:, 2 * top_k, :experts], axis=0)) / total_tok
-
-        turned = jnp.take(packets, dev_order, axis=0)
+
 
         def by_block(rows):
             return rows.reshape(devices, top_k, dev_blocks, BLOCK).transpose(0, 2, 1, 3).reshape(devices * dev_blocks, top_k, BLOCK)
 
         first_expert = ep_at * local_experts + core_at * n_exp
-        block_ids = by_block(turned[:, :top_k]).astype(jnp.int32) - first_expert
+        block_ids = by_block(jnp.take(id_packets, dev_order, axis=0)).astype(jnp.int32) - first_expert
         block_ids = jnp.where((block_ids >= 0) & (block_ids < n_exp), block_ids, n_exp)
-        block_gates = by_block(turned[:, top_k:2 * top_k])
         plan, pos = make_plan(block_ids, own_blocks, n_exp, max_tiles, max_own, core_at * n_exp)
-        plan.update(dev_blocks=dev_blocks, n_exp=n_exp)
+        plan = plan._replace(dev_blocks=dev_blocks, n_exp=n_exp)
+        prob_sums = jnp.pad(jnp.sum(router_probs, axis=0), (0, tok_rows - experts))
+        packet, (pos, tail_at) = after(jnp.concatenate([gate_vals.T, prob_sums[None]], axis=0), (pos, plan.tail_at))
+        plan = plan._replace(tail_at=tail_at)
+        packets = lax.all_gather(packet, ("dp", "ep"))
+        normed_late, packets = after(normed, packets)
+        own_normed, x_normed = spread(normed_late)
+        block_gates = by_block(jnp.take(packets, dev_order, axis=0)[:, :top_k])
         pos_t = pos[:own_blocks].transpose(0, 2, 1)
         gates_t = block_gates[:own_blocks].transpose(0, 2, 1)
 
+        aux_loss = AUX_COEF * experts * jnp.sum(expert_frac * jnp.sum(packets[:, top_k, :experts], axis=0)) / total_tok
         rows = max_tiles * TILE
         d_rows = dispatch(own_d_out, pos, block_gates, plan, 0, None, rows, True)
         x = dispatch(own_normed, pos, block_gates, plan, 0, None, rows, False)

time: 1130 us -> 1100 us (0.973)
  waiting for transfers between devices: 35.3 us -> 154 us
  blocking collectives: 139 us -> 27.3 us
  Pallas kernels: 736 us -> 711 us
  starting transfers between devices: 105 us -> 91.5 us
    all_gather x1, blocking collectives: 139 us -> 12.8 us  [device_step(): packets = lax.all_gather(packet, ('dp', 'ep'))]
    ppermute x5, waiting for transfers between devices: 12.1 us -> 131 us  [to_ep(): return lax.ppermute(far, 'ep', ep_perm)]
    pallas_call x4, Pallas kernels: 155 us -> 139 us  [dispatch(): pl.pallas_call(functools.partial(dispatch_kernel, scaled, begun, first, n...]
    all_gather x0 -> x1, blocking collectives: none -> 14.5 us  [device_step(): id_packets = lax.all_gather(expert_ids.astype(jnp.float32).T, ('dp', 'ep'))]
  transfers between devices with their start and end apart: 27 -> 27, of which waited for: 3 -> 5; matrix products, arithmetic and copies ran while one was open for 6% -> 5% of each run, Pallas kernels for 61% -> 61%
where the time goes in v5:
time: 1100 us; the launch traced here: 1090 us
  Pallas kernels  711 us (65%)
  waiting for transfers between devices  154 us (14%)
  starting transfers between devices  91.5 us (8%)
  other arithmetic  67.2 us (6%)
  blocking collectives  27.3 us (2%)
  between operations  19.2 us (2%)
  local copies, waits for them, and re-layouts  16.4 us (1%)
    pallas_call x2, Pallas kernels, rest_tiles(): pl.pallas_call(functools.partial(rest_kernel, begun is not None), out_sha...  231 us
    pallas_call x3, Pallas kernels, combine(): pl.pallas_call(functools.partial(combine_kernel, weighted, first, counts,...  153 us
    pallas_call x1, Pallas kernels, own_tiles(): pl.pallas_call(own_kernel, out_shape=[thin_shape] * 3 + [wide_shape] * 2,...  140 us
    pallas_call x4, Pallas kernels, dispatch(): pl.pallas_call(functools.partial(dispatch_kernel, scaled, begun, first, n...  139 us
    ppermute x5, waiting for transfers between devices, to_ep(): return lax.ppermute(far, 'ep', ep_perm)  131 us
    ppermute x5, starting transfers between devices, to_ep(): return lax.ppermute(far, 'ep', ep_perm)  60.9 us
    pallas_call x6, Pallas kernels, merge(): pl.pallas_call(merge_kernel, out_shape=jax.ShapeDtypeStruct(whole.shape,...  48.8 us
    ppermute x17, starting transfers between devices, to_core(): return lax.ppermute(away, 'dp', core_perm)  28 us
  transfers between devices with their start and end apart: 27, of which 5 were waited for; matrix products, arithmetic and copies ran while one was open for 5% of the time, Pallas kernels for 61%

profile of v5, /device:TPU:0, one launch (start us, length us, event | category | flops | bytes accessed | tf_op | source)
XLA Modules:
  0.0 1093.7 jit_solution(7813868270650516665)
XLA Ops:
  8.2 14.5 %all-gather = f32[64,1024]{1,0:T(8,128)S(1)} all-gather(f32[8,1024]{1,0:T(8,128)S(1)} %convert_bitcast_fusion), channel_id=2, replica_groups=mesh['ep'=2,'dp'=4] {'dp','ep'}, dimensions={0}, use_global_device_ids=true | all-gather | bytes 294912 | tf_op jit(solution)/shard_map/all_gather | solution.py:598
  46.2 12.8 %all-gather.2 = f32[8,9,1024]{2,1,0:T(8,128)S(1)} all-gather(f32[1,9,1024]{2,1,0:T(8,128)S(1)} %bitcast.114), channel_id=3, replica_groups=mesh['ep'=2,'dp'=4] {'dp','ep'}, dimensions={0}, use_global_device_ids=true | all-gather | bytes 331776 | tf_op jit(solution)/shard_map/all_gather | solution.py:617
  62.0 68.4 %collective-permute-done.1.rest_2_ = bf16[1024,1536]{1,0:T(8,128)(2,1)} collective-permute-done((bf16[1024,1536]{1,0:T(8,128)(2,1)}, bf16[1024,1536]{1,0:T(8,128)(2,1)}, u32[]{:S(2)}, u32[]{:S(2)}) %collective-permute-start.1) | collective-permute-done | bytes 3145760 | tf_op jit(solution)/shard_map/ppermute | solution.py:551
  143.5 50.7 %collective-permute-done.4.rest_2_.rest_0_ = bf16[1024,1536]{1,0:T(8,128)(2,1)} collective-permute-done((bf16[1024,1536]{1,0:T(8,128)(2,1)}, bf16[1024,1536]{1,0:T(8,128)(2,1)}, u32[]{:S(2)}, u32[]{:S(2)}) %collective-permute-start.4) | collective-permute-done | bytes 3145760 | tf_op jit(solution)/shard_map/ppermute | solution.py:551
  195.7 35.2 %dispatch.2.x.rest_0_ = bf16[40960,1536]{1,0:T(8,128)(2,1)} custom-call(s32[32]{0:T(128)} %and_select_fusion.6.n_chunk.n_mix, s32[32]{0:T(128)} %get-tuple-element.148.n_group, s32[320]{0:T(512)} %copy-done.24, s32[320]{0:T(512)} %sub.228.seg_src, s32[320]{0:T(512)} %reshape.643.seg_dst, s32[20]{0:T(128)} %get-tuple-element.62.tail_at, ...), custom_call_target="tpu_custom_call" | custom-call | flops 40000000000 | bytes 80000000 | tf_op jit(solution)/shard_map/dispatch/pallas_call | solution.py:152
  231.0 38.1 %dispatch_scaled.2.d_rows.rest_0_ = bf16[40960,1536]{1,0:T(8,128)(2,1)} custom-call(s32[32]{0:T(128)} %and_select_fusion.6.n_chunk.n_mix, s32[32]{0:T(128)} %get-tuple-element.148.n_group, s32[320]{0:T(512)} %copy-done.24, s32[320]{0:T(512)} %sub.228.seg_src, s32[320]{0:T(512)} %reshape.643.seg_dst, s32[20]{0:T(128)} %get-tuple-element.62.tail_at, ...), custom_call_target="tpu_custom_call" | custom-call | flops 40000000000 | bytes 80000000 | tf_op jit(solution)/shard_map/dispatch_scaled/pallas_call | solution.py:152
  269.1 139.5 %own_tiles.1 = (bf16[20480,512]{1,0:T(8,128)(2,1)}, bf16[20480,512]{1,0:T(8,128)(2,1)}, bf16[20480,512]{1,0:T(8,128)(2,1)}, bf16[20480,1536]{1,0:T(8,128)(2,1)}, bf16[20480,1536]{1,0:T(8,128)(2,1)}) custom-call(s32[40]{0:T(128)} %get-tuple-element.196.tile_exp, s32[40]{0:T(128)} %get-tuple-element.194.tile_at, s32[40]{0:T(128)} %copy-done.51, ...), custom_call_target="tpu_custom_call" | custom-call | flops 120000004096 | bytes 250000000 | tf_op jit(solution)/shard_map/own_tiles/pallas_call | solution.py:386
  408.7 48.0 %combine.1 = (f32[2048,1536]{1,0:T(8,128)}, f32[1024,1536]{1,0:T(8,128)}, f32[1024,1536]{1,0:T(8,128)}) custom-call(s32[32]{0:T(128)} %and_select_fusion.6.n_chunk.n_mix, s32[32]{0:T(128)} %get-tuple-element.148.n_group, s32[320]{0:T(512)} %copy-done.24, s32[320]{0:T(512)} %sub.228.seg_src, s32[320]{0:T(512)} %get-tuple-element.142.seg_dst, ...), custom_call_target="tpu_custom_call" | custom-call | flops 80000000000 | bytes 60000000 | tf_op jit(solution)/shard_map/combine/pallas_call | solution.py:280
  456.7 11.1 %collective-permute-start.10 = (f32[2048,1536]{1,0:T(8,128)}, f32[2048,1536]{1,0:T(8,128)}, u32[]{:S(2)}, u32[]{:S(2)}) collective-permute-start(f32[2048,1536]{1,0:T(8,128)} %get-tuple-element.75), channel_id=1, source_target_pairs={{0,1},{1,0},{2,3},{3,2},{4,5},{5,4},{6,7},{7,6}} | collective-permute-start | bytes 37748744 | tf_op jit(solution)/shard_map/ppermute | solution.py:548
  467.8 51.0 %combine_weighted.2 = (f32[2048,1536]{1,0:T(8,128)}, f32[8,256,8]{2,1,0:T(8,128)}) custom-call(s32[32]{0:T(128)} %and_select_fusion.6.n_chunk.n_mix, s32[32]{0:T(128)} %get-tuple-element.148.n_group, s32[320]{0:T(512)} %copy-done.24, s32[320]{0:T(512)} %sub.228.seg_src, s32[320]{0:T(512)} %get-tuple-element.142.seg_dst, ...), custom_call_target="tpu_custom_call" | custom-call | flops 40000000000 | bytes 60000000 | tf_op jit(solution)/shard_map/combine_weighted/pallas_call | solution.py:280
  518.9 8.7 slice_add_fusion.3
  527.6 8.3 collective-permute-start.11
  540.9 18.4 %collective-permute-done.16.rest_3_ = bf16[1024,1536]{1,0:T(8,128)(2,1)S(1)} collective-permute-done((bf16[1024,1536]{1,0:T(8,128)(2,1)}, bf16[1024,1536]{1,0:T(8,128)(2,1)S(1)}, u32[]{:S(2)}, u32[]{:S(2)}) %collective-permute-start.16) | collective-permute-done | bytes 3145760 | tf_op jit(solution)/shard_map/ppermute | solution.py:548
  564.0 31.5 %dispatch.3.x = bf16[40960,1536]{1,0:T(8,128)(2,1)} custom-call(s32[32]{0:T(128)} %and_select_fusion.6.n_chunk.n_mix, s32[32]{0:T(128)} %get-tuple-element.148.n_group, s32[320]{0:T(512)} %copy-done.24, s32[320]{0:T(512)} %sub.228.seg_src, s32[320]{0:T(512)} %reshape.643.seg_dst, s32[20]{0:T(128)} %get-tuple-element.62.tail_at, ...), custom_call_target="tpu_custom_call", output_to_operand_aliasing={{}: (9, {})} | custom-call | flops 40000000000 | bytes 80000000 | tf_op jit(solution)/shard_map/dispatch/pallas_call | solution.py:152
  597.8 21.1 %collective-permute-start.14 = (f32[1024,1536]{1,0:T(8,128)}, f32[1024,1536]{1,0:T(8,128)}, u32[]{:S(2)}, u32[]{:S(2)}) collective-permute-start(f32[1024,1536]{1,0:T(8,128)} %slice_add_fusion.3), channel_id=1, source_target_pairs={{0,4},{4,0},{1,5},{5,1},{2,6},{6,2},{3,7},{7,3}} | collective-permute-start | bytes 18874376 | tf_op jit(solution)/shard_map/ppermute | solution.py:551
  619.0 53.9 %combine_weighted.3 = (f32[1024,1536]{1,0:T(8,128)}, f32[1024,1536]{1,0:T(8,128)}, f32[8,256,8]{2,1,0:T(8,128)}) custom-call(s32[32]{0:T(128)} %and_select_fusion.6.n_chunk.n_mix, s32[32]{0:T(128)} %get-tuple-element.148.n_group, s32[320]{0:T(512)} %copy-done.24, s32[320]{0:T(512)} %sub.228.seg_src, s32[320]{0:T(512)} %get-tuple-element.142.seg_dst, ...), custom_call_target="tpu_custom_call" | custom-call | flops 40000000000 | bytes 60000000 | tf_op jit(solution)/shard_map/combine_weighted/pallas_call | solution.py:280
  676.5 8.6 slice_add_fusion.1
  685.1 6.1 collective-permute-start.13
  691.2 34.2 %dispatch_scaled.3.d_rows = bf16[40960,1536]{1,0:T(8,128)(2,1)} custom-call(s32[32]{0:T(128)} %and_select_fusion.6.n_chunk.n_mix, s32[32]{0:T(128)} %get-tuple-element.148.n_group, s32[320]{0:T(512)} %copy-done.24, s32[320]{0:T(512)} %sub.228.seg_src, s32[320]{0:T(512)} %reshape.643.seg_dst, ...), custom_call_target="tpu_custom_call", output_to_operand_aliasing={{}: (9, {})} | custom-call | flops 40000000000 | bytes 80000000 | tf_op jit(solution)/shard_map/dispatch_scaled/pallas_call | solution.py:152
  725.4 125.0 %rest_tiles.2 = (bf16[5,1536,512]{2,1,0:T(8,128)(2,1)}, bf16[5,1536,512]{2,1,0:T(8,128)(2,1)}, bf16[5,512,1536]{2,1,0:T(8,128)(2,1)}, bf16[20,1536,512]{2,1,0:T(...) custom-call(s32[40]{0:T(128)} %copy-done.36, s32[40]{0:T(128)} %get-tuple-element.187.tile_at, ...), custom_call_target="tpu_custom_call" | custom-call | flops 80000000000 | bytes 150000000 | tf_op jit(solution)/shard_map/rest_tiles/pallas_call | solution.py:406
  850.9 106.0 %rest_tiles.3 = (bf16[5,1536,512]{2,1,0:T(8,128)(2,1)}, bf16[5,1536,512]{2,1,0:T(8,128)(2,1)}, bf16[5,512,1536]{2,1,0:T(8,128)(2,1)}, bf16[20,1536,512]{2,1,0:T(...) custom-call(s32[40]{0:T(128)} %copy-done.35, ...), custom_call_target="tpu_custom_call", output_to_operand_aliasing={{3}: (16, {}), {4}: (17, {}), {5}: (18, {})} | custom-call | flops 80000000000 | bytes 150000000 | tf_op jit(solution)/shard_map/rest_tiles/pallas_call | solution.py:406
  956.9 5.5 collective-permute-start.21
  962.3 31.6 %collective-permute-start.15 = (f32[4,256,8]{2,1,0:T(8,128)S(1)}, f32[4,256,8]{2,1,0:T(8,128)S(1)}, u32[]{:S(2)}, u32[]{:S(2)}) collective-permute-start(f32[4,256,8]{2,1,0:T(8,128)S(1)} %copy-done.16), channel_id=1, source_target_pairs={{0,4},{4,0},{1,5},{5,1},{2,6},{6,2},{3,7},{7,3}} | collective-permute-start | bytes 98312 | tf_op jit(solution)/shard_map/ppermute | solution.py:551
  993.9 12.1 %collective-permute-done.15 = f32[4,256,8]{2,1,0:T(8,128)S(1)} collective-permute-done((f32[4,256,8]{2,1,0:T(8,128)S(1)}, f32[4,256,8]{2,1,0:T(8,128)S(1)}, u32[]{:S(2)}, u32[]{:S(2)}) %collective-permute-start.15) | collective-permute-done | bytes 32800 | tf_op jit(solution)/shard_map/ppermute | solution.py:551
  1015.4 7.6 fusion.9
  1023.1 11.7 %fusion.8 = (bf16[1024,1536]{1,0:T(8,128)(2,1)}, bf16[1024,1536]{1,0:T(8,128)(2,1)}) fusion(f32[1024,1536]{1,0:T(8,128)S(1)} %get-tuple-element.141, bf16[1024,1536]{1,0:T(8,128)(2,1)S(1)} %copy-done.2, bf16[1024,1536]{1,0:T(8,128)(2,1)} %rest_1_, f32[1024]{0:T(1024)S(1)} %broadcast_multiply_fusion, f32[1024]{0:T(1024)S(1)} %copy-done.26, ...), kind=kLoop, calls=%fused_computation.17 | loop fusion | flops 18874368 | bytes 37761024 | tf_op jit(solution)/shard_map/convert_element_type | solution.py:667
  1034.8 8.2 merge.6.whole_in
  1042.9 8.2 merge.8.whole_in
  1051.1 8.1 merge.7
  1059.2 8.1 merge.9
  1067.4 8.1 merge.10.whole_in
  1075.5 8.1 merge.11
  (251 shorter events, 66.2 us)
Async XLA Ops:
  7.2 1076.4 %all-reduce.3.cloned.1.call-start = ((), (), s32[]{:S(2)}) async-start(), calls=%async_computation | async-start | bytes 491520 | tf_op jit(solution)/shard_map/psum | solution.py:658
  44.8 150.9 %copy-start.6 = (s32[32,8,256]{2,1,0:T(8,128)}, s32[32,8,256]{2,1,0:T(8,128)S(1)}, u32[]{:S(2)}) copy-start(s32[32,8,256]{2,1,0:T(8,128)S(1)} %convert_add_fusion.1.pos) | copy-start | bytes 786436
  59.1 71.3 %collective-permute-start.1 = (bf16[1024,1536]{1,0:T(8,128)(2,1)}, bf16[1024,1536]{1,0:T(8,128)(2,1)}, u32[]{:S(2)}, u32[]{:S(2)}) collective-permute-start(bf16[1024,1536]{1,0:T(8,128)(2,1)} %copy-done.3), channel_id=1, source_target_pairs={{0,4},{4,0},{1,5},{5,1},{2,6},{6,2},{3,7},{7,3}} | collective-permute-start | bytes 9437192 | tf_op jit(solution)/shard_map/ppermute | solution.py:551
  59.6 83.4 %collective-permute-start.9 = (bf16[1024,1536]{1,0:T(8,128)(2,1)}, bf16[1024,1536]{1,0:T(8,128)(2,1)}, u32[]{:S(2)}, u32[]{:S(2)}) collective-permute-start(bf16[1024,1536]{1,0:T(8,128)(2,1)} %copy-done.3), channel_id=1, source_target_pairs={{0,1},{1,0},{2,3},{3,2},{4,5},{5,4},{6,7},{7,6}} | collective-permute-start | bytes 9437192 | tf_op jit(solution)/shard_map/ppermute | solution.py:548
  59.6 134.6 %collective-permute-start.4 = (bf16[1024,1536]{1,0:T(8,128)(2,1)}, bf16[1024,1536]{1,0:T(8,128)(2,1)}, u32[]{:S(2)}, u32[]{:S(2)}) collective-permute-start(bf16[1024,1536]{1,0:T(8,128)(2,1)} %rest_1_), channel_id=1, source_target_pairs={{0,4},{4,0},{1,5},{5,1},{2,6},{6,2},{3,7},{7,3}} | collective-permute-start | bytes 9437192 | tf_op jit(solution)/shard_map/ppermute | solution.py:551
  61.1 169.9 %collective-permute-start.7 = (bf16[1024,1536]{1,0:T(8,128)(2,1)}, bf16[1024,1536]{1,0:T(8,128)(2,1)}, u32[]{:S(2)}, u32[]{:S(2)}) collective-permute-start(bf16[1024,1536]{1,0:T(8,128)(2,1)} %rest_1_), channel_id=1, source_target_pairs={{0,1},{1,0},{2,3},{3,2},{4,5},{5,4},{6,7},{7,6}} | collective-permute-start | bytes 9437192 | tf_op jit(solution)/shard_map/ppermute | solution.py:548
  61.3 347.3 %collective-permute-start = (bf16[1024,1536]{1,0:T(8,128)(2,1)}, bf16[1024,1536]{1,0:T(8,128)(2,1)}, u32[]{:S(2)}, u32[]{:S(2)}) collective-permute-start(bf16[1024,1536]{1,0:T(8,128)(2,1)} %copy-done.3), channel_id=1, source_target_pairs={{0,2},{1,3},{2,0},{3,1},{4,6},{5,7},{6,4},{7,5}} | collective-permute-start | bytes 9437192 | tf_op jit(solution)/shard_map/ppermute | solution.py:554
  130.4 65.3 %collective-permute-start.8 = (bf16[1024,1536]{1,0:T(8,128)(2,1)}, bf16[1024,1536]{1,0:T(8,128)(2,1)}, u32[]{:S(2)}, u32[]{:S(2)}) collective-permute-start(bf16[1024,1536]{1,0:T(8,128)(2,1)} %collective-permute-done.1.rest_2_), channel_id=1, source_target_pairs={{0,1},{1,0},{2,3},{3,2},{4,5},{5,4},{6,7},{7,6}} | collective-permute-start | bytes 9437192 | tf_op jit(solution)/shard_map/ppermute | solution.py:548
  143.0 265.7 %collective-permute-start.3 = (bf16[1024,1536]{1,0:T(8,128)(2,1)}, bf16[1024,1536]{1,0:T(8,128)(2,1)}, u32[]{:S(2)}, u32[]{:S(2)}) collective-permute-start(bf16[1024,1536]{1,0:T(8,128)(2,1)} %rest_1_), channel_id=1, source_target_pairs={{0,2},{1,3},{2,0},{3,1},{4,6},{5,7},{6,4},{7,5}} | collective-permute-start | bytes 9437192 | tf_op jit(solution)/shard_map/ppermute | solution.py:554
  194.2 214.5 %collective-permute-start.2 = (bf16[1024,1536]{1,0:T(8,128)(2,1)}, bf16[1024,1536]{1,0:T(8,128)(2,1)}, u32[]{:S(2)}, u32[]{:S(2)}) collective-permute-start(bf16[1024,1536]{1,0:T(8,128)(2,1)} %collective-permute-done.1.rest_2_), channel_id=1, source_target_pairs={{0,2},{1,3},{2,0},{3,1},{4,6},{5,7},{6,4},{7,5}} | collective-permute-start | bytes 9437192 | tf_op jit(solution)/shard_map/ppermute | solution.py:554
  195.7 35.3 %collective-permute-start.6 = (bf16[1024,1536]{1,0:T(8,128)(2,1)}, bf16[1024,1536]{1,0:T(8,128)(2,1)}, u32[]{:S(2)}, u32[]{:S(2)}) collective-permute-start(bf16[1024,1536]{1,0:T(8,128)(2,1)} %collective-permute-done.4.rest_2_.rest_0_), channel_id=1, source_target_pairs={{0,1},{1,0},{2,3},{3,2},{4,5},{5,4},{6,7},{7,6}} | collective-permute-start | bytes 9437192 | tf_op jit(solution)/shard_map/ppermute | solution.py:548
  231.0 177.7 %collective-permute-start.5 = (bf16[1024,1536]{1,0:T(8,128)(2,1)}, bf16[1024,1536]{1,0:T(8,128)(2,1)}, u32[]{:S(2)}, u32[]{:S(2)}) collective-permute-start(bf16[1024,1536]{1,0:T(8,128)(2,1)} %collective-permute-done.4.rest_2_.rest_0_), channel_id=1, source_target_pairs={{0,2},{1,3},{2,0},{3,1},{4,6},{5,7},{6,4},{7,5}} | collective-permute-start | bytes 9437192 | tf_op jit(solution)/shard_map/ppermute | solution.py:554
  456.7 62.1 %collective-permute-start.10 = (f32[2048,1536]{1,0:T(8,128)}, f32[2048,1536]{1,0:T(8,128)}, u32[]{:S(2)}, u32[]{:S(2)}) collective-permute-start(f32[2048,1536]{1,0:T(8,128)} %get-tuple-element.75), channel_id=1, source_target_pairs={{0,1},{1,0},{2,3},{3,2},{4,5},{5,4},{6,7},{7,6}} | collective-permute-start | bytes 37748744 | tf_op jit(solution)/shard_map/ppermute | solution.py:548
  527.6 148.9 %collective-permute-start.11 = (f32[2048,1536]{1,0:T(8,128)}, f32[2048,1536]{1,0:T(8,128)}, u32[]{:S(2)}, u32[]{:S(2)}) collective-permute-start(f32[2048,1536]{1,0:T(8,128)} %get-tuple-element.78), channel_id=1, source_target_pairs={{0,1},{1,0},{2,3},{3,2},{4,5},{5,4},{6,7},{7,6}} | collective-permute-start | bytes 37748744 | tf_op jit(solution)/shard_map/ppermute | solution.py:548
  535.9 23.5 %collective-permute-start.16 = (bf16[1024,1536]{1,0:T(8,128)(2,1)}, bf16[1024,1536]{1,0:T(8,128)(2,1)S(1)}, u32[]{:S(2)}, u32[]{:S(2)}) collective-permute-start(bf16[1024,1536]{1,0:T(8,128)(2,1)} %collective-permute-done.rest_1_), channel_id=1, source_target_pairs={{0,1},{1,0},{2,3},{3,2},{4,5},{5,4},{6,7},{7,6}} | collective-permute-start | bytes 9437192 | tf_op jit(solution)/shard_map/ppermute | solution.py:548
  535.9 28.1 %collective-permute-start.17 = (bf16[1024,1536]{1,0:T(8,128)(2,1)}, bf16[1024,1536]{1,0:T(8,128)(2,1)}, u32[]{:S(2)}, u32[]{:S(2)}) collective-permute-start(bf16[1024,1536]{1,0:T(8,128)(2,1)} %collective-permute-done.2.rest_2_), channel_id=1, source_target_pairs={{0,1},{1,0},{2,3},{3,2},{4,5},{5,4},{6,7},{7,6}} | collective-permute-start | bytes 9437192 | tf_op jit(solution)/shard_map/ppermute | solution.py:548
  540.4 150.7 %collective-permute-start.18 = (bf16[1024,1536]{1,0:T(8,128)(2,1)}, bf16[1024,1536]{1,0:T(8,128)(2,1)}, u32[]{:S(2)}, u32[]{:S(2)}) collective-permute-start(bf16[1024,1536]{1,0:T(8,128)(2,1)} %collective-permute-done.3.rest_1_), channel_id=1, source_target_pairs={{0,1},{1,0},{2,3},{3,2},{4,5},{5,4},{6,7},{7,6}} | collective-permute-start | bytes 9437192 | tf_op jit(solution)/shard_map/ppermute | solution.py:548
  540.4 150.7 %collective-permute-start.19 = (bf16[1024,1536]{1,0:T(8,128)(2,1)}, bf16[1024,1536]{1,0:T(8,128)(2,1)}, u32[]{:S(2)}, u32[]{:S(2)}) collective-permute-start(bf16[1024,1536]{1,0:T(8,128)(2,1)} %collective-permute-done.5.rest_2_), channel_id=1, source_target_pairs={{0,1},{1,0},{2,3},{3,2},{4,5},{5,4},{6,7},{7,6}} | collective-permute-start | bytes 9437192 | tf_op jit(solution)/shard_map/ppermute | solution.py:548
  597.0 75.9 %collective-permute-start.12 = (f32[8,256,8]{1,2,0:T(8,128)S(1)}, f32[8,256,8]{1,2,0:T(8,128)S(1)}, u32[]{:S(2)}, u32[]{:S(2)}) collective-permute-start(f32[8,256,8]{1,2,0:T(8,128)S(1)} %copy.68), channel_id=1, source_target_pairs={{0,1},{1,0},{2,3},{3,2},{4,5},{5,4},{6,7},{7,6}} | collective-permute-start | bytes 196616 | tf_op jit(solution)/shard_map/ppermute | solution.py:548
  597.8 364.5 %collective-permute-start.14 = (f32[1024,1536]{1,0:T(8,128)}, f32[1024,1536]{1,0:T(8,128)}, u32[]{:S(2)}, u32[]{:S(2)}) collective-permute-start(f32[1024,1536]{1,0:T(8,128)} %slice_add_fusion.3), channel_id=1, source_target_pairs={{0,4},{4,0},{1,5},{5,1},{2,6},{6,2},{3,7},{7,3}} | collective-permute-start | bytes 18874376 | tf_op jit(solution)/shard_map/ppermute | solution.py:551
  685.1 323.4 %collective-permute-start.13 = (f32[1024,1536]{1,0:T(8,128)}, f32[1024,1536]{1,0:T(8,128)}, u32[]{:S(2)}, u32[]{:S(2)}) collective-permute-start(f32[1024,1536]{1,0:T(8,128)} %slice_add_fusion.1), channel_id=1, source_target_pairs={{0,4},{4,0},{1,5},{5,1},{2,6},{6,2},{3,7},{7,3}} | collective-permute-start | bytes 18874376 | tf_op jit(solution)/shard_map/ppermute | solution.py:551
  850.4 160.4 %collective-permute-start.20 = (bf16[5,1536,512]{2,1,0:T(8,128)(2,1)}, bf16[5,1536,512]{2,1,0:T(8,128)(2,1)}, u32[]{:S(2)}, u32[]{:S(2)}) collective-permute-start(bf16[5,1536,512]{2,1,0:T(8,128)(2,1)} %get-tuple-element.101), channel_id=1, source_target_pairs={{0,1},{1,0},{2,3},{3,2},{4,5},{5,4},{6,7},{7,6}} | collective-permute-start | bytes 23592968 | tf_op jit(solution)/shard_map/ppermute | solution.py:548
  850.4 192.5 %collective-permute-start.22 = (bf16[5,1536,512]{2,1,0:T(8,128)(2,1)}, bf16[5,1536,512]{2,1,0:T(8,128)(2,1)}, u32[]{:S(2)}, u32[]{:S(2)}) collective-permute-start(bf16[5,1536,512]{2,1,0:T(8,128)(2,1)} %get-tuple-element.104), channel_id=1, source_target_pairs={{0,1},{1,0},{2,3},{3,2},{4,5},{5,4},{6,7},{7,6}} | collective-permute-start | bytes 23592968 | tf_op jit(solution)/shard_map/ppermute | solution.py:548
  850.9 155.2 %copy-start.12 = (f32[64,1024]{1,0:T(8,128)S(1)}, f32[64,1024]{1,0:T(8,128)}, u32[]{:S(2)}) copy-start(f32[64,1024]{1,0:T(8,128)} %copy-done.11) | copy-start | bytes 786436
  850.9 159.4 %copy-start.5 = (f32[8,256,8]{2,1,0:T(8,128)S(1)}, f32[8,256,8]{2,1,0:T(8,128)}, u32[]{:S(2)}) copy-start(f32[8,256,8]{2,1,0:T(8,128)} %copy-done.4) | copy-start | bytes 196612
  850.9 159.6 %copy-start.17 = (s32[1024,8]{0,1:T(8,128)S(1)}, s32[1024,8]{0,1:T(8,128)}, u32[]{:S(2)}) copy-start(s32[1024,8]{0,1:T(8,128)} %param.10) | copy-start | bytes 98308
  850.9 159.8 %copy-start.10 = (f32[1024,40]{0,1:T(8,128)S(1)}, f32[1024,40]{0,1:T(8,128)}, u32[]{:S(2)}) copy-start(f32[1024,40]{0,1:T(8,128)} %copy-done.9) | copy-start | bytes 491524
  956.9 94.2 %collective-permute-start.21 = (bf16[5,1536,512]{2,1,0:T(8,128)(2,1)}, bf16[5,1536,512]{2,1,0:T(8,128)(2,1)}, u32[]{:S(2)}, u32[]{:S(2)}) collective-permute-start(bf16[5,1536,512]{2,1,0:T(8,128)(2,1)} %get-tuple-element.102), channel_id=1, source_target_pairs={{0,1},{1,0},{2,3},{3,2},{4,5},{5,4},{6,7},{7,6}} | collective-permute-start | bytes 23592968 | tf_op jit(solution)/shard_map/ppermute | solution.py:548
  962.3 43.7 %collective-permute-start.15 = (f32[4,256,8]{2,1,0:T(8,128)S(1)}, f32[4,256,8]{2,1,0:T(8,128)S(1)}, u32[]{:S(2)}, u32[]{:S(2)}) collective-permute-start(f32[4,256,8]{2,1,0:T(8,128)S(1)} %copy-done.16), channel_id=1, source_target_pairs={{0,4},{4,0},{1,5},{5,1},{2,6},{6,2},{3,7},{7,3}} | collective-permute-start | bytes 98312 | tf_op jit(solution)/shard_map/ppermute | solution.py:551
  1006.1 53.2 %collective-permute-start.23 = (bf16[5,1536,512]{2,1,0:T(8,128)(2,1)}, bf16[5,1536,512]{2,1,0:T(8,128)(2,1)}, u32[]{:S(2)}, u32[]{:S(2)}) collective-permute-start(bf16[5,1536,512]{2,1,0:T(8,128)(2,1)} %get-tuple-element.105), channel_id=1, source_target_pairs={{0,1},{1,0},{2,3},{3,2},{4,5},{5,4},{6,7},{7,6}} | collective-permute-start | bytes 23592968 | tf_op jit(solution)/shard_map/ppermute | solution.py:548
  1008.5 58.9 %collective-permute-start.24 = (bf16[5,512,1536]{2,1,0:T(8,128)(2,1)}, bf16[5,512,1536]{2,1,0:T(8,128)(2,1)}, u32[]{:S(2)}, u32[]{:S(2)}) collective-permute-start(bf16[5,512,1536]{2,1,0:T(8,128)(2,1)} %get-tuple-element.107), channel_id=1, source_target_pairs={{0,1},{1,0},{2,3},{3,2},{4,5},{5,4},{6,7},{7,6}} | collective-permute-start | bytes 23592968 | tf_op jit(solution)/shard_map/ppermute | solution.py:548
  1010.8 64.7 %collective-permute-start.25 = (bf16[5,512,1536]{2,1,0:T(8,128)(2,1)}, bf16[5,512,1536]{2,1,0:T(8,128)(2,1)}, u32[]{:S(2)}, u32[]{:S(2)}) collective-permute-start(bf16[5,512,1536]{2,1,0:T(8,128)(2,1)} %get-tuple-element.108), channel_id=1, source_target_pairs={{0,1},{1,0},{2,3},{3,2},{4,5},{5,4},{6,7},{7,6}} | collective-permute-start | bytes 23592968 | tf_op jit(solution)/shard_map/ppermute | solution.py:548
  (47 other events, 1603.7 us)
Sparse Core Ops, SparseCore 0:
  1014.5 43.9 all-reduce.2
